TPU v7x, 8 devices: a whole 2x2x1 slice. The times are simulated.
8 devices in a mesh: dp: 2 (over z, y), tp: 4 (over x, core).
Axes of the slice: x: 2, y: 2, z: 1, core: 2. Of those that a mesh axis runs over, the one named last changes fastest.
Arguments:
- x_in: bfloat16 [1024, 1536], P('dp'), parts along dimension 0
- tok_pos: int32 [1024], P('dp'), parts along dimension 0
- self_k: bfloat16 [1024, 128, 16, 64], P('dp', None, 'tp'), parts along dimension 0
- self_v: bfloat16 [1024, 128, 16, 64], P('dp', None, 'tp'), parts along dimension 0
- cross_k: bfloat16 [1024, 64, 16, 64], P('dp', None, 'tp'), parts along dimension 0
- cross_v: bfloat16 [1024, 64, 16, 64], P('dp', None, 'tp'), parts along dimension 0
- enc_mask: int32 [1024, 64], P('dp'), parts along dimension 0
- rel_bias: float32 [32, 16], P(None, 'tp')
- w_q: bfloat16 [1536, 1024], P(None, 'tp')
- w_k: bfloat16 [1536, 1024], P(None, 'tp')
- w_v: bfloat16 [1536, 1024], P(None, 'tp')
- w_o: bfloat16 [1024, 1536], P('tp')
- cross_q: bfloat16 [1536, 1024], P(None, 'tp')
- cross_o: bfloat16 [1024, 1536], P('tp')
- w_gate: bfloat16 [1536, 3840], P(None, 'tp')
- w_up: bfloat16 [1536, 3840], P(None, 'tp')
- w_down: bfloat16 [3840, 1536], P('tp')
- norm_self: bfloat16 [1536], replicated
- norm_cross: bfloat16 [1536], replicated
- norm_mlp: bfloat16 [1536], replicated
Outputs:
- output 1: bfloat16 [1024, 1536], P('dp'), parts along dimension 0
- output 2: bfloat16 [1024, 128, 16, 64], P('dp', None, 'tp'), parts along dimension 0
- output 3: bfloat16 [1024, 128, 16, 64], P('dp', None, 'tp'), parts along dimension 0
There are 2 independent parts. A program takes and returns all parts, laid end to end along the dimension named above; an argument that names none is the same for every part.
All inputs are finite; a program needn't handle non-finite values.
Results may differ from a plain program's by a relative error of at most 0.0172771.
Values are sent between devices in bfloat16 or wider.
A program may use at most 1 GiB of HBM per device.

v0:
```python
import math
import jax
import jax.numpy as jnp
from jax import lax
from jax.sharding import PartitionSpec as P

BUCKET_EDGES = tuple(int(math.ceil(16.0 * 8.0 ** (bucket_step / 16.0))) for bucket_step in range(1, 16))
NEG_FILL = -1e30


def rms_norm(values, norm_scale):
    inv_rms = lax.rsqrt(jnp.mean(values * values, axis=-1, keepdims=True) + 1e-6)
    return (values * inv_rms * norm_scale.astype(jnp.float32)).astype(jnp.bfloat16)


def project(normed, weight):
    return jnp.dot(normed, weight, preferred_element_type=jnp.float32).astype(jnp.bfloat16)


def rel_bucket(distance):
    bucket_edges = jnp.array(BUCKET_EDGES, dtype=jnp.int32)
    far_bucket = 16 + jnp.sum((distance[..., None] >= bucket_edges).astype(jnp.int32), axis=-1)
    return jnp.where(distance < 16, distance, far_bucket)


def attend(queries, keys_all, values_all, extra):
    scores = jnp.einsum('bhk,bthk->bht', queries, keys_all, preferred_element_type=jnp.float32) + extra
    probs_bf = jax.nn.softmax(scores, axis=-1).astype(jnp.bfloat16)
    mixed_out = jnp.einsum('bht,bthk->bhk', probs_bf, values_all, preferred_element_type=jnp.float32)
    return mixed_out.astype(jnp.bfloat16)


def self_terms(tok_pos, rel_bias, t_len):
    key_index = jnp.arange(t_len)
    at_pos = (key_index[None, :] == tok_pos[:, None])[:, :, None, None]
    distance = jnp.maximum(tok_pos[:, None] - key_index[None, :], 0)
    bias_rows = jnp.swapaxes(jnp.take(rel_bias, rel_bucket(distance), axis=0), 1, 2)
    causal = (key_index[None, :] <= tok_pos[:, None])[:, None, :]
    return at_pos, jnp.where(causal, bias_rows, NEG_FILL)


def solution(mesh):
    def tp_sum(partial_out):
        return lax.psum(partial_out.astype(jnp.bfloat16), 'tp').astype(jnp.float32)

    def local_layer(x_in, tok_pos, self_k, self_v, cross_k, cross_v, enc_mask, rel_bias, w_q, w_k, w_v, w_o, cross_q, cross_o, w_gate, w_up, w_down, norm_self, norm_cross, norm_mlp):
        row_count, t_len, head_count, head_dim = self_k.shape
        head_shape = (row_count, head_count, head_dim)
        flat_dim = head_count * head_dim
        residual = x_in.astype(jnp.float32)
        normed = rms_norm(residual, norm_self)
        queries = project(normed, w_q).reshape(head_shape)
        new_keys = project(normed, w_k).reshape(head_shape)
        new_values = project(normed, w_v).reshape(head_shape)
        at_pos, self_extra = self_terms(tok_pos, rel_bias, t_len)
        new_self_k = jnp.where(at_pos, new_keys[:, None], self_k)
        new_self_v = jnp.where(at_pos, new_values[:, None], self_v)
        mixed_self = attend(queries, new_self_k, new_self_v, self_extra)
        residual = residual + tp_sum(jnp.dot(mixed_self.reshape(row_count, flat_dim), w_o, preferred_element_type=jnp.float32))
        normed = rms_norm(residual, norm_cross)
        cross_queries = project(normed, cross_q).reshape(head_shape)
        cross_extra = jnp.where(enc_mask[:, None, :] != 0, 0.0, NEG_FILL)
        mixed_cross = attend(cross_queries, cross_k, cross_v, cross_extra)
        residual = residual + tp_sum(jnp.dot(mixed_cross.reshape(row_count, flat_dim), cross_o, preferred_element_type=jnp.float32))
        normed = rms_norm(residual, norm_mlp)
        gate_pre = jnp.dot(normed, w_gate, preferred_element_type=jnp.float32)
        up_pre = jnp.dot(normed, w_up, preferred_element_type=jnp.float32)
        hidden = (jax.nn.gelu(gate_pre, approximate=True) * up_pre).astype(jnp.bfloat16)
        residual = residual + tp_sum(jnp.dot(hidden, w_down, preferred_element_type=jnp.float32))
        return residual.astype(jnp.bfloat16), new_self_k, new_self_v

    cache_spec = P('dp', None, 'tp', None)
    split_cols = P(None, 'tp')
    split_rows = P('tp', None)
    in_specs = (P('dp', None), P('dp'), cache_spec, cache_spec, cache_spec, cache_spec, P('dp', None), split_cols, split_cols, split_cols, split_cols, split_rows, split_cols, split_rows, split_cols, split_cols, split_rows, P(None), P(None), P(None))
    out_specs = (P('dp', None), cache_spec, cache_spec)
    return jax.shard_map(local_layer, mesh=mesh, in_specs=in_specs, out_specs=out_specs, check_vma=False)
```

profile of v0, /device:TPU:0, one launch (start us, length us, event | category | flops | bytes accessed | tf_op | source)
XLA Modules:
  0.0 571.4 jit_solution(5545238083336910327)
XLA Ops:
  8.2 1.3 convert_reduce_fusion
  9.5 1.6 iota_compare_fusion
  11.1 1.6 fusion.29
  13.3 1.8 fusion.6
  16.0 1.2 copy.60
  17.2 3.1 convolution_convert_fusion.4
  20.2 1.3 copy.32
  21.5 47.3 %multiply_reduce_fusion.1 = (f32[512,4,128]{2,1,0:T(4,128)}, bf16[512,128,4,64]{1,3,2,0:T(8,128)(2,1)}) fusion(f32[512,4,64]{2,1,0:T(4,128)} %copy.60, bf16[512,128,4,64]{1,3,2,0:T(8,128)(2,1)} %param.23, bf16[512,4,64]{2,1,0:T(4,128)(2,1)S(1)} %copy.32, pred[512,128]{1,0:T(8,128)(4,1)S(1)} %get-tuple-element.9), kind=kLoop, calls=%fused_computation.6 | loop fusion | flops 66846720 | bytes 69009408
  68.8 16.2 %copy.40 = f32[512,4,128]{1,2,0:T(8,128)} copy(f32[512,4,128]{2,1,0:T(4,128)} %get-tuple-element.5) | data formatting | bytes 2097152 | tf_op jit(solution)/shard_map/bhk,bthk->bht/dot_general | solution.py:27
  85.1 215.5 %gather_fusion = f32[65536,4]{1,0:T(8,128)} fusion(f32[32,4]{1,0:T(8,128)S(1)} %copy.33, s32[65536]{0:T(1024)S(1)} %copy-done.8), kind=kCustom, calls=%fused_computation | custom fusion | bytes 2359296 | tf_op jit(solution)/shard_map/jit(_take)/gather | solution.py:37
  300.6 33.1 %fusion.4 = f32[512,4,128]{1,2,0:T(8,128)} fusion(f32[512,4,128]{1,2,0:T(8,128)} %copy.40, f32[512,128,4]{2,1,0:T(8,128)} %bitcast.42, pred[512,128]{1,0:T(8,128)(4,1)S(1)} %copy-done.14, pred[512,128]{1,0:T(8,128)(4,1)S(1)} %copy-done.13), kind=kOutput, calls=%fused_computation.14 | output fusion | flops 1839358 | bytes 3276800 | tf_op jit(solution)/shard_map/div | solution.py:28
  333.7 18.3 %copy.61 = f32[512,4,128]{2,1,0:T(4,128)} copy(f32[512,4,128]{1,2,0:T(8,128)} %fusion.4) | data formatting | bytes 2097152
  352.0 3.1 convolution_convert_fusion.3
  355.1 1.3 copy.34
  356.4 41.9 %multiply_reduce_fusion = (bf16[512,4,64]{2,1,0:T(4,128)(2,1)}, bf16[512,128,4,64]{1,3,2,0:T(8,128)(2,1)}) fusion(f32[512,4,128]{2,1,0:T(4,128)} %copy.61, bf16[512,128,4,64]{1,3,2,0:T(8,128)(2,1)} %param.24, bf16[512,4,64]{2,1,0:T(4,128)(2,1)S(1)} %copy.34, pred[512,128]{1,0:T(8,128)(4,1)S(1)} %copy-done.11), kind=kLoop, calls=%fused_computation.5 | loop fusion | flops 66977792 | bytes 68747264
  398.3 1.3 copy.46
  399.6 2.9 convolution_convert_fusion.2
  403.4 39.3 %all-reduce.4.cloned.1.call-done = bf16[512,1536]{1,0:T(8,128)(2,1)} async-done(((bf16[512,1536]{1,0:T(8,128)(2,1)}), bf16[512,1536]{1,0:T(8,128)(2,1)}) %all-reduce.4.cloned.1.call-update) | async-done | bytes 1572880 | tf_op jit(solution)/shard_map/psum | solution.py:44
  442.8 2.6 multiply_reduce_fusion.5
  445.6 2.0 bitcast_convert_fusion
  447.6 8.2 %multiply_reduce_fusion.3 = f32[512,4,64]{0,1,2:T(4,128)S(1)} fusion(f32[512,4,64]{0,2,1:T(8,128)S(1)} %bitcast_convert_fusion, bf16[512,64,4,64]{0,3,2,1:T(8,128)(2,1)} %param.25), kind=kLoop, calls=%fused_computation.9 | loop fusion | flops 25034752 | bytes 17825792
  455.9 2.0 fusion.25
  457.9 1.4 copy.63
  459.3 7.5 %multiply_reduce_fusion.2 = bf16[512,4,64]{0,2,1:T(8,128)(2,1)S(1)} fusion(f32[512,4,64]{0,1,2:T(4,128)S(1)} %copy.63, bf16[512,64,4,64]{0,3,2,1:T(8,128)(2,1)} %param.26), kind=kLoop, calls=%fused_computation.8 | loop fusion | flops 25034752 | bytes 17563648 | tf_op jit(solution)/shard_map/bht,bthk->bhk/dot_general | solution.py:29
  466.8 1.7 convolution_convert_fusion.1
  468.7 37.4 %all-reduce.6.cloned.1.call-done = bf16[512,1536]{1,0:T(8,128)(2,1)} async-done(((bf16[512,1536]{1,0:T(8,128)(2,1)}), bf16[512,1536]{1,0:T(8,128)(2,1)}) %all-reduce.6.cloned.1.call-update) | async-done | bytes 1572880 | tf_op jit(solution)/shard_map/psum | solution.py:44
  506.1 3.3 multiply_reduce_fusion.4
  510.7 1.1 copy-done.7
  511.9 3.0 fusion.41
  514.9 7.8 %convolution_convert_fusion = bf16[512,1536]{1,0:T(8,128)(2,1)} fusion(bf16[960,1536]{1,0:T(8,128)(2,1)S(1)} %copy-done, f32[512,960]{0,1:T(8,128)} %fusion.41, bf16[512,1536]{1,0:T(8,128)(2,1)} %copy-done.7, bf16[1536,960]{0,1:T(8,128)(2,1)} %param.36), kind=kOutput, calls=%fused_computation.29 | convolution fusion | flops 3025600512 | bytes 11010048 | tf_op jit(solution)/shard_map/dot_general | solution.py:69
  522.7 37.4 %all-reduce.8.cloned.1.call-done = bf16[512,1536]{1,0:T(8,128)(2,1)} async-done(((bf16[512,1536]{1,0:T(8,128)(2,1)}), bf16[512,1536]{1,0:T(8,128)(2,1)}) %all-reduce.8.cloned.1.call-update) | async-done | bytes 1572880 | tf_op jit(solution)/shard_map/psum | solution.py:44
  560.1 4.8 add_convert_fusion
  (64 shorter events, 5.2 us)
Async XLA Ops:
  7.2 507.7 %copy-start = (bf16[960,1536]{1,0:T(8,128)(2,1)S(1)}, bf16[960,1536]{1,0:T(8,128)(2,1)}, u32[]{:S(2)}) copy-start(bf16[960,1536]{1,0:T(8,128)(2,1)} %param.37) | copy-start | bytes 8847364
  7.2 435.6 %all-reduce.4.cloned.1.call-start = ((), (), s32[]{:S(2)}) async-start(), calls=%async_computation | async-start | bytes 3145728 | tf_op jit(solution)/shard_map/psum | solution.py:44
  7.2 7.9 %copy-start.1 = (bf16[512,1536]{1,0:T(8,128)(2,1)S(1)}, bf16[512,1536]{1,0:T(8,128)(2,1)}, u32[]{:S(2)}) copy-start(bf16[512,1536]{1,0:T(8,128)(2,1)} %param.21) | copy-start | bytes 4718596
  7.2 7.9 %copy-start.23 = (bf16[1536,256]{1,0:T(8,128)(2,1)S(1)}, bf16[1536,256]{1,0:T(8,128)(2,1)}, u32[]{:S(2)}) copy-start(bf16[1536,256]{1,0:T(8,128)(2,1)} %param.29) | copy-start | bytes 2359300
  11.1 10.4 %copy-start.10 = (pred[512,128]{1,0:T(8,128)(4,1)}, pred[512,128]{1,0:T(8,128)(4,1)S(1)}, u32[]{:S(2)}) copy-start(pred[512,128]{1,0:T(8,128)(4,1)S(1)} %get-tuple-element.9) | copy-start | bytes 196612
  13.3 3.8 copy-start.15
  15.2 5.1 copy-start.20
  68.8 16.2 %copy-start.19 = (f32[32,4]{0,1:T(4,128)S(1)}, f32[32,4]{0,1:T(4,128)}, u32[]{:S(2)}) copy-start(f32[32,4]{0,1:T(4,128)} %param.28) | copy-start | bytes 1540
  68.8 16.3 %copy-start.8 = (s32[65536]{0:T(1024)S(1)}, s32[65536]{0:T(1024)}, u32[]{:S(2)}) copy-start(s32[65536]{0:T(1024)} %fusion.29) | copy-start | bytes 786436
  85.1 215.5 %copy-start.13 = (pred[512,128]{1,0:T(8,128)(4,1)S(1)}, pred[512,128]{1,0:T(8,128)(4,1)}, u32[]{:S(2)}) copy-start(pred[512,128]{1,0:T(8,128)(4,1)} %get-tuple-element.7) | copy-start | bytes 196612
  85.1 215.5 %copy-start.14 = (pred[512,128]{1,0:T(8,128)(4,1)S(1)}, pred[512,128]{1,0:T(8,128)(4,1)}, u32[]{:S(2)}) copy-start(pred[512,128]{1,0:T(8,128)(4,1)} %get-tuple-element.8) | copy-start | bytes 196612
  333.7 18.3 %copy-start.16 = (f32[1536]{0:T(1024)S(1)}, f32[1536]{0:T(1024)}, u32[]{:S(2)}) copy-start(f32[1536]{0:T(1024)} %copy-done.15) | copy-start | bytes 18436
  333.7 18.3 %copy-start.21 = (f32[512]{0:T(512)S(1)}, f32[512]{0:T(512)}, u32[]{:S(2)}) copy-start(f32[512]{0:T(512)} %copy-done.20) | copy-start | bytes 6148
  352.0 4.4 copy-start.11
  398.3 4.5 copy-start.17
  398.3 4.5 copy-start.12
  402.5 103.6 %all-reduce.6.cloned.1.call-start = ((), (), s32[]{:S(2)}) async-start(), calls=%async_computation.1 | async-start | bytes 3145728 | tf_op jit(solution)/shard_map/psum | solution.py:44
  442.8 2.6 copy-start.2
  442.8 2.8 copy-start.4
  459.3 7.6 %copy-start.9 = (bf16[256,1536]{1,0:T(8,128)(2,1)S(1)}, bf16[256,1536]{1,0:T(8,128)(2,1)}, u32[]{:S(2)}) copy-start(bf16[256,1536]{1,0:T(8,128)(2,1)} %param.34) | copy-start | bytes 2359300
  466.8 1.8 copy-start.18
  468.6 91.5 %all-reduce.8.cloned.1.call-start = ((), (), s32[]{:S(2)}) async-start(), calls=%async_computation.2 | async-start | bytes 3145728 | tf_op jit(solution)/shard_map/psum | solution.py:44
  506.1 3.3 copy-start.3
  506.1 3.3 copy-start.5
  506.1 3.8 copy-start.6
  509.8 2.1 copy-start.22
  510.7 1.1 copy-start.7
Sparse Core Ops, SparseCore 0:
  402.6 40.0 all-reduce.3
  468.7 37.2 all-reduce.5
  522.8 37.2 all-reduce.7
where the time goes:
time: 572 us; the launch traced here: 571 us
  local copies, waits for them, and re-layouts  258 us (45%)
  other arithmetic  160 us (28%)
  waiting for transfers between devices  114 us (20%)
  matrix products  24.4 us (4%)
  between operations  14 us (2%)
    gather x1, local copies, waits for them, and re-layouts, self_terms(): jnp.take(rel_bias, rel_bucket(distance), axis=0)  216 us
    psum x3, waiting for transfers between devices, tp_sum(): return lax.psum(partial_out.astype(jnp.bfloat16), 'tp').astype(jnp.float32)  114 us
    unnamed x3, other arithmetic  97.4 us
    div x2, other arithmetic, attend(): probs_bf = jax.nn.softmax(scores, axis=-1).astype(jnp.bfloat16)  35.1 us
    unnamed x52, local copies, waits for them, and re-layouts  22.8 us
    dot_general x1, local copies, waits for them, and re-layouts, attend(): jnp.einsum('bhk,bthk->bht', queries, keys_all, preferred_element_type=jnp...  16.2 us
  transfers between devices with their start and end apart: 3, of which 3 were waited for; matrix products, arithmetic and copies ran while one was open for 0% of the time, Pallas kernels for 0%

commit v1 on v0

v1 whole, which is shorter than its diff:
```python
import functools
import math
import jax
import jax.numpy as jnp
from jax import lax
from jax.experimental import pallas as pl
from jax.experimental.pallas import tpu as pltpu
from jax.sharding import PartitionSpec as P

BUCKET_EDGES = tuple(int(math.ceil(16.0 * 8.0 ** (bucket_step / 16.0))) for bucket_step in range(1, 16))
NEG_FILL = -1e30
STEP_ROWS = 32
LANES = 128
F32 = jnp.float32
BF16 = jnp.bfloat16


def rms_norm(values, norm_scale):
    inv_rms = lax.rsqrt(jnp.mean(values * values, axis=-1, keepdims=True) + 1e-6)
    return (values * inv_rms * norm_scale.astype(F32)).astype(BF16)


def dot(a, b):
    return jnp.dot(a, b, preferred_element_type=F32)


def dot_nt(a, b):
    return lax.dot_general(a, b, (((1,), (1,)), ((), ())), preferred_element_type=F32)


def iota(shape, axis):
    return lax.broadcasted_iota(jnp.int32, shape, axis)


def self_kernel(heads, head_dim, pos_ref, bias_ref, x_ref, wq_ref, wk_ref, wv_ref, norm_ref, k_ref, v_ref,
                mixed_ref, ko_ref, vo_ref, q_s, kt_s, vt_s, table_s, score_s, out_s):
    step = pl.program_id(0)
    flat = heads * head_dim
    rows_total = x_ref.shape[0]

    @pl.when(step == 0)
    def _():
        lane = iota((4 * heads, LANES), 1)
        head_of = lax.rem(iota((4 * heads, LANES), 0), heads)
        far = jnp.full_like(lane, 16)
        for edge in BUCKET_EDGES:
            far = far + jnp.where(lane >= edge, 1, 0)
        bucket = jnp.where(lane < 16, lane, far)
        table = jnp.zeros((4 * heads, LANES), F32)
        for b in range(32):
            here = jnp.zeros((4 * heads, LANES), F32)
            for h in range(heads):
                here = jnp.where(head_of == h, bias_ref[h, b], here)
            table = jnp.where(bucket == b, here, table)
        table_s[...] = table

        @pl.loop(0, rows_total // LANES)
        def _(g):
            rows = pl.ds(pl.multiple_of(g * LANES, LANES), LANES)
            normed = rms_norm(x_ref[rows, :].astype(F32), norm_ref[...])
            q_s[rows, :] = dot(normed, wq_ref[...]).astype(BF16)
            kt_s[g] = dot(normed, wk_ref[...]).astype(BF16).astype(F32).T
            vt_s[g] = dot(normed, wv_ref[...]).astype(BF16).astype(F32).T

    n = STEP_ROWS
    first = pl.multiple_of(step * n, n)
    per = LANES // n
    group, part = step // per, lax.rem(step, per)
    shift = lax.rem(LANES - part * n, LANES)
    k_new = pltpu.roll(kt_s[group], shift, 1)
    v_new = pltpu.roll(vt_s[group], shift, 1)

    spread = jnp.where(iota((n * heads, n), 0) // heads == iota((n * heads, n), 1), 1.0, 0.0).astype(BF16)
    own_head = iota((n * heads, flat), 1) // head_dim == lax.rem(iota((n * heads, flat), 0), heads)
    q_rows = jnp.where(own_head, dot(spread, q_s[pl.ds(first, n), :]), 0.0).astype(BF16)

    lane_bf = iota((flat, LANES), 1).astype(F32).astype(BF16)
    quad_row = iota((4 * heads, LANES), 0)
    table = table_s[...]

    def update(cache_ref, new_cols, out_ref, b):
        at_pos = lane_bf == pos_ref[first + b].astype(F32).astype(BF16)
        col = jnp.broadcast_to(new_cols[:, b:b + 1], (flat, LANES)).astype(BF16)
        updated = jnp.where(at_pos, col, cache_ref[b])
        out_ref[b] = updated
        return updated

    for g in range(n // 4):
        lhs = q_rows[4 * heads * g:4 * heads * (g + 1), :]
        picked = None
        distance = None
        for half in range(2):
            b = 4 * g + 2 * half
            pair = jnp.concatenate([update(k_ref, k_new, ko_ref, b), update(k_ref, k_new, ko_ref, b + 1)], axis=1)
            both = dot(lhs, pair)
            for j in range(2):
                mine = both[:, LANES * j:LANES * (j + 1)]
                at = 2 * half + j
                pos = pos_ref[first + 4 * g + at]
                picked = mine if picked is None else jnp.where(quad_row >= heads * at, mine, picked)
                distance = jnp.full((4 * heads, LANES), pos, jnp.int32) if distance is None else jnp.where(quad_row >= heads * at, pos, distance)
        distance = distance - iota((4 * heads, LANES), 1)
        bias = jnp.take_along_axis(table, jnp.maximum(distance, 0), axis=1)
        score_s[4 * heads * g:4 * heads * (g + 1), :] = jnp.where(distance >= 0, picked + bias, NEG_FILL)

    scores = score_s[...]
    exps = jnp.exp(scores - jnp.max(scores, axis=1, keepdims=True))
    probs = exps * pl.reciprocal(jnp.sum(exps, axis=1, keepdims=True))

    for g in range(n // 4):
        quad = probs[4 * heads * g:4 * heads * (g + 1), :]
        picked = None
        for half in range(2):
            b = 4 * g + 2 * half
            pair = jnp.concatenate([update(v_ref, v_new, vo_ref, b), update(v_ref, v_new, vo_ref, b + 1)], axis=1)
            low = jnp.where(quad_row // heads == 2 * half, quad, 0.0)
            high = jnp.where(quad_row // heads == 2 * half + 1, quad, 0.0)
            lhs = jnp.concatenate([low, high], axis=1).astype(BF16)
            both = dot_nt(lhs, pair)
            picked = both if half == 0 else jnp.where(iota(both.shape, 0) >= 2 * heads, both, picked)
        out_s[4 * heads * g:4 * heads * (g + 1), :] = picked
    gather = jnp.where(iota((n, n * heads), 1) // heads == iota((n, n * heads), 0), 1.0, 0.0).astype(BF16)
    mixed_ref[...] = dot(gather, jnp.where(own_head, out_s[...], 0.0).astype(BF16)).astype(BF16)


def self_attention(tok_pos, bias_t, x_in, w_q, w_k, w_v, norm_self, keys, values, heads):
    rows, flat, t_len = keys.shape
    d_model = x_in.shape[1]
    n = STEP_ROWS
    smem = pl.BlockSpec(memory_space=pltpu.SMEM)
    whole = lambda *shape: pl.BlockSpec(shape, lambda i: (0,) * len(shape))
    cache = pl.BlockSpec((n, flat, t_len), lambda i: (i, 0, 0))
    cache_shape = jax.ShapeDtypeStruct(keys.shape, BF16)
    return pl.pallas_call(
        functools.partial(self_kernel, heads, flat // heads),
        grid=(rows // n,),
        in_specs=[smem, smem, whole(rows, d_model), whole(d_model, flat), whole(d_model, flat), whole(d_model, flat),
                  whole(1, d_model), cache, cache],
        out_specs=[pl.BlockSpec((n, flat), lambda i: (i, 0)), cache, cache],
        out_shape=[jax.ShapeDtypeStruct((rows, flat), BF16), cache_shape, cache_shape],
        scratch_shapes=[
            pltpu.VMEM((rows, flat), BF16),
            pltpu.VMEM((rows // LANES, flat, LANES), F32),
            pltpu.VMEM((rows // LANES, flat, LANES), F32),
            pltpu.VMEM((4 * heads, LANES), F32),
            pltpu.VMEM((n * heads, LANES), F32),
            pltpu.VMEM((n * heads, flat), F32),
        ],
        compiler_params=pltpu.CompilerParams(dimension_semantics=('arbitrary',), vmem_limit_bytes=48 * 1024 * 1024),
        cost_estimate=pl.CostEstimate(flops=4 * rows * flat * t_len * 16 + 6 * rows * d_model * flat, bytes_accessed=8 * rows * flat * t_len, transcendentals=rows * heads * t_len),
        name='self_attention',
    )(tok_pos, bias_t, x_in, w_q, w_k, w_v, norm_self.reshape(1, d_model), keys, values)


def attend(queries, keys_all, values_all, extra):
    scores = jnp.einsum('bhk,bthk->bht', queries, keys_all, preferred_element_type=jnp.float32) + extra
    probs_bf = jax.nn.softmax(scores, axis=-1).astype(jnp.bfloat16)
    mixed_out = jnp.einsum('bht,bthk->bhk', probs_bf, values_all, preferred_element_type=jnp.float32)
    return mixed_out.astype(jnp.bfloat16)


def solution(mesh):
    def tp_sum(partial_out):
        return lax.psum(partial_out.astype(jnp.bfloat16), 'tp').astype(jnp.float32)

    def local_layer(x_in, tok_pos, self_k, self_v, cross_k, cross_v, enc_mask, rel_bias, w_q, w_k, w_v, w_o, cross_q, cross_o, w_gate, w_up, w_down, norm_self, norm_cross, norm_mlp):
        rows, t_len, heads, head_dim = self_k.shape
        flat = heads * head_dim
        head_shape = (rows, heads, head_dim)
        to_kernel = lambda c: jnp.transpose(c, (0, 2, 3, 1)).reshape(rows, flat, t_len)
        from_kernel = lambda c: jnp.transpose(c.reshape(rows, heads, head_dim, t_len), (0, 3, 1, 2))
        mixed_self, new_k, new_v = self_attention(tok_pos, rel_bias.T, x_in, w_q, w_k, w_v, norm_self, to_kernel(self_k), to_kernel(self_v), heads)
        residual = x_in.astype(F32)
        residual = residual + tp_sum(dot(mixed_self, w_o))
        normed = rms_norm(residual, norm_cross)
        cross_queries = dot(normed, cross_q).astype(BF16).reshape(head_shape)
        cross_extra = jnp.where(enc_mask[:, None, :] != 0, 0.0, NEG_FILL)
        mixed_cross = attend(cross_queries, cross_k, cross_v, cross_extra)
        residual = residual + tp_sum(dot(mixed_cross.reshape(rows, flat), cross_o))
        normed = rms_norm(residual, norm_mlp)
        gate_pre = dot(normed, w_gate)
        up_pre = dot(normed, w_up)
        hidden = (jax.nn.gelu(gate_pre, approximate=True) * up_pre).astype(BF16)
        residual = residual + tp_sum(dot(hidden, w_down))
        return residual.astype(BF16), from_kernel(new_k), from_kernel(new_v)

    cache_spec = P('dp', None, 'tp', None)
    split_cols = P(None, 'tp')
    split_rows = P('tp', None)
    in_specs = (P('dp', None), P('dp'), cache_spec, cache_spec, cache_spec, cache_spec, P('dp', None), split_cols, split_cols, split_cols, split_cols, split_rows, split_cols, split_rows, split_cols, split_cols, split_rows, P(None), P(None), P(None))
    out_specs = (P('dp', None), cache_spec, cache_spec)
    return jax.shard_map(local_layer, mesh=mesh, in_specs=in_specs, out_specs=out_specs, check_vma=False)
```

time: 572 us -> 244 us (0.43)
  local copies, waits for them, and re-layouts: 258 us -> 10.2 us
  other arithmetic: 160 us -> 30 us
  Pallas kernels: 0 us -> 58.7 us
  matrix products: 24.4 us -> 16.3 us
    gather x1 -> x0, local copies, waits for them, and re-layouts: 216 us -> none  [self_terms(): jnp.take(rel_bias, rel_bucket(distance), axis=0)]
    unnamed x3 -> x1, other arithmetic: 97.4 us -> 8.22 us
    pallas_call x0 -> x1, Pallas kernels: none -> 58.7 us  [self_attention(): pl.pallas_call(functools.partial(self_kernel, heads, flat // heads), grid...]
    div x2 -> x1, other arithmetic: 35.1 us -> 2.02 us  [attend(): probs_bf = jax.nn.softmax(scores, axis=-1).astype(jnp.bfloat16)]
    dot_general x2 -> x0, local copies, waits for them, and re-layouts: 17.5 us -> none  [the longest x1 16.2 us: attend(): jnp.einsum('bhk,bthk->bht', queries, keys_all, preferred_element_type=jnp...]
    unnamed x52 -> x39, local copies, waits for them, and re-layouts: 22.8 us -> 9.38 us
    dot_general x8 -> x5, matrix products: 24.4 us -> 16.3 us  [dot(): return jnp.dot(a, b, preferred_element_type=F32)]
where the time goes in v1:
time: 244 us
  waiting for transfers between devices  114 us (47%)
  Pallas kernels  58.7 us (24%)
  other arithmetic  30 us (12%)
  matrix products  16.3 us (7%)
  between operations  13.9 us (6%)
  local copies, waits for them, and re-layouts  10.2 us (4%)
    psum x3, waiting for transfers between devices, tp_sum(): return lax.psum(partial_out.astype(jnp.bfloat16), 'tp').astype(jnp.float32)  114 us
    pallas_call x1, Pallas kernels, self_attention(): pl.pallas_call(functools.partial(self_kernel, heads, flat // heads), grid...  58.7 us
    dot_general x5, matrix products, dot(): return jnp.dot(a, b, preferred_element_type=F32)  16.3 us
    unnamed x39, local copies, waits for them, and re-layouts  9.38 us
    unnamed x1, other arithmetic  8.22 us
    dot_general x1, other arithmetic, attend(): jnp.einsum('bht,bthk->bhk', probs_bf, values_all, preferred_element_type=...  7.52 us
    reduce_sum x2, other arithmetic, rms_norm(): jnp.mean(values * values, axis=-1, keepdims=True) + 1e-06  5.9 us
  transfers between devices with their start and end apart: 3, of which 3 were waited for; matrix products, arithmetic and copies ran while one was open for 0% of the time, Pallas kernels for 0%

profile of v1, /device:TPU:0, one launch (start us, length us, event | category | flops | bytes accessed | tf_op | source)
XLA Modules:
  0.0 243.7 jit_solution(3776413766936082877)
XLA Ops:
  7.2 0.0 all-reduce.4.cloned.1.call-start
  7.2 0.8 reshape.50.norm_ref
  8.1 1.4 copy-done.1
  9.5 1.1 copy-done.4
  10.6 1.1 copy-done.5
  11.8 1.1 copy-done.6
  12.9 0.7 copy-done.7
  13.6 0.7 copy-done.8
  14.3 58.7 %self_attention.1 = (bf16[512,256]{1,0:T(8,128)(2,1)S(1)}, bf16[512,256,128]{2,1,0:T(8,128)(2,1)}, bf16[512,256,128]{2,1,0:T(8,128)(2,1)}) custom-call(s32[512]{0:T(512)S(1)} %copy-done.7, f32[4,32]{1,0:T(4,128)S(1)} %bitcast.30, bf16[512,1536]{1,0:T(8,128)(2,1)S(1)} %copy-done.1, bf16[1536,256]{1,0:T(8,128)(2,1)S(1)} %copy-done.4, ...), custom_call_target="tpu_custom_call" | custom-call | flops 2281701376 | bytes 134217728 | tf_op jit(solution)/shard_map/self_attention/pallas_call | solution.py:134
  73.0 1.7 convolution_convert_fusion.2
  74.7 0.0 all-reduce.4.cloned.1.call-update
  74.7 0.0 all-reduce.6.cloned.1.call-start
  74.8 0.7 compare_select_fusion
  75.5 39.5 %all-reduce.4.cloned.1.call-done = bf16[512,1536]{1,0:T(8,128)(2,1)} async-done(((bf16[512,1536]{1,0:T(8,128)(2,1)}), bf16[512,1536]{1,0:T(8,128)(2,1)}) %all-reduce.4.cloned.1.call-update) | async-done | bytes 1572880 | tf_op jit(solution)/shard_map/psum | solution.py:164
  115.0 2.6 %multiply_reduce_fusion.3 = f32[512]{0:T(512)S(1)} fusion(bf16[512,1536]{1,0:T(8,128)(2,1)} %all-reduce.4.cloned.1.call-done, bf16[512,1536]{1,0:T(8,128)(2,1)} %x_ref.1), kind=kLoop, calls=%fused_computation.9 | loop fusion | flops 3931648 | bytes 3147776 | tf_op jit(solution)/shard_map/reduce_sum | solution.py:19
  117.6 0.2 copy-done.9
  117.8 2.0 bitcast_convert_fusion
  119.9 8.2 %multiply_reduce_fusion.1 = f32[512,4,64]{0,1,2:T(4,128)S(1)} fusion(f32[512,4,64]{0,2,1:T(8,128)S(1)} %bitcast_convert_fusion, bf16[512,64,4,64]{0,3,2,1:T(8,128)(2,1)} %param.24), kind=kLoop, calls=%fused_computation.3 | loop fusion | flops 25034752 | bytes 17825792
  128.1 2.0 fusion.18
  130.1 1.4 copy.39
  131.5 7.5 %multiply_reduce_fusion = bf16[512,4,64]{0,2,1:T(8,128)(2,1)S(1)} fusion(f32[512,4,64]{0,1,2:T(4,128)S(1)} %copy.39, bf16[512,64,4,64]{0,3,2,1:T(8,128)(2,1)} %param.25), kind=kLoop, calls=%fused_computation.2 | loop fusion | flops 25034752 | bytes 17563648 | tf_op jit(solution)/shard_map/bht,bthk->bhk/dot_general | solution.py:158
  139.1 1.7 convolution_convert_fusion.1
  140.8 0.2 all-reduce.8.cloned.1.call-start
  141.1 37.2 %all-reduce.6.cloned.1.call-done = bf16[512,1536]{1,0:T(8,128)(2,1)} async-done(((bf16[512,1536]{1,0:T(8,128)(2,1)}), bf16[512,1536]{1,0:T(8,128)(2,1)}) %all-reduce.6.cloned.1.call-update) | async-done | bytes 1572880 | tf_op jit(solution)/shard_map/psum | solution.py:164
  178.3 3.3 %multiply_reduce_fusion.2 = f32[512]{0:T(512)S(1)} fusion(bf16[512,1536]{1,0:T(8,128)(2,1)} %all-reduce.6.cloned.1.call-done, bf16[512,1536]{1,0:T(8,128)(2,1)} %all-reduce.4.cloned.1.call-done, bf16[512,1536]{1,0:T(8,128)(2,1)} %x_ref.1), kind=kLoop, calls=%fused_computation.6 | loop fusion | flops 5504512 | bytes 4720640 | tf_op jit(solution)/shard_map/reduce_sum | solution.py:19
  181.6 0.5 copy-done.11
  182.1 0.9 multiply_convert_fusion
  183.0 1.1 copy-done.12
  184.1 3.0 %fusion.27 = f32[512,960]{0,1:T(8,128)} fusion(bf16[512,1536]{1,0:T(8,128)(2,1)S(1)} %multiply_convert_fusion, bf16[1536,960]{0,1:T(8,128)(2,1)S(1)} %copy-done.18), kind=kOutput, calls=%fused_computation.45 | convolution fusion | flops 1509949440 | bytes 6488064 | tf_op jit(solution)/shard_map/dot_general | solution.py:24
  187.1 7.8 %convolution_convert_fusion = bf16[512,1536]{1,0:T(8,128)(2,1)} fusion(bf16[960,1536]{1,0:T(8,128)(2,1)S(1)} %copy-done, f32[512,960]{0,1:T(8,128)} %fusion.27, bf16[512,1536]{1,0:T(8,128)(2,1)} %copy-done.12, bf16[1536,960]{0,1:T(8,128)(2,1)} %param.35), kind=kOutput, calls=%fused_computation.11 | convolution fusion | flops 3025600512 | bytes 11010048 | tf_op jit(solution)/shard_map/dot_general | solution.py:24
  195.0 37.5 %all-reduce.8.cloned.1.call-done = bf16[512,1536]{1,0:T(8,128)(2,1)} async-done(((bf16[512,1536]{1,0:T(8,128)(2,1)}), bf16[512,1536]{1,0:T(8,128)(2,1)}) %all-reduce.8.cloned.1.call-update) | async-done | bytes 1572880 | tf_op jit(solution)/shard_map/psum | solution.py:164
  232.4 4.8 %add_convert_fusion = bf16[512,1536]{1,0:T(8,128)(2,1)} fusion(bf16[512,1536]{1,0:T(8,128)(2,1)} %all-reduce.8.cloned.1.call-done, bf16[512,1536]{1,0:T(8,128)(2,1)} %all-reduce.6.cloned.1.call-done, bf16[512,1536]{1,0:T(8,128)(2,1)} %all-reduce.4.cloned.1.call-done, bf16[512,1536]{1,0:T(8,128)(2,1)} %x_ref.1), kind=kLoop, calls=%fused_computation.4 | loop fusion | flops 6291456 | bytes 7864320 | tf_op jit(solution)/shard_map/convert_element_type | solution.py:185
  (35 shorter events, 0.1 us)
Async XLA Ops:
  7.2 180.0 %copy-start = (bf16[960,1536]{1,0:T(8,128)(2,1)S(1)}, bf16[960,1536]{1,0:T(8,128)(2,1)}, u32[]{:S(2)}) copy-start(bf16[960,1536]{1,0:T(8,128)(2,1)} %param.36) | copy-start | bytes 8847364
  7.2 107.8 %all-reduce.4.cloned.1.call-start = ((), (), s32[]{:S(2)}) async-start(), calls=%async_computation | async-start | bytes 3145728 | tf_op jit(solution)/shard_map/psum | solution.py:164
  8.1 1.4 copy-start.1
  9.5 1.1 copy-start.4
  10.6 1.1 copy-start.5
  11.8 1.1 copy-start.6
  12.9 0.7 copy-start.7
  13.6 0.7 copy-start.8
  14.2 58.7 %copy-start.13 = (bf16[256,1536]{1,0:T(8,128)(2,1)S(1)}, bf16[256,1536]{1,0:T(8,128)(2,1)}, u32[]{:S(2)}) copy-start(bf16[256,1536]{1,0:T(8,128)(2,1)} %param.31) | copy-start | bytes 2359300
  73.0 1.8 copy-start.16
  73.0 1.8 copy-start.15
  74.7 103.6 %all-reduce.6.cloned.1.call-start = ((), (), s32[]{:S(2)}) async-start(), calls=%async_computation.1 | async-start | bytes 3145728 | tf_op jit(solution)/shard_map/psum | solution.py:164
  115.0 2.6 %copy-start.2 = (bf16[512,1536]{1,0:T(8,128)(2,1)S(1)}, bf16[512,1536]{1,0:T(8,128)(2,1)}, u32[]{:S(2)}) copy-start(bf16[512,1536]{1,0:T(8,128)(2,1)} %x_ref.1) | copy-start | bytes 4718596
  115.0 2.8 %copy-start.9 = (bf16[512,1536]{1,0:T(8,128)(2,1)S(1)}, bf16[512,1536]{1,0:T(8,128)(2,1)}, u32[]{:S(2)}) copy-start(bf16[512,1536]{1,0:T(8,128)(2,1)} %all-reduce.4.cloned.1.call-done) | copy-start | bytes 4718596
  131.5 7.6 %copy-start.14 = (bf16[256,1536]{1,0:T(8,128)(2,1)S(1)}, bf16[256,1536]{1,0:T(8,128)(2,1)}, u32[]{:S(2)}) copy-start(bf16[256,1536]{1,0:T(8,128)(2,1)} %param.33) | copy-start | bytes 2359300
  139.0 2.0 copy-start.17
  140.8 91.6 %all-reduce.8.cloned.1.call-start = ((), (), s32[]{:S(2)}) async-start(), calls=%async_computation.2 | async-start | bytes 3145728 | tf_op jit(solution)/shard_map/psum | solution.py:164
  178.3 3.3 %copy-start.3 = (bf16[512,1536]{1,0:T(8,128)(2,1)S(1)}, bf16[512,1536]{1,0:T(8,128)(2,1)}, u32[]{:S(2)}) copy-start(bf16[512,1536]{1,0:T(8,128)(2,1)} %x_ref.1) | copy-start | bytes 4718596
  178.3 3.3 %copy-start.10 = (bf16[512,1536]{1,0:T(8,128)(2,1)S(1)}, bf16[512,1536]{1,0:T(8,128)(2,1)}, u32[]{:S(2)}) copy-start(bf16[512,1536]{1,0:T(8,128)(2,1)} %all-reduce.4.cloned.1.call-done) | copy-start | bytes 4718596
  178.3 3.8 %copy-start.11 = (bf16[512,1536]{1,0:T(8,128)(2,1)S(1)}, bf16[512,1536]{1,0:T(8,128)(2,1)}, u32[]{:S(2)}) copy-start(bf16[512,1536]{1,0:T(8,128)(2,1)} %all-reduce.6.cloned.1.call-done) | copy-start | bytes 4718596
  182.1 2.1 copy-start.18
  183.0 1.1 copy-start.12
Sparse Core Ops, SparseCore 0:
  74.9 40.0 all-reduce.3
  140.9 37.2 all-reduce.5
  195.1 37.3 all-reduce.7

commit v2 on v1

--- a/solution.py
+++ b/solution.py
@@ -146,43 +146,309 @@
             pltpu.VMEM((n * heads, LANES), F32),
             pltpu.VMEM((n * heads, flat), F32),
         ],
-        compiler_params=pltpu.CompilerParams(dimension_semantics=('arbitrary',), vmem_limit_bytes=48 * 1024 * 1024),
+        compiler_params=pltpu.CompilerParams(dimension_semantics=('arbitrary',), vmem_limit_bytes=63 * 1024 * 1024),
         cost_estimate=pl.CostEstimate(flops=4 * rows * flat * t_len * 16 + 6 * rows * d_model * flat, bytes_accessed=8 * rows * flat * t_len, transcendentals=rows * heads * t_len),
         name='self_attention',
     )(tok_pos, bias_t, x_in, w_q, w_k, w_v, norm_self.reshape(1, d_model), keys, values)
 
 
-def attend(queries, keys_all, values_all, extra):
-    scores = jnp.einsum('bhk,bthk->bht', queries, keys_all, preferred_element_type=jnp.float32) + extra
-    probs_bf = jax.nn.softmax(scores, axis=-1).astype(jnp.bfloat16)
-    mixed_out = jnp.einsum('bht,bthk->bhk', probs_bf, values_all, preferred_element_type=jnp.float32)
-    return mixed_out.astype(jnp.bfloat16)
+CHUNK = 128
+MESH = pl.DeviceIdType.MESH
+
+
+def rest_kernel(heads, n_cross_slots,
+                x_ref, mixed_ref, wo_ref, wox_ref, co_ref, cox_ref, cq_ref, gate_ref, up_ref, down_ref, norm_c_ref, norm_m_ref,
+                mask_ref, ck_ref, cv_ref, out_ref,
+                x_s, res_s, mix_s, cmix_s, wo_s, co_s, cq_s, gate_s, up_s, down_s, k_s, v_s, mask_s,
+                qt_s, score_s, hid_s, part_s, near_s, chip_s, far_s, done_s,
+                ag_send, ag_recv, w_send, w_recv, sum_send, sum_recv, load_sem, cross_sem, out_sem):
+    me = lax.axis_index('tp')
+    core = lax.rem(me, 2)
+    mate = me + 1 - 2 * core
+    over = lax.rem(me + 2, 4)
+    cater = lax.rem(mate + 2, 4)
+    rows_total, d_model = x_ref.shape
+    flat = mixed_ref.shape[1]
+    head_dim = flat // heads
+    src_len = ck_ref.shape[0]
+    d_ff = gate_ref.shape[0]
+    chunks = rows_total // CHUNK
+    half = CHUNK // 2
+
+    def remote(src, dst, send_sem, recv_sem, to):
+        return pltpu.make_async_remote_copy(src_ref=src, dst_ref=dst, send_sem=send_sem, recv_sem=recv_sem,
+                                            device_id={'tp': to}, device_id_type=MESH)
+
+    def block(buf, who, c):
+        return buf.at[who, pl.ds(CHUNK * c, CHUNK), :]
+
+    def shard(buf, who):
+        return buf.at[pl.ds(pl.multiple_of(who * flat, flat), flat), :]
+
+    loads = []
+
+    def load(src, dst):
+        copy = pltpu.make_async_copy(src, dst, load_sem.at[len(loads)])
+        copy.start()
+        loads.append(copy)
+        return copy
+
+    def cross_load(c):
+        slot = c % n_cross_slots
+        cols = pl.ds(CHUNK * c, CHUNK)
+        return (pltpu.make_async_copy(ck_ref.at[:, :, cols], k_s.at[slot], cross_sem.at[0, slot]),
+                pltpu.make_async_copy(cv_ref.at[:, :, cols], v_s.at[slot], cross_sem.at[1, slot]))
+
+    own_mixed = load(mixed_ref, mix_s.at[me])
+    x_load = load(x_ref, x_s)
+    own_wo = (load(wo_ref, shard(wo_s, me)), load(wox_ref, shard(wo_s, over)))
+    q_load = load(cq_ref, cq_s)
+    mask_load = load(mask_ref, mask_s)
+    first_cross = cross_load(0)
+    for copy in first_cross:
+        copy.start()
+    own_co = (load(co_ref, shard(co_s, me)), load(cox_ref, shard(co_s, over)))
+    mlp_loads = (load(gate_ref, gate_s), load(up_ref, up_s), load(down_ref, down_s))
+    for c in range(1, n_cross_slots):
+        for copy in cross_load(c):
+            copy.start()
+
+    barrier = pltpu.get_barrier_semaphore()
+    for peer in (mate, over):
+        pl.semaphore_signal(barrier, inc=1, device_id={'tp': peer}, device_id_type=MESH)
+    pl.semaphore_wait(barrier, 2)
+
+    sends = []
+
+    def send(copy):
+        copy.start()
+        sends.append(copy)
+
+    def gather_send(stage, src, buf, c):
+        send(remote(src, block(buf, me, c), ag_send.at[stage, 0, c], ag_recv.at[stage, 0, c], over))
+        send(remote(src, block(buf, me, c), ag_send.at[stage, 1, c], ag_recv.at[stage, 1, c], mate))
+
+    def gather_relay(stage, buf, c):
+        remote(block(buf, over, c), block(buf, over, c), ag_send.at[stage, 0, c], ag_recv.at[stage, 0, c], over).wait_recv()
+        send(remote(block(buf, over, c), block(buf, over, c), ag_send.at[stage, 2, c], ag_recv.at[stage, 2, c], mate))
+
+    def gather_wait(stage, buf, c):
+        remote(block(buf, mate, c), block(buf, mate, c), ag_send.at[stage, 1, c], ag_recv.at[stage, 1, c], mate).wait_recv()
+        remote(block(buf, cater, c), block(buf, cater, c), ag_send.at[stage, 2, c], ag_recv.at[stage, 2, c], mate).wait_recv()
+
+    def weight_send(which, ref, ref_x, buf):
+        send(remote(ref, shard(buf, me), w_send.at[which, 0], w_recv.at[which, 0], mate))
+        send(remote(ref_x, shard(buf, over), w_send.at[which, 1], w_recv.at[which, 1], mate))
+
+    def weight_wait(which, buf):
+        remote(shard(buf, mate), shard(buf, mate), w_send.at[which, 0], w_recv.at[which, 0], mate).wait_recv()
+        remote(shard(buf, cater), shard(buf, cater), w_send.at[which, 1], w_recv.at[which, 1], mate).wait_recv()
+
+    for c in range(chunks):
+        gather_send(0, mixed_ref.at[pl.ds(CHUNK * c, CHUNK), :], mix_s, c)
+    weight_send(0, wo_ref, wox_ref, wo_s)
+
+    def project_heads(buf, weight, c, add_to):
+        lhs = jnp.concatenate([buf[i, CHUNK * c:CHUNK * (c + 1), :] for i in range(4)], axis=1)
+        for n in range(0, d_model, 512):
+            res_s[CHUNK * c:CHUNK * (c + 1), n:n + 512] = add_to[CHUNK * c:CHUNK * (c + 1), n:n + 512].astype(F32) + dot(lhs, weight[:, n:n + 512])
+
+    def cross_query(c):
+        if c == 0:
+            own_mixed.wait()
+            x_load.wait()
+            for copy in own_wo:
+                copy.wait()
+        gather_wait(0, mix_s, c)
+        if c == 0:
+            weight_wait(0, wo_s)
+            q_load.wait()
+        project_heads(mix_s, wo_s, c, x_s)
+        normed = rms_norm(res_s[CHUNK * c:CHUNK * (c + 1), :], norm_c_ref[...])
+        qt_s[...] = dot(normed, cq_s[...]).astype(BF16).astype(F32).T
+
+    def cross_attend(c):
+        slot = c % n_cross_slots
+        for copy in cross_load(c):
+            copy.wait()
+        if c == 0:
+            mask_load.wait()
+        step = 8
+
+        @pl.loop(0, src_len // step)
+        def _(i):
+            at = pl.ds(pl.multiple_of(i * step, step), step)
+            for h in range(heads):
+                d = slice(head_dim * h, head_dim * (h + 1))
+                score_s[h, at, :] = jnp.sum(k_s[slot, at, d, :].astype(F32) * qt_s[d, :][None], axis=1)
+
+        valid = mask_s[:, CHUNK * c:CHUNK * (c + 1)] != 0
+        for h in range(heads):
+            scores = jnp.where(valid, score_s[h], NEG_FILL)
+            exps = jnp.exp(scores - jnp.max(scores, axis=0, keepdims=True))
+            probs = exps * pl.reciprocal(jnp.sum(exps, axis=0, keepdims=True))
+            score_s[h] = probs.astype(BF16).astype(F32)
+
+        def mix(i, acc):
+            acc = list(acc)
+            for j in range(step):
+                s = i * step + j
+                for h in range(heads):
+                    d = slice(head_dim * h, head_dim * (h + 1))
+                    acc[h] = acc[h] + v_s[slot, s, d, :].astype(F32) * score_s[h, pl.ds(s, 1), :]
+            return tuple(acc)
+
+        zero = jnp.zeros((head_dim, CHUNK), F32)
+        acc = lax.fori_loop(0, src_len // step, mix, (zero,) * heads)
+        cmix_s[me, CHUNK * c:CHUNK * (c + 1), :] = jnp.concatenate(acc, axis=0).T.astype(BF16)
+        gather_send(1, block(cmix_s, me, c), cmix_s, c)
+        if c + n_cross_slots < chunks:
+            for copy in cross_load(c + n_cross_slots):
+                copy.start()
+
+    def mlp(c):
+        if c == 0:
+            for copy in own_co:
+                copy.wait()
+            weight_wait(1, co_s)
+        gather_wait(1, cmix_s, c)
+        project_heads(cmix_s, co_s, c, res_s)
+        if c == 0:
+            for copy in mlp_loads:
+                copy.wait()
+        normed = rms_norm(res_s[CHUNK * c:CHUNK * (c + 1), :], norm_m_ref[...])
+        for n in range(0, d_ff, 256):
+            end = min(d_ff, n + 256)
+            gate = dot_nt(normed, gate_s[n:end, :])
+            up = dot_nt(normed, up_s[n:end, :])
+            hid_s[:, n:end] = (jax.nn.gelu(gate, approximate=True) * up).astype(BF16)
+        hidden = hid_s[...]
+        for n in range(0, d_model, 512):
+            part_s[c, :, n:n + 512] = dot(hidden, down_s[:, n:n + 512]).astype(BF16)
+        give = pl.ds(pl.multiple_of((1 - core) * half, half), half)
+        send(remote(part_s.at[c, give, :], near_s.at[c], sum_send.at[0, c], sum_recv.at[0, c], mate))
+
+    keep = pl.ds(pl.multiple_of(core * half, half), half)
+
+    def chip_sum(c):
+        remote(near_s.at[c], near_s.at[c], sum_send.at[0, c], sum_recv.at[0, c], mate).wait_recv()
+        chip_s[c] = (part_s[c, keep, :].astype(F32) + near_s[c].astype(F32)).astype(BF16)
+        send(remote(chip_s.at[c], far_s.at[c], sum_send.at[1, c], sum_recv.at[1, c], over))
+
+    def full_sum(c):
+        remote(far_s.at[c], far_s.at[c], sum_send.at[1, c], sum_recv.at[1, c], over).wait_recv()
+        mine = pl.ds(pl.multiple_of(CHUNK * c + core * half, half), half)
+        done_s[mine, :] = (res_s[mine, :] + (chip_s[c].astype(F32) + far_s[c].astype(F32))).astype(BF16)
+        send(remote(done_s.at[mine, :], done_s.at[mine, :], sum_send.at[2, c], sum_recv.at[2, c], mate))
+
+    def store(c):
+        other = pl.ds(pl.multiple_of(CHUNK * c + (1 - core) * half, half), half)
+        remote(done_s.at[other, :], done_s.at[other, :], sum_send.at[2, c], sum_recv.at[2, c], mate).wait_recv()
+        rows = pl.ds(CHUNK * c, CHUNK)
+        copy = pltpu.make_async_copy(done_s.at[rows, :], out_ref.at[rows, :], out_sem.at[c])
+        copy.start()
+        return copy
+
+    for c in range(chunks):
+        gather_relay(0, mix_s, c)
+        if c == 0:
+            cross_query(0)
+    weight_send(1, co_ref, cox_ref, co_s)
+    cross_attend(0)
+    cross_query(1)
+    gather_relay(1, cmix_s, 0)
+    cross_attend(1)
+    mlp(0)
+    cross_query(2)
+    gather_relay(1, cmix_s, 1)
+    chip_sum(0)
+    cross_attend(2)
+    mlp(1)
+    cross_query(3)
+    gather_relay(1, cmix_s, 2)
+    chip_sum(1)
+    cross_attend(3)
+    mlp(2)
+    full_sum(0)
+    gather_relay(1, cmix_s, 3)
+    chip_sum(2)
+    mlp(3)
+    full_sum(1)
+    stores = [store(0)]
+    chip_sum(3)
+    full_sum(2)
+    stores.append(store(1))
+    full_sum(3)
+    stores.append(store(2))
+    stores.append(store(3))
+    for copy in stores:
+        copy.wait()
+    for copy in sends:
+        copy.wait_send()
+
+
+def rest_of_layer(x_in, mixed, w_o, w_o_over, cross_o, cross_o_over, cross_q, gate_t, up_t, w_down, norm_cross, norm_mlp, mask_t, cross_k, cross_v, heads):
+    rows, d_model = x_in.shape
+    flat = mixed.shape[1]
+    d_ff = gate_t.shape[0]
+    src_len = cross_k.shape[0]
+    chunks = rows // CHUNK
+    slots = 3
+    anywhere = pl.BlockSpec(memory_space=pl.ANY)
+    vmem = pl.BlockSpec(memory_space=pltpu.VMEM)
+    dma = pltpu.SemaphoreType.DMA
+    return pl.pallas_call(
+        functools.partial(rest_kernel, heads, slots),
+        in_specs=[anywhere] * 10 + [vmem, vmem] + [anywhere] * 3,
+        out_specs=anywhere,
+        out_shape=jax.ShapeDtypeStruct((rows, d_model), BF16),
+        scratch_shapes=[
+            pltpu.VMEM((rows, d_model), BF16),
+            pltpu.VMEM((rows, d_model), F32),
+            pltpu.VMEM((4, rows, flat), BF16),
+            pltpu.VMEM((4, rows, flat), BF16),
+            pltpu.VMEM((4 * flat, d_model), BF16),
+            pltpu.VMEM((4 * flat, d_model), BF16),
+            pltpu.VMEM((d_model, flat), BF16),
+            pltpu.VMEM((d_ff, d_model), BF16),
+            pltpu.VMEM((d_ff, d_model), BF16),
+            pltpu.VMEM((d_ff, d_model), BF16),
+            pltpu.VMEM((slots, src_len, flat, CHUNK), BF16),
+            pltpu.VMEM((slots, src_len, flat, CHUNK), BF16),
+            pltpu.VMEM((src_len, rows), jnp.int32),
+            pltpu.VMEM((flat, CHUNK), F32),
+            pltpu.VMEM((heads, src_len, CHUNK), F32),
+            pltpu.VMEM((CHUNK, d_ff), BF16),
+            pltpu.VMEM((chunks, CHUNK, d_model), BF16),
+            pltpu.VMEM((chunks, CHUNK // 2, d_model), BF16),
+            pltpu.VMEM((chunks, CHUNK // 2, d_model), BF16),
+            pltpu.VMEM((chunks, CHUNK // 2, d_model), BF16),
+            pltpu.VMEM((rows, d_model), BF16),
+            dma((2, 3, chunks)), dma((2, 3, chunks)),
+            dma((2, 2)), dma((2, 2)),
+            dma((3, chunks)), dma((3, chunks)),
+            dma((16,)), dma((2, slots)), dma((chunks,)),
+        ],
+        compiler_params=pltpu.CompilerParams(collective_id=0, has_side_effects=True, vmem_limit_bytes=63 * 1024 * 1024),
+        cost_estimate=pl.CostEstimate(flops=2 * rows * d_model * (8 * flat + flat + 3 * d_ff), bytes_accessed=50_000_000, transcendentals=rows * d_ff),
+        name='rest_of_layer',
+    )(x_in, mixed, w_o, w_o_over, cross_o, cross_o_over, cross_q, gate_t, up_t, w_down, norm_cross.reshape(1, d_model), norm_mlp.reshape(1, d_model), mask_t, cross_k, cross_v)
 
 
 def solution(mesh):
-    def tp_sum(partial_out):
-        return lax.psum(partial_out.astype(jnp.bfloat16), 'tp').astype(jnp.float32)
-
     def local_layer(x_in, tok_pos, self_k, self_v, cross_k, cross_v, enc_mask, rel_bias, w_q, w_k, w_v, w_o, cross_q, cross_o, w_gate, w_up, w_down, norm_self, norm_cross, norm_mlp):
         rows, t_len, heads, head_dim = self_k.shape
         flat = heads * head_dim
-        head_shape = (rows, heads, head_dim)
         to_kernel = lambda c: jnp.transpose(c, (0, 2, 3, 1)).reshape(rows, flat, t_len)
         from_kernel = lambda c: jnp.transpose(c.reshape(rows, heads, head_dim, t_len), (0, 3, 1, 2))
+        cross_view = lambda c: jnp.transpose(c, (1, 2, 3, 0)).reshape(c.shape[1], flat, rows)
+        swap = [(0, 2), (1, 3), (2, 0), (3, 1)]
+        w_o_over = lax.ppermute(w_o, 'tp', swap)
+        cross_o_over = lax.ppermute(cross_o, 'tp', swap)
         mixed_self, new_k, new_v = self_attention(tok_pos, rel_bias.T, x_in, w_q, w_k, w_v, norm_self, to_kernel(self_k), to_kernel(self_v), heads)
-        residual = x_in.astype(F32)
-        residual = residual + tp_sum(dot(mixed_self, w_o))
-        normed = rms_norm(residual, norm_cross)
-        cross_queries = dot(normed, cross_q).astype(BF16).reshape(head_shape)
-        cross_extra = jnp.where(enc_mask[:, None, :] != 0, 0.0, NEG_FILL)
-        mixed_cross = attend(cross_queries, cross_k, cross_v, cross_extra)
-        residual = residual + tp_sum(dot(mixed_cross.reshape(rows, flat), cross_o))
-        normed = rms_norm(residual, norm_mlp)
-        gate_pre = dot(normed, w_gate)
-        up_pre = dot(normed, w_up)
-        hidden = (jax.nn.gelu(gate_pre, approximate=True) * up_pre).astype(BF16)
-        residual = residual + tp_sum(dot(hidden, w_down))
-        return residual.astype(BF16), from_kernel(new_k), from_kernel(new_v)
+        x_out = rest_of_layer(x_in, mixed_self, w_o, w_o_over, cross_o, cross_o_over, cross_q, w_gate.T, w_up.T, w_down, norm_cross, norm_mlp,
+                              enc_mask.T, cross_view(cross_k), cross_view(cross_v), heads)
+        return x_out, from_kernel(new_k), from_kernel(new_v)
 
     cache_spec = P('dp', None, 'tp', None)
     split_cols = P(None, 'tp')

time: 244 us -> 121 us (0.50)
  waiting for transfers between devices: 114 us -> 0.01 us
  Pallas kernels: 58.7 us -> 109 us
  other arithmetic: 30 us -> 0 us
  matrix products: 16.3 us -> 0 us
  between operations: 13.9 us -> 0.66 us
  starting transfers between devices: 0.3 us -> 3.4 us
  local copies, waits for them, and re-layouts: 10.2 us -> 7.37 us
    psum x3 -> x0, waiting for transfers between devices: 114 us -> none  [tp_sum(): return lax.psum(partial_out.astype(jnp.bfloat16), 'tp').astype(jnp.float32)]
    pallas_call x0 -> x1, Pallas kernels: none -> 49.7 us  [rest_of_layer(): pl.pallas_call(functools.partial(rest_kernel, heads, slots), in_specs=[an...]
    dot_general x5 -> x0, matrix products: 16.3 us -> none  [dot(): return jnp.dot(a, b, preferred_element_type=F32)]
    unnamed x1 -> x0, other arithmetic: 8.22 us -> none
    dot_general x1 -> x0, other arithmetic: 7.52 us -> none  [attend(): jnp.einsum('bht,bthk->bhk', probs_bf, values_all, preferred_element_type=...]
    reduce_sum x2 -> x0, other arithmetic: 5.9 us -> none  [rms_norm(): jnp.mean(values * values, axis=-1, keepdims=True) + 1e-06]
    unnamed x39 -> x3, local copies, waits for them, and re-layouts: 9.38 us -> 3.52 us
    convert_element_type x4 -> x0, other arithmetic: 5.67 us -> none  [the longest x1 4.76 us: local_layer(): return (residual.astype(BF16), from_kernel(new_k), from_kernel(new_v))]
  transfers between devices with their start and end apart: 3 -> 2, of which waited for: 3 -> 0; matrix products, arithmetic and copies ran while one was open for 0% -> 3% of each run, Pallas kernels for 0% -> 49%
where the time goes in v2:
time: 121 us
  Pallas kernels  109 us (90%)
  local copies, waits for them, and re-layouts  7.37 us (6%)
  starting transfers between devices  3.4 us (3%)
    pallas_call x1, Pallas kernels, self_attention(): pl.pallas_call(functools.partial(self_kernel, heads, flat // heads), grid...  59.6 us
    pallas_call x1, Pallas kernels, rest_of_layer(): pl.pallas_call(functools.partial(rest_kernel, heads, slots), in_specs=[an...  49.7 us
    unnamed x3, local copies, waits for them, and re-layouts  3.52 us
    ppermute x1, starting transfers between devices, local_layer(): w_o_over = lax.ppermute(w_o, 'tp', swap)  3.36 us
  transfers between devices with their start and end apart: 2, of which 0 were waited for; matrix products, arithmetic and copies ran while one was open for 3% of the time, Pallas kernels for 49%

profile of v2, /device:TPU:0, one launch (start us, length us, event | category | flops | bytes accessed | tf_op | source)
XLA Modules:
  0.0 120.7 jit_solution(9606709373790246343)
XLA Ops:
  0.6 3.4 %collective-permute-start = (bf16[256,1536]{1,0:T(8,128)(2,1)}, bf16[256,1536]{1,0:T(8,128)(2,1)S(1)}, u32[]{:S(2)}, u32[]{:S(2)}) collective-permute-start(bf16[256,1536]{1,0:T(8,128)(2,1)} %wo_ref.1), channel_id=1, source_target_pairs={{0,2},{1,3},{2,0},{3,1},{4,6},{5,7},{6,4},{7,5}} | collective-permute-start | bytes 2359304 | tf_op jit(solution)/shard_map/ppermute | solution.py:446
  4.0 0.0 collective-permute-start.1
  4.0 1.3 %reshape.33.norm_ref = bf16[1,1536]{1,0:T(2,128)(2,1)} reshape(bf16[1536]{0:T(1024)(128)(2,1)} %param.37) | data formatting | bytes 6144 | tf_op jit(solution)/shard_map/reshape | solution.py:152
  5.3 1.3 %reshape.36.norm_c_ref = bf16[1,1536]{1,0:T(2,128)(2,1)} reshape(bf16[1536]{0:T(1024)(128)(2,1)} %param.38) | data formatting | bytes 6144 | tf_op jit(solution)/shard_map/reshape | solution.py:435
  6.6 1.3 %reshape.37.norm_m_ref = bf16[1,1536]{1,0:T(2,128)(2,1)} reshape(bf16[1536]{0:T(1024)(128)(2,1)} %param.39) | data formatting | bytes 6144 | tf_op jit(solution)/shard_map/reshape | solution.py:435
  7.9 59.6 %self_attention.1 = (bf16[512,256]{1,0:T(8,128)(2,1)}, bf16[512,256,128]{2,1,0:T(8,128)(2,1)}, bf16[512,256,128]{2,1,0:T(8,128)(2,1)}) custom-call(s32[512]{0:T(512)} %pos_ref.1, f32[4,32]{1,0:T(4,128)} %bitcast.29, bf16[512,1536]{1,0:T(8,128)(2,1)} %x_ref.3, bf16[1536,256]{1,0:T(8,128)(2,1)} %wq_ref.1, bf16[1536,256]{1,0:T(8,128)(2,1)} %wk_ref.1, ...), custom_call_target="tpu_custom_call" | custom-call | flops 2281701376 | bytes 134217728 | tf_op jit(solution)/shard_map/self_attention/pallas_call | solution.py:134
  67.5 0.0 collective-permute-done.wox_ref
  67.5 0.0 copy-start
  67.5 0.0 collective-permute-done.1.cox_ref
  67.6 0.9 copy-done
  68.4 49.7 %rest_of_layer.1 = bf16[512,1536]{1,0:T(8,128)(2,1)} custom-call(bf16[512,1536]{1,0:T(8,128)(2,1)} %x_ref.3, bf16[512,256]{1,0:T(8,128)(2,1)} %get-tuple-element.6.mixed_ref, bf16[256,1536]{1,0:T(8,128)(2,1)} %wo_ref.1, bf16[256,1536]{1,0:T(8,128)(2,1)} %copy-done, bf16[256,1536]{1,0:T(8,128)(2,1)} %co_ref.1, ...), custom_call_target="tpu_custom_call" | custom-call | flops 8153726976 | bytes 50000000 | tf_op jit(solution)/shard_map/rest_of_layer/pallas_call | solution.py:400
  118.1 2.7 %copy.24 = bf16[512,1536]{1,0:T(8,128)(2,1)} copy(bf16[512,1536]{1,0:T(8,128)(2,1)} %rest_of_layer.1) | data formatting | bytes 3145728
Async XLA Ops:
  0.6 66.9 %collective-permute-start = (bf16[256,1536]{1,0:T(8,128)(2,1)}, bf16[256,1536]{1,0:T(8,128)(2,1)S(1)}, u32[]{:S(2)}, u32[]{:S(2)}) collective-permute-start(bf16[256,1536]{1,0:T(8,128)(2,1)} %wo_ref.1), channel_id=1, source_target_pairs={{0,2},{1,3},{2,0},{3,1},{4,6},{5,7},{6,4},{7,5}} | collective-permute-start | bytes 2359304 | tf_op jit(solution)/shard_map/ppermute | solution.py:446
  4.0 63.6 %collective-permute-start.1 = (bf16[256,1536]{1,0:T(8,128)(2,1)}, bf16[256,1536]{1,0:T(8,128)(2,1)}, u32[]{:S(2)}, u32[]{:S(2)}) collective-permute-start(bf16[256,1536]{1,0:T(8,128)(2,1)} %co_ref.1), channel_id=1, source_target_pairs={{0,2},{1,3},{2,0},{3,1},{4,6},{5,7},{6,4},{7,5}} | collective-permute-start | bytes 2359304 | tf_op jit(solution)/shard_map/ppermute | solution.py:447
  67.5 0.9 copy-start

commit v3 on v2

--- a/solution.py
+++ b/solution.py
@@ -10,6 +10,9 @@
 BUCKET_EDGES = tuple(int(math.ceil(16.0 * 8.0 ** (bucket_step / 16.0))) for bucket_step in range(1, 16))
 NEG_FILL = -1e30
 STEP_ROWS = 32
+SLOTS = 8
+AHEAD = 4
+VMEM_BYTES = 67043328
 LANES = 128
 F32 = jnp.float32
 BF16 = jnp.bfloat16
@@ -33,94 +36,140 @@
 
 
 def self_kernel(heads, head_dim, pos_ref, bias_ref, x_ref, wq_ref, wk_ref, wv_ref, norm_ref, k_ref, v_ref,
-                mixed_ref, ko_ref, vo_ref, q_s, kt_s, vt_s, table_s, score_s, out_s):
-    step = pl.program_id(0)
+                mixed_ref, ko_ref, vo_ref, x_s, wq_s, wk_s, wv_s, k_s, v_s, mixed_s, q_s, kt_s, vt_s, score_s, out_s,
+                load_sem, in_sem, out_sem, mixed_sem):
     flat = heads * head_dim
     rows_total = x_ref.shape[0]
-
-    @pl.when(step == 0)
-    def _():
-        lane = iota((4 * heads, LANES), 1)
-        head_of = lax.rem(iota((4 * heads, LANES), 0), heads)
-        far = jnp.full_like(lane, 16)
-        for edge in BUCKET_EDGES:
-            far = far + jnp.where(lane >= edge, 1, 0)
-        bucket = jnp.where(lane < 16, lane, far)
-        table = jnp.zeros((4 * heads, LANES), F32)
-        for b in range(32):
-            here = jnp.zeros((4 * heads, LANES), F32)
-            for h in range(heads):
-                here = jnp.where(head_of == h, bias_ref[h, b], here)
-            table = jnp.where(bucket == b, here, table)
-        table_s[...] = table
-
-        @pl.loop(0, rows_total // LANES)
-        def _(g):
-            rows = pl.ds(pl.multiple_of(g * LANES, LANES), LANES)
-            normed = rms_norm(x_ref[rows, :].astype(F32), norm_ref[...])
-            q_s[rows, :] = dot(normed, wq_ref[...]).astype(BF16)
-            kt_s[g] = dot(normed, wk_ref[...]).astype(BF16).astype(F32).T
-            vt_s[g] = dot(normed, wv_ref[...]).astype(BF16).astype(F32).T
-
     n = STEP_ROWS
-    first = pl.multiple_of(step * n, n)
-    per = LANES // n
-    group, part = step // per, lax.rem(step, per)
-    shift = lax.rem(LANES - part * n, LANES)
-    k_new = pltpu.roll(kt_s[group], shift, 1)
-    v_new = pltpu.roll(vt_s[group], shift, 1)
+    steps = rows_total // n
+
+    def rows_of(step):
+        return pl.ds(pl.multiple_of(step * n, n), n)
+
+    def fetch(step):
+        slot = lax.rem(step, SLOTS)
+        return (pltpu.make_async_copy(k_ref.at[rows_of(step)], k_s.at[slot], in_sem.at[0, slot]),
+                pltpu.make_async_copy(v_ref.at[rows_of(step)], v_s.at[slot], in_sem.at[1, slot]))
+
+    def write(step):
+        slot = lax.rem(step, SLOTS)
+        return (pltpu.make_async_copy(k_s.at[slot], ko_ref.at[rows_of(step)], out_sem.at[0, slot]),
+                pltpu.make_async_copy(v_s.at[slot], vo_ref.at[rows_of(step)], out_sem.at[1, slot]))
+
+    loads = [pltpu.make_async_copy(src, dst, load_sem.at[i])
+             for i, (src, dst) in enumerate(((x_ref, x_s), (wq_ref, wq_s), (wk_ref, wk_s), (wv_ref, wv_s)))]
+    for copy in loads:
+        copy.start()
+    for step in range(AHEAD):
+        for copy in fetch(step):
+            copy.start()
+
+    lane = iota((4 * heads, LANES), 1)
+    head_of = lax.rem(iota((4 * heads, LANES), 0), heads)
+    far = jnp.full_like(lane, 16)
+    for edge in BUCKET_EDGES:
+        far = far + jnp.where(lane >= edge, 1, 0)
+    bucket = jnp.where(lane < 16, lane, far)
+    table = jnp.zeros((4 * heads, LANES), F32)
+    for b in range(32):
+        here = jnp.zeros((4 * heads, LANES), F32)
+        for h in range(heads):
+            here = jnp.where(head_of == h, bias_ref[h, b], here)
+        table = jnp.where(bucket == b, here, table)
+
+    for copy in loads:
+        copy.wait()
+
+    @pl.loop(0, rows_total // LANES)
+    def _(g):
+        rows = pl.ds(pl.multiple_of(g * LANES, LANES), LANES)
+        normed = rms_norm(x_s[rows, :].astype(F32), norm_ref[...])
+        q_s[rows, :] = dot(normed, wq_s[...]).astype(BF16)
+        kt_s[g] = dot(normed, wk_s[...]).astype(BF16).astype(F32).T
+        vt_s[g] = dot(normed, wv_s[...]).astype(BF16).astype(F32).T
 
     spread = jnp.where(iota((n * heads, n), 0) // heads == iota((n * heads, n), 1), 1.0, 0.0).astype(BF16)
+    gather = jnp.where(iota((n, n * heads), 1) // heads == iota((n, n * heads), 0), 1.0, 0.0).astype(BF16)
     own_head = iota((n * heads, flat), 1) // head_dim == lax.rem(iota((n * heads, flat), 0), heads)
-    q_rows = jnp.where(own_head, dot(spread, q_s[pl.ds(first, n), :]), 0.0).astype(BF16)
-
     lane_bf = iota((flat, LANES), 1).astype(F32).astype(BF16)
     quad_row = iota((4 * heads, LANES), 0)
-    table = table_s[...]
-
-    def update(cache_ref, new_cols, out_ref, b):
-        at_pos = lane_bf == pos_ref[first + b].astype(F32).astype(BF16)
-        col = jnp.broadcast_to(new_cols[:, b:b + 1], (flat, LANES)).astype(BF16)
-        updated = jnp.where(at_pos, col, cache_ref[b])
-        out_ref[b] = updated
-        return updated
-
-    for g in range(n // 4):
-        lhs = q_rows[4 * heads * g:4 * heads * (g + 1), :]
-        picked = None
-        distance = None
-        for half in range(2):
-            b = 4 * g + 2 * half
-            pair = jnp.concatenate([update(k_ref, k_new, ko_ref, b), update(k_ref, k_new, ko_ref, b + 1)], axis=1)
-            both = dot(lhs, pair)
-            for j in range(2):
-                mine = both[:, LANES * j:LANES * (j + 1)]
-                at = 2 * half + j
-                pos = pos_ref[first + 4 * g + at]
-                picked = mine if picked is None else jnp.where(quad_row >= heads * at, mine, picked)
-                distance = jnp.full((4 * heads, LANES), pos, jnp.int32) if distance is None else jnp.where(quad_row >= heads * at, pos, distance)
-        distance = distance - iota((4 * heads, LANES), 1)
-        bias = jnp.take_along_axis(table, jnp.maximum(distance, 0), axis=1)
-        score_s[4 * heads * g:4 * heads * (g + 1), :] = jnp.where(distance >= 0, picked + bias, NEG_FILL)
-
-    scores = score_s[...]
-    exps = jnp.exp(scores - jnp.max(scores, axis=1, keepdims=True))
-    probs = exps * pl.reciprocal(jnp.sum(exps, axis=1, keepdims=True))
-
-    for g in range(n // 4):
-        quad = probs[4 * heads * g:4 * heads * (g + 1), :]
-        picked = None
-        for half in range(2):
-            b = 4 * g + 2 * half
-            pair = jnp.concatenate([update(v_ref, v_new, vo_ref, b), update(v_ref, v_new, vo_ref, b + 1)], axis=1)
-            low = jnp.where(quad_row // heads == 2 * half, quad, 0.0)
-            high = jnp.where(quad_row // heads == 2 * half + 1, quad, 0.0)
-            lhs = jnp.concatenate([low, high], axis=1).astype(BF16)
-            both = dot_nt(lhs, pair)
-            picked = both if half == 0 else jnp.where(iota(both.shape, 0) >= 2 * heads, both, picked)
-        out_s[4 * heads * g:4 * heads * (g + 1), :] = picked
-    gather = jnp.where(iota((n, n * heads), 1) // heads == iota((n, n * heads), 0), 1.0, 0.0).astype(BF16)
-    mixed_ref[...] = dot(gather, jnp.where(own_head, out_s[...], 0.0).astype(BF16)).astype(BF16)
+    per = LANES // n
+
+    @pl.loop(0, steps)
+    def _(step):
+        ahead = step + AHEAD
+
+        @pl.when(ahead < steps)
+        def _():
+            @pl.when(ahead >= SLOTS)
+            def _():
+                for copy in write(ahead - SLOTS):
+                    copy.wait()
+            for copy in fetch(ahead):
+                copy.start()
+
+        first = pl.multiple_of(step * n, n)
+        slot = lax.rem(step, SLOTS)
+        group, part = step // per, lax.rem(step, per)
+        shift = lax.rem(LANES - part * n, LANES)
+        k_new = pltpu.roll(kt_s[group], shift, 1)
+        v_new = pltpu.roll(vt_s[group], shift, 1)
+        q_rows = jnp.where(own_head, dot(spread, q_s[pl.ds(first, n), :]), 0.0).astype(BF16)
+        in_k, in_v = fetch(step)
+
+        def update(cache, new_cols, b):
+            at_pos = lane_bf == pos_ref[first + b].astype(F32).astype(BF16)
+            col = jnp.broadcast_to(new_cols[:, b:b + 1], (flat, LANES)).astype(BF16)
+            updated = jnp.where(at_pos, col, cache[slot, b])
+            cache[slot, b] = updated
+            return updated
+
+        in_k.wait()
+        for g in range(n // 4):
+            lhs = q_rows[4 * heads * g:4 * heads * (g + 1), :]
+            picked = None
+            distance = None
+            for half in range(2):
+                b = 4 * g + 2 * half
+                pair = jnp.concatenate([update(k_s, k_new, b), update(k_s, k_new, b + 1)], axis=1)
+                both = dot(lhs, pair)
+                for j in range(2):
+                    mine = both[:, LANES * j:LANES * (j + 1)]
+                    at = 2 * half + j
+                    pos = pos_ref[first + 4 * g + at]
+                    picked = mine if picked is None else jnp.where(quad_row >= heads * at, mine, picked)
+                    distance = jnp.full((4 * heads, LANES), pos, jnp.int32) if distance is None else jnp.where(quad_row >= heads * at, pos, distance)
+            distance = distance - iota((4 * heads, LANES), 1)
+            bias = jnp.take_along_axis(table, jnp.maximum(distance, 0), axis=1)
+            score_s[4 * heads * g:4 * heads * (g + 1), :] = jnp.where(distance >= 0, picked + bias, NEG_FILL)
+        write(step)[0].start()
+
+        scores = score_s[...]
+        exps = jnp.exp(scores - jnp.max(scores, axis=1, keepdims=True))
+        probs = exps * pl.reciprocal(jnp.sum(exps, axis=1, keepdims=True))
+
+        in_v.wait()
+        for g in range(n // 4):
+            quad = probs[4 * heads * g:4 * heads * (g + 1), :]
+            picked = None
+            for half in range(2):
+                b = 4 * g + 2 * half
+                pair = jnp.concatenate([update(v_s, v_new, b), update(v_s, v_new, b + 1)], axis=1)
+                low = jnp.where(quad_row // heads == 2 * half, quad, 0.0)
+                high = jnp.where(quad_row // heads == 2 * half + 1, quad, 0.0)
+                lhs = jnp.concatenate([low, high], axis=1).astype(BF16)
+                both = dot_nt(lhs, pair)
+                picked = both if half == 0 else jnp.where(iota(both.shape, 0) >= 2 * heads, both, picked)
+            out_s[4 * heads * g:4 * heads * (g + 1), :] = picked
+        write(step)[1].start()
+        mixed_s[pl.ds(first, n), :] = dot(gather, jnp.where(own_head, out_s[...], 0.0).astype(BF16)).astype(BF16)
+
+    mixed_copy = pltpu.make_async_copy(mixed_s, mixed_ref, mixed_sem)
+    mixed_copy.start()
+    for step in range(steps - SLOTS, steps):
+        for copy in write(step):
+            copy.wait()
+    mixed_copy.wait()
 
 
 def self_attention(tok_pos, bias_t, x_in, w_q, w_k, w_v, norm_self, keys, values, heads):
@@ -128,28 +177,35 @@
     d_model = x_in.shape[1]
     n = STEP_ROWS
     smem = pl.BlockSpec(memory_space=pltpu.SMEM)
-    whole = lambda *shape: pl.BlockSpec(shape, lambda i: (0,) * len(shape))
-    cache = pl.BlockSpec((n, flat, t_len), lambda i: (i, 0, 0))
+    anywhere = pl.BlockSpec(memory_space=pl.ANY)
     cache_shape = jax.ShapeDtypeStruct(keys.shape, BF16)
     return pl.pallas_call(
         functools.partial(self_kernel, heads, flat // heads),
-        grid=(rows // n,),
-        in_specs=[smem, smem, whole(rows, d_model), whole(d_model, flat), whole(d_model, flat), whole(d_model, flat),
-                  whole(1, d_model), cache, cache],
-        out_specs=[pl.BlockSpec((n, flat), lambda i: (i, 0)), cache, cache],
+        in_specs=[smem, smem] + [anywhere] * 4 + [pl.BlockSpec(memory_space=pltpu.VMEM)] + [anywhere] * 2,
+        out_specs=[anywhere] * 3,
         out_shape=[jax.ShapeDtypeStruct((rows, flat), BF16), cache_shape, cache_shape],
         scratch_shapes=[
+            pltpu.VMEM((rows, d_model), BF16),
+            pltpu.VMEM((d_model, flat), BF16),
+            pltpu.VMEM((d_model, flat), BF16),
+            pltpu.VMEM((d_model, flat), BF16),
+            pltpu.VMEM((SLOTS, n, flat, t_len), BF16),
+            pltpu.VMEM((SLOTS, n, flat, t_len), BF16),
+            pltpu.VMEM((rows, flat), BF16),
             pltpu.VMEM((rows, flat), BF16),
             pltpu.VMEM((rows // LANES, flat, LANES), F32),
             pltpu.VMEM((rows // LANES, flat, LANES), F32),
-            pltpu.VMEM((4 * heads, LANES), F32),
             pltpu.VMEM((n * heads, LANES), F32),
             pltpu.VMEM((n * heads, flat), F32),
+            pltpu.SemaphoreType.DMA((4,)),
+            pltpu.SemaphoreType.DMA((2, SLOTS)),
+            pltpu.SemaphoreType.DMA((2, SLOTS)),
+            pltpu.SemaphoreType.DMA,
         ],
-        compiler_params=pltpu.CompilerParams(dimension_semantics=('arbitrary',), vmem_limit_bytes=63 * 1024 * 1024),
+        compiler_params=pltpu.CompilerParams(vmem_limit_bytes=VMEM_BYTES),
         cost_estimate=pl.CostEstimate(flops=4 * rows * flat * t_len * 16 + 6 * rows * d_model * flat, bytes_accessed=8 * rows * flat * t_len, transcendentals=rows * heads * t_len),
         name='self_attention',
-    )(tok_pos, bias_t, x_in, w_q, w_k, w_v, norm_self.reshape(1, d_model), keys, values)
+    )(tok_pos, bias_t, x_in, w_q, w_k, w_v, norm_self, keys, values)
 
 
 CHUNK = 128
@@ -267,7 +323,7 @@
         normed = rms_norm(res_s[CHUNK * c:CHUNK * (c + 1), :], norm_c_ref[...])
         qt_s[...] = dot(normed, cq_s[...]).astype(BF16).astype(F32).T
 
-    def cross_attend(c):
+    def cross_score(c):
         slot = c % n_cross_slots
         for copy in cross_load(c):
             copy.wait()
@@ -282,6 +338,9 @@
                 d = slice(head_dim * h, head_dim * (h + 1))
                 score_s[h, at, :] = jnp.sum(k_s[slot, at, d, :].astype(F32) * qt_s[d, :][None], axis=1)
 
+    def cross_mix(c):
+        slot = c % n_cross_slots
+        step = 8
         valid = mask_s[:, CHUNK * c:CHUNK * (c + 1)] != 0
         for h in range(heads):
             scores = jnp.where(valid, score_s[h], NEG_FILL)
@@ -349,37 +408,41 @@
         copy.start()
         return copy
 
-    for c in range(chunks):
+    gather_relay(0, mix_s, 0)
+    cross_query(0)
+    for c in range(1, chunks):
         gather_relay(0, mix_s, c)
-        if c == 0:
-            cross_query(0)
     weight_send(1, co_ref, cox_ref, co_s)
-    cross_attend(0)
+    cross_score(0)
+    cross_mix(0)
     cross_query(1)
+    cross_score(1)
+    cross_mix(1)
+    cross_query(2)
+    cross_score(2)
     gather_relay(1, cmix_s, 0)
-    cross_attend(1)
+    cross_mix(2)
     mlp(0)
-    cross_query(2)
     gather_relay(1, cmix_s, 1)
+    cross_query(3)
+    cross_score(3)
     chip_sum(0)
-    cross_attend(2)
+    gather_relay(1, cmix_s, 2)
+    cross_mix(3)
     mlp(1)
-    cross_query(3)
-    gather_relay(1, cmix_s, 2)
+    mlp(2)
     chip_sum(1)
-    cross_attend(3)
-    mlp(2)
+    chip_sum(2)
     full_sum(0)
     gather_relay(1, cmix_s, 3)
-    chip_sum(2)
     mlp(3)
+    stores = [store(0)]
     full_sum(1)
-    stores = [store(0)]
     chip_sum(3)
+    stores.append(store(1))
     full_sum(2)
-    stores.append(store(1))
+    stores.append(store(2))
     full_sum(3)
-    stores.append(store(2))
     stores.append(store(3))
     for copy in stores:
         copy.wait()
@@ -429,10 +492,10 @@
             dma((3, chunks)), dma((3, chunks)),
             dma((16,)), dma((2, slots)), dma((chunks,)),
         ],
-        compiler_params=pltpu.CompilerParams(collective_id=0, has_side_effects=True, vmem_limit_bytes=63 * 1024 * 1024),
+        compiler_params=pltpu.CompilerParams(collective_id=0, has_side_effects=True, vmem_limit_bytes=VMEM_BYTES),
         cost_estimate=pl.CostEstimate(flops=2 * rows * d_model * (8 * flat + flat + 3 * d_ff), bytes_accessed=50_000_000, transcendentals=rows * d_ff),
         name='rest_of_layer',
-    )(x_in, mixed, w_o, w_o_over, cross_o, cross_o_over, cross_q, gate_t, up_t, w_down, norm_cross.reshape(1, d_model), norm_mlp.reshape(1, d_model), mask_t, cross_k, cross_v)
+    )(x_in, mixed, w_o, w_o_over, cross_o, cross_o_over, cross_q, gate_t, up_t, w_down, norm_cross, norm_mlp, mask_t, cross_k, cross_v)
 
 
 def solution(mesh):

time: 121 us -> 104 us (0.86)
  Pallas kernels: 109 us -> 96.7 us
  local copies, waits for them, and re-layouts: 7.37 us -> 2.65 us
    pallas_call x1, Pallas kernels: 59.6 us -> 48.6 us  [self_attention(): pl.pallas_call(functools.partial(self_kernel, heads, flat // heads), in_s...]
    reshape x3 -> x0, local copies, waits for them, and re-layouts: 3.85 us -> none  [the longest x1 1.29 us: rest_of_layer(): norm_mlp.reshape(1, d_model)]
    pallas_call x1, Pallas kernels: 49.7 us -> 48.1 us  [rest_of_layer(): pl.pallas_call(functools.partial(rest_kernel, heads, slots), in_specs=[an...]
    unnamed x3 -> x1, local copies, waits for them, and re-layouts: 3.52 us -> 2.65 us
  transfers between devices with their start and end apart: 2 -> 2, of which waited for: 0 -> 0; matrix products, arithmetic and copies ran while one was open for 3% -> 0% of each run, Pallas kernels for 49% -> 47%
where the time goes in v3:
time: 104 us; the launch traced here: 103 us
  Pallas kernels  96.7 us (93%)
  starting transfers between devices  3.4 us (3%)
  local copies, waits for them, and re-layouts  2.65 us (3%)
    pallas_call x1, Pallas kernels, self_attention(): pl.pallas_call(functools.partial(self_kernel, heads, flat // heads), in_s...  48.6 us
    pallas_call x1, Pallas kernels, rest_of_layer(): pl.pallas_call(functools.partial(rest_kernel, heads, slots), in_specs=[an...  48.1 us
    ppermute x1, starting transfers between devices, local_layer(): w_o_over = lax.ppermute(w_o, 'tp', swap)  3.36 us
    unnamed x1, local copies, waits for them, and re-layouts  2.65 us
  transfers between devices with their start and end apart: 2, of which 0 were waited for; matrix products, arithmetic and copies ran while one was open for 0% of the time, Pallas kernels for 47%

profile of v3, /device:TPU:0, one launch (start us, length us, event | category | flops | bytes accessed | tf_op | source)
XLA Modules:
  0.0 103.4 jit_solution(16706016881910389271)
XLA Ops:
  0.6 3.4 %collective-permute-start = (bf16[256,1536]{1,0:T(8,128)(2,1)}, bf16[256,1536]{1,0:T(8,128)(2,1)}, u32[]{:S(2)}, u32[]{:S(2)}) collective-permute-start(bf16[256,1536]{1,0:T(8,128)(2,1)} %wo_ref.1), channel_id=1, source_target_pairs={{0,2},{1,3},{2,0},{3,1},{4,6},{5,7},{6,4},{7,5}} | collective-permute-start | bytes 2359304 | tf_op jit(solution)/shard_map/ppermute | solution.py:509
  4.0 0.0 collective-permute-start.1
  4.0 48.6 %self_attention.1 = (bf16[512,256]{1,0:T(8,128)(2,1)}, bf16[512,256,128]{2,1,0:T(8,128)(2,1)}, bf16[512,256,128]{2,1,0:T(8,128)(2,1)}) custom-call(s32[512]{0:T(512)} %pos_ref.1, f32[4,32]{1,0:T(4,128)} %bitcast.29, bf16[512,1536]{1,0:T(8,128)(2,1)} %x_ref.3, bf16[1536,256]{1,0:T(8,128)(2,1)} %wq_ref.1, bf16[1536,256]{1,0:T(8,128)(2,1)} %wk_ref.1, ...), custom_call_target="tpu_custom_call" | custom-call | flops 2281701376 | bytes 134217728 | tf_op jit(solution)/shard_map/self_attention/pallas_call | solution.py:182
  52.6 0.0 collective-permute-done.wox_ref
  52.6 0.0 collective-permute-done.1.cox_ref
  52.7 48.1 %rest_of_layer.1 = bf16[512,1536]{1,0:T(8,128)(2,1)} custom-call(bf16[512,1536]{1,0:T(8,128)(2,1)} %x_ref.3, bf16[512,256]{1,0:T(8,128)(2,1)} %get-tuple-element.6.mixed_ref, bf16[256,1536]{1,0:T(8,128)(2,1)} %wo_ref.1, bf16[256,1536]{1,0:T(8,128)(2,1)} %collective-permute-done.wox_ref, bf16[256,1536]{1,0:T(8,128)(2,1)} %co_ref.1, ...), custom_call_target="tpu_custom_call" | custom-call | flops 8153726976 | bytes 50000000 | tf_op jit(solution)/shard_map/rest_of_layer/pallas_call | solution.py:463
  100.7 2.7 %copy.24 = bf16[512,1536]{1,0:T(8,128)(2,1)} copy(bf16[512,1536]{1,0:T(8,128)(2,1)} %rest_of_layer.1) | data formatting | bytes 3145728
Async XLA Ops:
  0.6 52.0 %collective-permute-start = (bf16[256,1536]{1,0:T(8,128)(2,1)}, bf16[256,1536]{1,0:T(8,128)(2,1)}, u32[]{:S(2)}, u32[]{:S(2)}) collective-permute-start(bf16[256,1536]{1,0:T(8,128)(2,1)} %wo_ref.1), channel_id=1, source_target_pairs={{0,2},{1,3},{2,0},{3,1},{4,6},{5,7},{6,4},{7,5}} | collective-permute-start | bytes 2359304 | tf_op jit(solution)/shard_map/ppermute | solution.py:509
  4.0 48.6 %collective-permute-start.1 = (bf16[256,1536]{1,0:T(8,128)(2,1)}, bf16[256,1536]{1,0:T(8,128)(2,1)}, u32[]{:S(2)}, u32[]{:S(2)}) collective-permute-start(bf16[256,1536]{1,0:T(8,128)(2,1)} %co_ref.1), channel_id=1, source_target_pairs={{0,2},{1,3},{2,0},{3,1},{4,6},{5,7},{6,4},{7,5}} | collective-permute-start | bytes 2359304 | tf_op jit(solution)/shard_map/ppermute | solution.py:510

commit v4 on v3

--- a/solution.py
+++ b/solution.py
@@ -255,17 +255,7 @@
         return (pltpu.make_async_copy(ck_ref.at[:, :, cols], k_s.at[slot], cross_sem.at[0, slot]),
                 pltpu.make_async_copy(cv_ref.at[:, :, cols], v_s.at[slot], cross_sem.at[1, slot]))
 
-    own_mixed = load(mixed_ref, mix_s.at[me])
-    x_load = load(x_ref, x_s)
-    own_wo = (load(wo_ref, shard(wo_s, me)), load(wox_ref, shard(wo_s, over)))
-    q_load = load(cq_ref, cq_s)
-    mask_load = load(mask_ref, mask_s)
-    first_cross = cross_load(0)
-    for copy in first_cross:
-        copy.start()
-    own_co = (load(co_ref, shard(co_s, me)), load(cox_ref, shard(co_s, over)))
-    mlp_loads = (load(gate_ref, gate_s), load(up_ref, up_s), load(down_ref, down_s))
-    for c in range(1, n_cross_slots):
+    def cross_start(c):
         for copy in cross_load(c):
             copy.start()
 
@@ -302,7 +292,13 @@
 
     for c in range(chunks):
         gather_send(0, mixed_ref.at[pl.ds(CHUNK * c, CHUNK), :], mix_s, c)
+    own_mixed = load(mixed_ref, mix_s.at[me])
+    own_wo = (load(wo_ref, shard(wo_s, me)), load(wox_ref, shard(wo_s, over)))
+    x_load = load(x_ref, x_s)
+    q_load = load(cq_ref, cq_s)
+    mask_load = load(mask_ref, mask_s)
     weight_send(0, wo_ref, wox_ref, wo_s)
+    cross_start(0)
 
     def project_heads(buf, weight, c, add_to):
         lhs = jnp.concatenate([buf[i, CHUNK * c:CHUNK * (c + 1), :] for i in range(4)], axis=1)
@@ -361,9 +357,6 @@
         acc = lax.fori_loop(0, src_len // step, mix, (zero,) * heads)
         cmix_s[me, CHUNK * c:CHUNK * (c + 1), :] = jnp.concatenate(acc, axis=0).T.astype(BF16)
         gather_send(1, block(cmix_s, me, c), cmix_s, c)
-        if c + n_cross_slots < chunks:
-            for copy in cross_load(c + n_cross_slots):
-                copy.start()
 
     def mlp(c):
         if c == 0:
@@ -412,16 +405,21 @@
     cross_query(0)
     for c in range(1, chunks):
         gather_relay(0, mix_s, c)
-    weight_send(1, co_ref, cox_ref, co_s)
+    cross_start(1)
     cross_score(0)
     cross_mix(0)
+    weight_send(1, co_ref, cox_ref, co_s)
+    own_co = (load(co_ref, shard(co_s, me)), load(cox_ref, shard(co_s, over)))
+    cross_start(2)
     cross_query(1)
     cross_score(1)
     cross_mix(1)
+    mlp_loads = (load(gate_ref, gate_s), load(up_ref, up_s), load(down_ref, down_s))
     cross_query(2)
     cross_score(2)
     gather_relay(1, cmix_s, 0)
     cross_mix(2)
+    cross_start(3)
     mlp(0)
     gather_relay(1, cmix_s, 1)
     cross_query(3)

time: 104 us -> 104 us (level)
  no operation moved by 1% of the time
where the time goes in v4:
time: 104 us; the launch traced here: 103 us
  Pallas kernels  96.7 us (93%)
  starting transfers between devices  3.4 us (3%)
  local copies, waits for them, and re-layouts  2.65 us (3%)
    pallas_call x1, Pallas kernels, self_attention(): pl.pallas_call(functools.partial(self_kernel, heads, flat // heads), in_s...  48.6 us
    pallas_call x1, Pallas kernels, rest_of_layer(): pl.pallas_call(functools.partial(rest_kernel, heads, slots), in_specs=[an...  48.1 us
    ppermute x1, starting transfers between devices, local_layer(): w_o_over = lax.ppermute(w_o, 'tp', swap)  3.36 us
    unnamed x1, local copies, waits for them, and re-layouts  2.65 us
  transfers between devices with their start and end apart: 2, of which 0 were waited for; matrix products, arithmetic and copies ran while one was open for 0% of the time, Pallas kernels for 47%

profile of v4, /device:TPU:0, one launch (start us, length us, event | category | flops | bytes accessed | tf_op | source)
XLA Modules:
  0.0 103.4 jit_solution(1560372550398105881)
XLA Ops:
  0.6 3.4 %collective-permute-start = (bf16[256,1536]{1,0:T(8,128)(2,1)}, bf16[256,1536]{1,0:T(8,128)(2,1)}, u32[]{:S(2)}, u32[]{:S(2)}) collective-permute-start(bf16[256,1536]{1,0:T(8,128)(2,1)} %wo_ref.1), channel_id=1, source_target_pairs={{0,2},{1,3},{2,0},{3,1},{4,6},{5,7},{6,4},{7,5}} | collective-permute-start | bytes 2359304 | tf_op jit(solution)/shard_map/ppermute | solution.py:507
  4.0 0.0 collective-permute-start.1
  4.0 48.6 %self_attention.1 = (bf16[512,256]{1,0:T(8,128)(2,1)}, bf16[512,256,128]{2,1,0:T(8,128)(2,1)}, bf16[512,256,128]{2,1,0:T(8,128)(2,1)}) custom-call(s32[512]{0:T(512)} %pos_ref.1, f32[4,32]{1,0:T(4,128)} %bitcast.29, bf16[512,1536]{1,0:T(8,128)(2,1)} %x_ref.3, bf16[1536,256]{1,0:T(8,128)(2,1)} %wq_ref.1, bf16[1536,256]{1,0:T(8,128)(2,1)} %wk_ref.1, ...), custom_call_target="tpu_custom_call" | custom-call | flops 2281701376 | bytes 134217728 | tf_op jit(solution)/shard_map/self_attention/pallas_call | solution.py:182
  52.6 0.0 collective-permute-done.wox_ref
  52.6 0.0 collective-permute-done.1.cox_ref
  52.7 48.1 %rest_of_layer.1 = bf16[512,1536]{1,0:T(8,128)(2,1)} custom-call(bf16[512,1536]{1,0:T(8,128)(2,1)} %x_ref.3, bf16[512,256]{1,0:T(8,128)(2,1)} %get-tuple-element.6.mixed_ref, bf16[256,1536]{1,0:T(8,128)(2,1)} %wo_ref.1, bf16[256,1536]{1,0:T(8,128)(2,1)} %collective-permute-done.wox_ref, bf16[256,1536]{1,0:T(8,128)(2,1)} %co_ref.1, ...), custom_call_target="tpu_custom_call" | custom-call | flops 8153726976 | bytes 50000000 | tf_op jit(solution)/shard_map/rest_of_layer/pallas_call | solution.py:461
  100.8 2.7 %copy.24 = bf16[512,1536]{1,0:T(8,128)(2,1)} copy(bf16[512,1536]{1,0:T(8,128)(2,1)} %rest_of_layer.1) | data formatting | bytes 3145728
Async XLA Ops:
  0.6 52.0 %collective-permute-start = (bf16[256,1536]{1,0:T(8,128)(2,1)}, bf16[256,1536]{1,0:T(8,128)(2,1)}, u32[]{:S(2)}, u32[]{:S(2)}) collective-permute-start(bf16[256,1536]{1,0:T(8,128)(2,1)} %wo_ref.1), channel_id=1, source_target_pairs={{0,2},{1,3},{2,0},{3,1},{4,6},{5,7},{6,4},{7,5}} | collective-permute-start | bytes 2359304 | tf_op jit(solution)/shard_map/ppermute | solution.py:507
  4.0 48.6 %collective-permute-start.1 = (bf16[256,1536]{1,0:T(8,128)(2,1)}, bf16[256,1536]{1,0:T(8,128)(2,1)}, u32[]{:S(2)}, u32[]{:S(2)}) collective-permute-start(bf16[256,1536]{1,0:T(8,128)(2,1)} %co_ref.1), channel_id=1, source_target_pairs={{0,2},{1,3},{2,0},{3,1},{4,6},{5,7},{6,4},{7,5}} | collective-permute-start | bytes 2359304 | tf_op jit(solution)/shard_map/ppermute | solution.py:508

commit v5 on v4

--- a/solution.py
+++ b/solution.py
@@ -9,9 +9,9 @@
 
 BUCKET_EDGES = tuple(int(math.ceil(16.0 * 8.0 ** (bucket_step / 16.0))) for bucket_step in range(1, 16))
 NEG_FILL = -1e30
-STEP_ROWS = 32
-SLOTS = 8
-AHEAD = 4
+STEP_ROWS = 16
+SLOTS = 16
+AHEAD = 8
 VMEM_BYTES = 67043328
 LANES = 128
 F32 = jnp.float32
@@ -215,7 +215,7 @@
 def rest_kernel(heads, n_cross_slots,
                 x_ref, mixed_ref, wo_ref, wox_ref, co_ref, cox_ref, cq_ref, gate_ref, up_ref, down_ref, norm_c_ref, norm_m_ref,
                 mask_ref, ck_ref, cv_ref, out_ref,
-                x_s, res_s, mix_s, cmix_s, wo_s, co_s, cq_s, gate_s, up_s, down_s, k_s, v_s, mask_s,
+                x_s, res_s, mix_s, cmix_s, wo_s, co_s, cq_s, gate_s, up_s, gate_t, up_t, down_s, k_s, v_s, mask_s,
                 qt_s, score_s, hid_s, part_s, near_s, chip_s, far_s, done_s,
                 ag_send, ag_recv, w_send, w_recv, sum_send, sum_recv, load_sem, cross_sem, out_sem):
     me = lax.axis_index('tp')
@@ -298,7 +298,15 @@
     q_load = load(cq_ref, cq_s)
     mask_load = load(mask_ref, mask_s)
     weight_send(0, wo_ref, wox_ref, wo_s)
+    gate_load = load(gate_ref, gate_s)
+    up_load = load(up_ref, up_s)
     cross_start(0)
+
+    def turn(wide, tall):
+        @pl.loop(0, d_model // CHUNK)
+        def _(i):
+            at = pl.ds(pl.multiple_of(i * CHUNK, CHUNK), CHUNK)
+            tall[at, :] = wide[:, at].T
 
     def project_heads(buf, weight, c, add_to):
         lhs = jnp.concatenate([buf[i, CHUNK * c:CHUNK * (c + 1), :] for i in range(4)], axis=1)
@@ -366,13 +374,12 @@
         gather_wait(1, cmix_s, c)
         project_heads(cmix_s, co_s, c, res_s)
         if c == 0:
-            for copy in mlp_loads:
-                copy.wait()
+            down_load.wait()
         normed = rms_norm(res_s[CHUNK * c:CHUNK * (c + 1), :], norm_m_ref[...])
         for n in range(0, d_ff, 256):
             end = min(d_ff, n + 256)
-            gate = dot_nt(normed, gate_s[n:end, :])
-            up = dot_nt(normed, up_s[n:end, :])
+            gate = dot(normed, gate_t[:, n:end])
+            up = dot(normed, up_t[:, n:end])
             hid_s[:, n:end] = (jax.nn.gelu(gate, approximate=True) * up).astype(BF16)
         hidden = hid_s[...]
         for n in range(0, d_model, 512):
@@ -401,7 +408,11 @@
         copy.start()
         return copy
 
+    gate_load.wait()
+    turn(gate_s, gate_t)
     gather_relay(0, mix_s, 0)
+    up_load.wait()
+    turn(up_s, up_t)
     cross_query(0)
     for c in range(1, chunks):
         gather_relay(0, mix_s, c)
@@ -414,25 +425,25 @@
     cross_query(1)
     cross_score(1)
     cross_mix(1)
-    mlp_loads = (load(gate_ref, gate_s), load(up_ref, up_s), load(down_ref, down_s))
+    down_load = load(down_ref, down_s)
+    cross_start(3)
     cross_query(2)
+    gather_relay(1, cmix_s, 0)
     cross_score(2)
-    gather_relay(1, cmix_s, 0)
-    cross_mix(2)
-    cross_start(3)
     mlp(0)
     gather_relay(1, cmix_s, 1)
+    cross_mix(2)
+    chip_sum(0)
     cross_query(3)
     cross_score(3)
-    chip_sum(0)
-    gather_relay(1, cmix_s, 2)
     cross_mix(3)
     mlp(1)
+    gather_relay(1, cmix_s, 2)
+    chip_sum(1)
     mlp(2)
-    chip_sum(1)
+    gather_relay(1, cmix_s, 3)
+    full_sum(0)
     chip_sum(2)
-    full_sum(0)
-    gather_relay(1, cmix_s, 3)
     mlp(3)
     stores = [store(0)]
     full_sum(1)
@@ -454,7 +465,7 @@
     d_ff = gate_t.shape[0]
     src_len = cross_k.shape[0]
     chunks = rows // CHUNK
-    slots = 3
+    slots = 2
     anywhere = pl.BlockSpec(memory_space=pl.ANY)
     vmem = pl.BlockSpec(memory_space=pltpu.VMEM)
     dma = pltpu.SemaphoreType.DMA
@@ -473,6 +484,8 @@
             pltpu.VMEM((d_model, flat), BF16),
             pltpu.VMEM((d_ff, d_model), BF16),
             pltpu.VMEM((d_ff, d_model), BF16),
+            pltpu.VMEM((d_model, d_ff), BF16),
+            pltpu.VMEM((d_model, d_ff), BF16),
             pltpu.VMEM((d_ff, d_model), BF16),
             pltpu.VMEM((slots, src_len, flat, CHUNK), BF16),
             pltpu.VMEM((slots, src_len, flat, CHUNK), BF16),

time: 104 us -> 113 us (1.087)
  Pallas kernels: 96.7 us -> 106 us
    pallas_call x1, Pallas kernels: 48.6 us -> 58.8 us  [self_attention(): pl.pallas_call(functools.partial(self_kernel, heads, flat // heads), in_s...]
  transfers between devices with their start and end apart: 2 -> 2, of which waited for: 0 -> 0; matrix products, arithmetic and copies ran while one was open for 0% -> 0% of each run, Pallas kernels for 47% -> 52%
where the time goes in v5:
time: 113 us
  Pallas kernels  106 us (94%)
  starting transfers between devices  3.4 us (3%)
  local copies, waits for them, and re-layouts  2.65 us (2%)
    pallas_call x1, Pallas kernels, self_attention(): pl.pallas_call(functools.partial(self_kernel, heads, flat // heads), in_s...  58.8 us
    pallas_call x1, Pallas kernels, rest_of_layer(): pl.pallas_call(functools.partial(rest_kernel, heads, slots), in_specs=[an...  47.2 us
    ppermute x1, starting transfers between devices, local_layer(): w_o_over = lax.ppermute(w_o, 'tp', swap)  3.36 us
    unnamed x1, local copies, waits for them, and re-layouts  2.65 us
  transfers between devices with their start and end apart: 2, of which 0 were waited for; matrix products, arithmetic and copies ran while one was open for 0% of the time, Pallas kernels for 52%

profile of v5, /device:TPU:0, one launch (start us, length us, event | category | flops | bytes accessed | tf_op | source)
XLA Modules:
  0.0 112.7 jit_solution(10949847296550924524)
XLA Ops:
  0.6 3.4 %collective-permute-start = (bf16[256,1536]{1,0:T(8,128)(2,1)}, bf16[256,1536]{1,0:T(8,128)(2,1)}, u32[]{:S(2)}, u32[]{:S(2)}) collective-permute-start(bf16[256,1536]{1,0:T(8,128)(2,1)} %wo_ref.1), channel_id=1, source_target_pairs={{0,2},{1,3},{2,0},{3,1},{4,6},{5,7},{6,4},{7,5}} | collective-permute-start | bytes 2359304 | tf_op jit(solution)/shard_map/ppermute | solution.py:520
  4.0 0.0 collective-permute-start.1
  4.0 58.8 %self_attention.1 = (bf16[512,256]{1,0:T(8,128)(2,1)}, bf16[512,256,128]{2,1,0:T(8,128)(2,1)}, bf16[512,256,128]{2,1,0:T(8,128)(2,1)}) custom-call(s32[512]{0:T(512)} %pos_ref.1, f32[4,32]{1,0:T(4,128)} %bitcast.29, bf16[512,1536]{1,0:T(8,128)(2,1)} %x_ref.3, bf16[1536,256]{1,0:T(8,128)(2,1)} %wq_ref.1, bf16[1536,256]{1,0:T(8,128)(2,1)} %wk_ref.1, ...), custom_call_target="tpu_custom_call" | custom-call | flops 2281701376 | bytes 134217728 | tf_op jit(solution)/shard_map/self_attention/pallas_call | solution.py:182
  62.8 0.0 collective-permute-done.wox_ref
  62.9 0.0 collective-permute-done.1.cox_ref
  62.9 47.2 %rest_of_layer.1 = bf16[512,1536]{1,0:T(8,128)(2,1)} custom-call(bf16[512,1536]{1,0:T(8,128)(2,1)} %x_ref.3, bf16[512,256]{1,0:T(8,128)(2,1)} %get-tuple-element.6.mixed_ref, bf16[256,1536]{1,0:T(8,128)(2,1)} %wo_ref.1, bf16[256,1536]{1,0:T(8,128)(2,1)} %collective-permute-done.wox_ref, bf16[256,1536]{1,0:T(8,128)(2,1)} %co_ref.1, ...), custom_call_target="tpu_custom_call" | custom-call | flops 8153726976 | bytes 50000000 | tf_op jit(solution)/shard_map/rest_of_layer/pallas_call | solution.py:472
  110.1 2.7 %copy.24 = bf16[512,1536]{1,0:T(8,128)(2,1)} copy(bf16[512,1536]{1,0:T(8,128)(2,1)} %rest_of_layer.1) | data formatting | bytes 3145728
Async XLA Ops:
  0.6 62.2 %collective-permute-start = (bf16[256,1536]{1,0:T(8,128)(2,1)}, bf16[256,1536]{1,0:T(8,128)(2,1)}, u32[]{:S(2)}, u32[]{:S(2)}) collective-permute-start(bf16[256,1536]{1,0:T(8,128)(2,1)} %wo_ref.1), channel_id=1, source_target_pairs={{0,2},{1,3},{2,0},{3,1},{4,6},{5,7},{6,4},{7,5}} | collective-permute-start | bytes 2359304 | tf_op jit(solution)/shard_map/ppermute | solution.py:520
  4.0 58.9 %collective-permute-start.1 = (bf16[256,1536]{1,0:T(8,128)(2,1)}, bf16[256,1536]{1,0:T(8,128)(2,1)}, u32[]{:S(2)}, u32[]{:S(2)}) collective-permute-start(bf16[256,1536]{1,0:T(8,128)(2,1)} %co_ref.1), channel_id=1, source_target_pairs={{0,2},{1,3},{2,0},{3,1},{4,6},{5,7},{6,4},{7,5}} | collective-permute-start | bytes 2359304 | tf_op jit(solution)/shard_map/ppermute | solution.py:521

commit v6 on v5

--- a/solution.py
+++ b/solution.py
@@ -9,9 +9,9 @@
 
 BUCKET_EDGES = tuple(int(math.ceil(16.0 * 8.0 ** (bucket_step / 16.0))) for bucket_step in range(1, 16))
 NEG_FILL = -1e30
-STEP_ROWS = 16
-SLOTS = 16
-AHEAD = 8
+STEP_ROWS = 32
+SLOTS = 8
+AHEAD = 4
 VMEM_BYTES = 67043328
 LANES = 128
 F32 = jnp.float32
@@ -112,14 +112,14 @@
         slot = lax.rem(step, SLOTS)
         group, part = step // per, lax.rem(step, per)
         shift = lax.rem(LANES - part * n, LANES)
-        k_new = pltpu.roll(kt_s[group], shift, 1)
-        v_new = pltpu.roll(vt_s[group], shift, 1)
+        k_new = pltpu.roll(kt_s[group], shift, 1).astype(BF16)
+        v_new = pltpu.roll(vt_s[group], shift, 1).astype(BF16)
         q_rows = jnp.where(own_head, dot(spread, q_s[pl.ds(first, n), :]), 0.0).astype(BF16)
         in_k, in_v = fetch(step)
 
         def update(cache, new_cols, b):
             at_pos = lane_bf == pos_ref[first + b].astype(F32).astype(BF16)
-            col = jnp.broadcast_to(new_cols[:, b:b + 1], (flat, LANES)).astype(BF16)
+            col = jnp.broadcast_to(new_cols[:, b:b + 1], (flat, LANES))
             updated = jnp.where(at_pos, col, cache[slot, b])
             cache[slot, b] = updated
             return updated
@@ -213,7 +213,7 @@
 
 
 def rest_kernel(heads, n_cross_slots,
-                x_ref, mixed_ref, wo_ref, wox_ref, co_ref, cox_ref, cq_ref, gate_ref, up_ref, down_ref, norm_c_ref, norm_m_ref,
+                x_ref, mixed_ref, wo_ref, wox_ref, wom_ref, co_ref, cox_ref, com_ref, cq_ref, gate_ref, up_ref, down_ref, norm_c_ref, norm_m_ref,
                 mask_ref, ck_ref, cv_ref, out_ref,
                 x_s, res_s, mix_s, cmix_s, wo_s, co_s, cq_s, gate_s, up_s, gate_t, up_t, down_s, k_s, v_s, mask_s,
                 qt_s, score_s, hid_s, part_s, near_s, chip_s, far_s, done_s,
@@ -282,22 +282,20 @@
         remote(block(buf, mate, c), block(buf, mate, c), ag_send.at[stage, 1, c], ag_recv.at[stage, 1, c], mate).wait_recv()
         remote(block(buf, cater, c), block(buf, cater, c), ag_send.at[stage, 2, c], ag_recv.at[stage, 2, c], mate).wait_recv()
 
-    def weight_send(which, ref, ref_x, buf):
-        send(remote(ref, shard(buf, me), w_send.at[which, 0], w_recv.at[which, 0], mate))
-        send(remote(ref_x, shard(buf, over), w_send.at[which, 1], w_recv.at[which, 1], mate))
+    def weight_send(which, ref_x, buf):
+        send(remote(ref_x, shard(buf, over), w_send.at[which], w_recv.at[which], mate))
 
     def weight_wait(which, buf):
-        remote(shard(buf, mate), shard(buf, mate), w_send.at[which, 0], w_recv.at[which, 0], mate).wait_recv()
-        remote(shard(buf, cater), shard(buf, cater), w_send.at[which, 1], w_recv.at[which, 1], mate).wait_recv()
+        remote(shard(buf, cater), shard(buf, cater), w_send.at[which], w_recv.at[which], mate).wait_recv()
 
     for c in range(chunks):
         gather_send(0, mixed_ref.at[pl.ds(CHUNK * c, CHUNK), :], mix_s, c)
     own_mixed = load(mixed_ref, mix_s.at[me])
-    own_wo = (load(wo_ref, shard(wo_s, me)), load(wox_ref, shard(wo_s, over)))
+    own_wo = (load(wo_ref, shard(wo_s, me)), load(wox_ref, shard(wo_s, over)), load(wom_ref, shard(wo_s, mate)))
     x_load = load(x_ref, x_s)
     q_load = load(cq_ref, cq_s)
     mask_load = load(mask_ref, mask_s)
-    weight_send(0, wo_ref, wox_ref, wo_s)
+    weight_send(0, wox_ref, wo_s)
     gate_load = load(gate_ref, gate_s)
     up_load = load(up_ref, up_s)
     cross_start(0)
@@ -416,11 +414,11 @@
     cross_query(0)
     for c in range(1, chunks):
         gather_relay(0, mix_s, c)
+    weight_send(1, cox_ref, co_s)
     cross_start(1)
     cross_score(0)
     cross_mix(0)
-    weight_send(1, co_ref, cox_ref, co_s)
-    own_co = (load(co_ref, shard(co_s, me)), load(cox_ref, shard(co_s, over)))
+    own_co = (load(co_ref, shard(co_s, me)), load(cox_ref, shard(co_s, over)), load(com_ref, shard(co_s, mate)))
     cross_start(2)
     cross_query(1)
     cross_score(1)
@@ -459,7 +457,7 @@
         copy.wait_send()
 
 
-def rest_of_layer(x_in, mixed, w_o, w_o_over, cross_o, cross_o_over, cross_q, gate_t, up_t, w_down, norm_cross, norm_mlp, mask_t, cross_k, cross_v, heads):
+def rest_of_layer(x_in, mixed, w_o, w_o_over, w_o_mate, cross_o, cross_o_over, cross_o_mate, cross_q, gate_t, up_t, w_down, norm_cross, norm_mlp, mask_t, cross_k, cross_v, heads):
     rows, d_model = x_in.shape
     flat = mixed.shape[1]
     d_ff = gate_t.shape[0]
@@ -471,7 +469,7 @@
     dma = pltpu.SemaphoreType.DMA
     return pl.pallas_call(
         functools.partial(rest_kernel, heads, slots),
-        in_specs=[anywhere] * 10 + [vmem, vmem] + [anywhere] * 3,
+        in_specs=[anywhere] * 12 + [vmem, vmem] + [anywhere] * 3,
         out_specs=anywhere,
         out_shape=jax.ShapeDtypeStruct((rows, d_model), BF16),
         scratch_shapes=[
@@ -499,14 +497,14 @@
             pltpu.VMEM((chunks, CHUNK // 2, d_model), BF16),
             pltpu.VMEM((rows, d_model), BF16),
             dma((2, 3, chunks)), dma((2, 3, chunks)),
-            dma((2, 2)), dma((2, 2)),
+            dma((2,)), dma((2,)),
             dma((3, chunks)), dma((3, chunks)),
             dma((16,)), dma((2, slots)), dma((chunks,)),
         ],
         compiler_params=pltpu.CompilerParams(collective_id=0, has_side_effects=True, vmem_limit_bytes=VMEM_BYTES),
         cost_estimate=pl.CostEstimate(flops=2 * rows * d_model * (8 * flat + flat + 3 * d_ff), bytes_accessed=50_000_000, transcendentals=rows * d_ff),
         name='rest_of_layer',
-    )(x_in, mixed, w_o, w_o_over, cross_o, cross_o_over, cross_q, gate_t, up_t, w_down, norm_cross, norm_mlp, mask_t, cross_k, cross_v)
+    )(x_in, mixed, w_o, w_o_over, w_o_mate, cross_o, cross_o_over, cross_o_mate, cross_q, gate_t, up_t, w_down, norm_cross, norm_mlp, mask_t, cross_k, cross_v)
 
 
 def solution(mesh):
@@ -519,8 +517,11 @@
         swap = [(0, 2), (1, 3), (2, 0), (3, 1)]
         w_o_over = lax.ppermute(w_o, 'tp', swap)
         cross_o_over = lax.ppermute(cross_o, 'tp', swap)
+        mates = [(0, 1), (1, 0), (2, 3), (3, 2)]
+        w_o_mate = lax.ppermute(w_o, 'tp', mates)
+        cross_o_mate = lax.ppermute(cross_o, 'tp', mates)
         mixed_self, new_k, new_v = self_attention(tok_pos, rel_bias.T, x_in, w_q, w_k, w_v, norm_self, to_kernel(self_k), to_kernel(self_v), heads)
-        x_out = rest_of_layer(x_in, mixed_self, w_o, w_o_over, cross_o, cross_o_over, cross_q, w_gate.T, w_up.T, w_down, norm_cross, norm_mlp,
+        x_out = rest_of_layer(x_in, mixed_self, w_o, w_o_over, w_o_mate, cross_o, cross_o_over, cross_o_mate, cross_q, w_gate.T, w_up.T, w_down, norm_cross, norm_mlp,
                               enc_mask.T, cross_view(cross_k), cross_view(cross_v), heads)
         return x_out, from_kernel(new_k), from_kernel(new_v)
 

time: 113 us -> 103 us (0.912)
  Pallas kernels: 106 us -> 95.4 us
    pallas_call x1, Pallas kernels: 58.8 us -> 48.4 us  [self_attention(): pl.pallas_call(functools.partial(self_kernel, heads, flat // heads), in_s...]
  transfers between devices with their start and end apart: 2 -> 4, of which waited for: 0 -> 0; matrix products, arithmetic and copies ran while one was open for 0% -> 0% of each run, Pallas kernels for 52% -> 47%
where the time goes in v6:
time: 103 us
  Pallas kernels  95.4 us (93%)
  starting transfers between devices  3.87 us (4%)
  local copies, waits for them, and re-layouts  2.65 us (3%)
    pallas_call x1, Pallas kernels, self_attention(): pl.pallas_call(functools.partial(self_kernel, heads, flat // heads), in_s...  48.4 us
    pallas_call x1, Pallas kernels, rest_of_layer(): pl.pallas_call(functools.partial(rest_kernel, heads, slots), in_specs=[an...  47 us
    ppermute x1, starting transfers between devices, local_layer(): w_o_over = lax.ppermute(w_o, 'tp', swap)  3.36 us
    unnamed x1, local copies, waits for them, and re-layouts  2.65 us
  transfers between devices with their start and end apart: 4, of which 0 were waited for; matrix products, arithmetic and copies ran while one was open for 0% of the time, Pallas kernels for 47%

profile of v6, /device:TPU:0, one launch (start us, length us, event | category | flops | bytes accessed | tf_op | source)
XLA Modules:
  0.0 102.7 jit_solution(1936851238734078497)
XLA Ops:
  0.6 3.4 %collective-permute-start = (bf16[256,1536]{1,0:T(8,128)(2,1)}, bf16[256,1536]{1,0:T(8,128)(2,1)}, u32[]{:S(2)}, u32[]{:S(2)}) collective-permute-start(bf16[256,1536]{1,0:T(8,128)(2,1)} %wo_ref.1), channel_id=1, source_target_pairs={{0,2},{1,3},{2,0},{3,1},{4,6},{5,7},{6,4},{7,5}} | collective-permute-start | bytes 2359304 | tf_op jit(solution)/shard_map/ppermute | solution.py:518
  4.0 0.0 collective-permute-start.1
  4.0 0.1 collective-permute-start.2
  4.1 0.4 collective-permute-start.3
  4.5 48.4 %self_attention.1 = (bf16[512,256]{1,0:T(8,128)(2,1)}, bf16[512,256,128]{2,1,0:T(8,128)(2,1)}, bf16[512,256,128]{2,1,0:T(8,128)(2,1)}) custom-call(s32[512]{0:T(512)} %pos_ref.1, f32[4,32]{1,0:T(4,128)} %bitcast.29, bf16[512,1536]{1,0:T(8,128)(2,1)} %x_ref.3, bf16[1536,256]{1,0:T(8,128)(2,1)} %wq_ref.1, bf16[1536,256]{1,0:T(8,128)(2,1)} %wk_ref.1, ...), custom_call_target="tpu_custom_call" | custom-call | flops 2281701376 | bytes 134217728 | tf_op jit(solution)/shard_map/self_attention/pallas_call | solution.py:182
  52.9 0.0 collective-permute-done.wox_ref
  53.0 0.0 collective-permute-done.1.wom_ref
  53.0 0.0 collective-permute-done.2.cox_ref
  53.0 0.0 collective-permute-done.3.com_ref
  53.0 47.0 %rest_of_layer.1 = bf16[512,1536]{1,0:T(8,128)(2,1)} custom-call(bf16[512,1536]{1,0:T(8,128)(2,1)} %x_ref.3, bf16[512,256]{1,0:T(8,128)(2,1)} %get-tuple-element.6.mixed_ref, bf16[256,1536]{1,0:T(8,128)(2,1)} %wo_ref.1, bf16[256,1536]{1,0:T(8,128)(2,1)} %collective-permute-done.wox_ref, bf16[256,1536]{1,0:T(8,128)(2,1)} %collective-permute-done.1.wom_ref, ...), custom_call_target="tpu_custom_call" | custom-call | flops 8153726976 | bytes 50000000 | tf_op jit(solution)/shard_map/rest_of_layer/pallas_call | solution.py:470
  100.0 2.7 %copy.24 = bf16[512,1536]{1,0:T(8,128)(2,1)} copy(bf16[512,1536]{1,0:T(8,128)(2,1)} %rest_of_layer.1) | data formatting | bytes 3145728
Async XLA Ops:
  0.6 52.3 %collective-permute-start = (bf16[256,1536]{1,0:T(8,128)(2,1)}, bf16[256,1536]{1,0:T(8,128)(2,1)}, u32[]{:S(2)}, u32[]{:S(2)}) collective-permute-start(bf16[256,1536]{1,0:T(8,128)(2,1)} %wo_ref.1), channel_id=1, source_target_pairs={{0,2},{1,3},{2,0},{3,1},{4,6},{5,7},{6,4},{7,5}} | collective-permute-start | bytes 2359304 | tf_op jit(solution)/shard_map/ppermute | solution.py:518
  4.0 49.0 %collective-permute-start.1 = (bf16[256,1536]{1,0:T(8,128)(2,1)}, bf16[256,1536]{1,0:T(8,128)(2,1)}, u32[]{:S(2)}, u32[]{:S(2)}) collective-permute-start(bf16[256,1536]{1,0:T(8,128)(2,1)} %wo_ref.1), channel_id=1, source_target_pairs={{0,1},{1,0},{2,3},{3,2},{4,5},{5,4},{6,7},{7,6}} | collective-permute-start | bytes 2359304 | tf_op jit(solution)/shard_map/ppermute | solution.py:521
  4.0 49.0 %collective-permute-start.2 = (bf16[256,1536]{1,0:T(8,128)(2,1)}, bf16[256,1536]{1,0:T(8,128)(2,1)}, u32[]{:S(2)}, u32[]{:S(2)}) collective-permute-start(bf16[256,1536]{1,0:T(8,128)(2,1)} %co_ref.1), channel_id=1, source_target_pairs={{0,2},{1,3},{2,0},{3,1},{4,6},{5,7},{6,4},{7,5}} | collective-permute-start | bytes 2359304 | tf_op jit(solution)/shard_map/ppermute | solution.py:519
  4.1 48.9 %collective-permute-start.3 = (bf16[256,1536]{1,0:T(8,128)(2,1)}, bf16[256,1536]{1,0:T(8,128)(2,1)}, u32[]{:S(2)}, u32[]{:S(2)}) collective-permute-start(bf16[256,1536]{1,0:T(8,128)(2,1)} %co_ref.1), channel_id=1, source_target_pairs={{0,1},{1,0},{2,3},{3,2},{4,5},{5,4},{6,7},{7,6}} | collective-permute-start | bytes 2359304 | tf_op jit(solution)/shard_map/ppermute | solution.py:522

commit v7 on v6

--- a/solution.py
+++ b/solution.py
@@ -10,8 +10,9 @@
 BUCKET_EDGES = tuple(int(math.ceil(16.0 * 8.0 ** (bucket_step / 16.0))) for bucket_step in range(1, 16))
 NEG_FILL = -1e30
 STEP_ROWS = 32
-SLOTS = 8
-AHEAD = 4
+BLOCK_ROWS = 64
+SLOTS = 6
+AHEAD = 3
 VMEM_BYTES = 67043328
 LANES = 128
 F32 = jnp.float32
@@ -41,10 +42,11 @@
     flat = heads * head_dim
     rows_total = x_ref.shape[0]
     n = STEP_ROWS
-    steps = rows_total // n
+    parts = BLOCK_ROWS // n
+    steps = rows_total // BLOCK_ROWS
 
     def rows_of(step):
-        return pl.ds(pl.multiple_of(step * n, n), n)
+        return pl.ds(pl.multiple_of(step * BLOCK_ROWS, BLOCK_ROWS), BLOCK_ROWS)
 
     def fetch(step):
         slot = lax.rem(step, SLOTS)
@@ -55,6 +57,13 @@
         slot = lax.rem(step, SLOTS)
         return (pltpu.make_async_copy(k_s.at[slot], ko_ref.at[rows_of(step)], out_sem.at[0, slot]),
                 pltpu.make_async_copy(v_s.at[slot], vo_ref.at[rows_of(step)], out_sem.at[1, slot]))
+
+    def write_part(part):
+        slot = (steps - 1) % SLOTS
+        here = pl.ds(pl.multiple_of(part * n, n), n)
+        there = pl.ds(pl.multiple_of(BLOCK_ROWS * (steps - 1) + part * n, n), n)
+        return (pltpu.make_async_copy(k_s.at[slot, here], ko_ref.at[there], out_sem.at[0, slot]),
+                pltpu.make_async_copy(v_s.at[slot, here], vo_ref.at[there], out_sem.at[1, slot]))
 
     loads = [pltpu.make_async_copy(src, dst, load_sem.at[i])
              for i, (src, dst) in enumerate(((x_ref, x_s), (wq_ref, wq_s), (wk_ref, wk_s), (wv_ref, wv_s)))]
@@ -108,61 +117,72 @@
             for copy in fetch(ahead):
                 copy.start()
 
-        first = pl.multiple_of(step * n, n)
         slot = lax.rem(step, SLOTS)
-        group, part = step // per, lax.rem(step, per)
-        shift = lax.rem(LANES - part * n, LANES)
-        k_new = pltpu.roll(kt_s[group], shift, 1).astype(BF16)
-        v_new = pltpu.roll(vt_s[group], shift, 1).astype(BF16)
-        q_rows = jnp.where(own_head, dot(spread, q_s[pl.ds(first, n), :]), 0.0).astype(BF16)
-        in_k, in_v = fetch(step)
-
-        def update(cache, new_cols, b):
-            at_pos = lane_bf == pos_ref[first + b].astype(F32).astype(BF16)
-            col = jnp.broadcast_to(new_cols[:, b:b + 1], (flat, LANES))
-            updated = jnp.where(at_pos, col, cache[slot, b])
-            cache[slot, b] = updated
-            return updated
-
-        in_k.wait()
-        for g in range(n // 4):
-            lhs = q_rows[4 * heads * g:4 * heads * (g + 1), :]
-            picked = None
-            distance = None
-            for half in range(2):
-                b = 4 * g + 2 * half
-                pair = jnp.concatenate([update(k_s, k_new, b), update(k_s, k_new, b + 1)], axis=1)
-                both = dot(lhs, pair)
-                for j in range(2):
-                    mine = both[:, LANES * j:LANES * (j + 1)]
-                    at = 2 * half + j
-                    pos = pos_ref[first + 4 * g + at]
-                    picked = mine if picked is None else jnp.where(quad_row >= heads * at, mine, picked)
-                    distance = jnp.full((4 * heads, LANES), pos, jnp.int32) if distance is None else jnp.where(quad_row >= heads * at, pos, distance)
-            distance = distance - iota((4 * heads, LANES), 1)
-            bias = jnp.take_along_axis(table, jnp.maximum(distance, 0), axis=1)
-            score_s[4 * heads * g:4 * heads * (g + 1), :] = jnp.where(distance >= 0, picked + bias, NEG_FILL)
-        write(step)[0].start()
-
-        scores = score_s[...]
-        exps = jnp.exp(scores - jnp.max(scores, axis=1, keepdims=True))
-        probs = exps * pl.reciprocal(jnp.sum(exps, axis=1, keepdims=True))
-
-        in_v.wait()
-        for g in range(n // 4):
-            quad = probs[4 * heads * g:4 * heads * (g + 1), :]
-            picked = None
-            for half in range(2):
-                b = 4 * g + 2 * half
-                pair = jnp.concatenate([update(v_s, v_new, b), update(v_s, v_new, b + 1)], axis=1)
-                low = jnp.where(quad_row // heads == 2 * half, quad, 0.0)
-                high = jnp.where(quad_row // heads == 2 * half + 1, quad, 0.0)
-                lhs = jnp.concatenate([low, high], axis=1).astype(BF16)
-                both = dot_nt(lhs, pair)
-                picked = both if half == 0 else jnp.where(iota(both.shape, 0) >= 2 * heads, both, picked)
-            out_s[4 * heads * g:4 * heads * (g + 1), :] = picked
-        write(step)[1].start()
-        mixed_s[pl.ds(first, n), :] = dot(gather, jnp.where(own_head, out_s[...], 0.0).astype(BF16)).astype(BF16)
+        for copy in fetch(step):
+            copy.wait()
+
+        @pl.loop(0, parts)
+        def _(sub):
+            base = pl.multiple_of(sub * n, n)
+            first = pl.multiple_of(step * BLOCK_ROWS + base, n)
+            group, part = first // LANES, lax.rem(first // n, per)
+            shift = lax.rem(LANES - part * n, LANES)
+            k_new = pltpu.roll(kt_s[group], shift, 1)
+            v_new = pltpu.roll(vt_s[group], shift, 1)
+            q_rows = jnp.where(own_head, dot(spread, q_s[pl.ds(first, n), :]), 0.0).astype(BF16)
+
+            def update(cache, new_cols, b):
+                at_pos = lane_bf == pos_ref[first + b].astype(F32).astype(BF16)
+                col = jnp.broadcast_to(new_cols[:, b:b + 1], (flat, LANES)).astype(BF16)
+                updated = jnp.where(at_pos, col, cache[slot, base + b])
+                cache[slot, base + b] = updated
+                return updated
+
+            for g in range(n // 4):
+                lhs = q_rows[4 * heads * g:4 * heads * (g + 1), :]
+                picked = None
+                distance = None
+                for half in range(2):
+                    b = 4 * g + 2 * half
+                    pair = jnp.concatenate([update(k_s, k_new, b), update(k_s, k_new, b + 1)], axis=1)
+                    both = dot(lhs, pair)
+                    for j in range(2):
+                        mine = both[:, LANES * j:LANES * (j + 1)]
+                        at = 2 * half + j
+                        pos = pos_ref[first + 4 * g + at]
+                        picked = mine if picked is None else jnp.where(quad_row >= heads * at, mine, picked)
+                        distance = jnp.full((4 * heads, LANES), pos, jnp.int32) if distance is None else jnp.where(quad_row >= heads * at, pos, distance)
+                distance = distance - iota((4 * heads, LANES), 1)
+                bias = jnp.take_along_axis(table, jnp.maximum(distance, 0), axis=1)
+                score_s[4 * heads * g:4 * heads * (g + 1), :] = jnp.where(distance >= 0, picked + bias, NEG_FILL)
+
+            scores = score_s[...]
+            exps = jnp.exp(scores - jnp.max(scores, axis=1, keepdims=True))
+            probs = exps * pl.reciprocal(jnp.sum(exps, axis=1, keepdims=True))
+
+            for g in range(n // 4):
+                quad = probs[4 * heads * g:4 * heads * (g + 1), :]
+                picked = None
+                for half in range(2):
+                    b = 4 * g + 2 * half
+                    pair = jnp.concatenate([update(v_s, v_new, b), update(v_s, v_new, b + 1)], axis=1)
+                    low = jnp.where(quad_row // heads == 2 * half, quad, 0.0)
+                    high = jnp.where(quad_row // heads == 2 * half + 1, quad, 0.0)
+                    lhs = jnp.concatenate([low, high], axis=1).astype(BF16)
+                    both = dot_nt(lhs, pair)
+                    picked = both if half == 0 else jnp.where(iota(both.shape, 0) >= 2 * heads, both, picked)
+                out_s[4 * heads * g:4 * heads * (g + 1), :] = picked
+            mixed_s[pl.ds(first, n), :] = dot(gather, jnp.where(own_head, out_s[...], 0.0).astype(BF16)).astype(BF16)
+
+            @pl.when(step == steps - 1)
+            def _():
+                for copy in write_part(sub):
+                    copy.start()
+
+        @pl.when(step < steps - 1)
+        def _():
+            for copy in write(step):
+                copy.start()
 
     mixed_copy = pltpu.make_async_copy(mixed_s, mixed_ref, mixed_sem)
     mixed_copy.start()
@@ -189,8 +209,8 @@
             pltpu.VMEM((d_model, flat), BF16),
             pltpu.VMEM((d_model, flat), BF16),
             pltpu.VMEM((d_model, flat), BF16),
-            pltpu.VMEM((SLOTS, n, flat, t_len), BF16),
-            pltpu.VMEM((SLOTS, n, flat, t_len), BF16),
+            pltpu.VMEM((SLOTS, BLOCK_ROWS, flat, t_len), BF16),
+            pltpu.VMEM((SLOTS, BLOCK_ROWS, flat, t_len), BF16),
             pltpu.VMEM((rows, flat), BF16),
             pltpu.VMEM((rows, flat), BF16),
             pltpu.VMEM((rows // LANES, flat, LANES), F32),
@@ -209,13 +229,14 @@
 
 
 CHUNK = 128
+SOURCE = 16
 MESH = pl.DeviceIdType.MESH
 
 
-def rest_kernel(heads, n_cross_slots,
+def rest_kernel(heads,
                 x_ref, mixed_ref, wo_ref, wox_ref, wom_ref, co_ref, cox_ref, com_ref, cq_ref, gate_ref, up_ref, down_ref, norm_c_ref, norm_m_ref,
                 mask_ref, ck_ref, cv_ref, out_ref,
-                x_s, res_s, mix_s, cmix_s, wo_s, co_s, cq_s, gate_s, up_s, gate_t, up_t, down_s, k_s, v_s, mask_s,
+                x_s, res_s, mix_s, cmix_s, wo_s, co_s, cq_s, gate_s, up_s, down_s, k_s, v_s, mask_s,
                 qt_s, score_s, hid_s, part_s, near_s, chip_s, far_s, done_s,
                 ag_send, ag_recv, w_send, w_recv, sum_send, sum_recv, load_sem, cross_sem, out_sem):
     me = lax.axis_index('tp')
@@ -249,62 +270,53 @@
         loads.append(copy)
         return copy
 
-    def cross_load(c):
-        slot = c % n_cross_slots
-        cols = pl.ds(CHUNK * c, CHUNK)
-        return (pltpu.make_async_copy(ck_ref.at[:, :, cols], k_s.at[slot], cross_sem.at[0, slot]),
-                pltpu.make_async_copy(cv_ref.at[:, :, cols], v_s.at[slot], cross_sem.at[1, slot]))
-
-    def cross_start(c):
-        for copy in cross_load(c):
-            copy.start()
+    def cross_part(which, i):
+        at = pl.ds(i * SOURCE, SOURCE)
+        src, dst = ((ck_ref, k_s), (cv_ref, v_s))[which]
+        return pltpu.make_async_copy(src.at[at], dst.at[at], cross_sem.at[which, i])
 
     barrier = pltpu.get_barrier_semaphore()
     for peer in (mate, over):
         pl.semaphore_signal(barrier, inc=1, device_id={'tp': peer}, device_id_type=MESH)
-    pl.semaphore_wait(barrier, 2)
-
-    sends = []
-
-    def send(copy):
-        copy.start()
-        sends.append(copy)
-
-    def gather_send(stage, src, buf, c):
-        send(remote(src, block(buf, me, c), ag_send.at[stage, 0, c], ag_recv.at[stage, 0, c], over))
-        send(remote(src, block(buf, me, c), ag_send.at[stage, 1, c], ag_recv.at[stage, 1, c], mate))
-
-    def gather_relay(stage, buf, c):
-        remote(block(buf, over, c), block(buf, over, c), ag_send.at[stage, 0, c], ag_recv.at[stage, 0, c], over).wait_recv()
-        send(remote(block(buf, over, c), block(buf, over, c), ag_send.at[stage, 2, c], ag_recv.at[stage, 2, c], mate))
-
-    def gather_wait(stage, buf, c):
-        remote(block(buf, mate, c), block(buf, mate, c), ag_send.at[stage, 1, c], ag_recv.at[stage, 1, c], mate).wait_recv()
-        remote(block(buf, cater, c), block(buf, cater, c), ag_send.at[stage, 2, c], ag_recv.at[stage, 2, c], mate).wait_recv()
-
-    def weight_send(which, ref_x, buf):
-        send(remote(ref_x, shard(buf, over), w_send.at[which], w_recv.at[which], mate))
-
-    def weight_wait(which, buf):
-        remote(shard(buf, cater), shard(buf, cater), w_send.at[which], w_recv.at[which], mate).wait_recv()
-
-    for c in range(chunks):
-        gather_send(0, mixed_ref.at[pl.ds(CHUNK * c, CHUNK), :], mix_s, c)
     own_mixed = load(mixed_ref, mix_s.at[me])
     own_wo = (load(wo_ref, shard(wo_s, me)), load(wox_ref, shard(wo_s, over)), load(wom_ref, shard(wo_s, mate)))
     x_load = load(x_ref, x_s)
     q_load = load(cq_ref, cq_s)
     mask_load = load(mask_ref, mask_s)
+    for which in range(2):
+        for i in range(src_len // SOURCE):
+            cross_part(which, i).start()
+    pl.semaphore_wait(barrier, 2)
+
+    sends = []
+
+    def send(copy):
+        copy.start()
+        sends.append(copy)
+
+    def gather_send(stage, src, buf, c):
+        send(remote(src, block(buf, me, c), ag_send.at[stage, 0, c], ag_recv.at[stage, 0, c], over))
+        send(remote(src, block(buf, me, c), ag_send.at[stage, 1, c], ag_recv.at[stage, 1, c], mate))
+
+    def gather_relay(stage, buf, c):
+        remote(block(buf, over, c), block(buf, over, c), ag_send.at[stage, 0, c], ag_recv.at[stage, 0, c], over).wait_recv()
+        send(remote(block(buf, over, c), block(buf, over, c), ag_send.at[stage, 2, c], ag_recv.at[stage, 2, c], mate))
+
+    def gather_wait(stage, buf, c):
+        remote(block(buf, mate, c), block(buf, mate, c), ag_send.at[stage, 1, c], ag_recv.at[stage, 1, c], mate).wait_recv()
+        remote(block(buf, cater, c), block(buf, cater, c), ag_send.at[stage, 2, c], ag_recv.at[stage, 2, c], mate).wait_recv()
+
+    def weight_send(which, ref_x, buf):
+        send(remote(ref_x, shard(buf, over), w_send.at[which], w_recv.at[which], mate))
+
+    def weight_wait(which, buf):
+        remote(shard(buf, cater), shard(buf, cater), w_send.at[which], w_recv.at[which], mate).wait_recv()
+
+    for c in range(chunks):
+        gather_send(0, mixed_ref.at[pl.ds(CHUNK * c, CHUNK), :], mix_s, c)
     weight_send(0, wox_ref, wo_s)
-    gate_load = load(gate_ref, gate_s)
-    up_load = load(up_ref, up_s)
-    cross_start(0)
-
-    def turn(wide, tall):
-        @pl.loop(0, d_model // CHUNK)
-        def _(i):
-            at = pl.ds(pl.multiple_of(i * CHUNK, CHUNK), CHUNK)
-            tall[at, :] = wide[:, at].T
+    own_co = (load(co_ref, shard(co_s, me)), load(cox_ref, shard(co_s, over)), load(com_ref, shard(co_s, mate)))
+    mlp_loads = (load(gate_ref, gate_s), load(up_ref, up_s), load(down_ref, down_s))
 
     def project_heads(buf, weight, c, add_to):
         lhs = jnp.concatenate([buf[i, CHUNK * c:CHUNK * (c + 1), :] for i in range(4)], axis=1)
@@ -326,11 +338,10 @@
         qt_s[...] = dot(normed, cq_s[...]).astype(BF16).astype(F32).T
 
     def cross_score(c):
-        slot = c % n_cross_slots
-        for copy in cross_load(c):
-            copy.wait()
         if c == 0:
             mask_load.wait()
+            for i in range(src_len // SOURCE):
+                cross_part(0, i).wait()
         step = 8
 
         @pl.loop(0, src_len // step)
@@ -338,10 +349,9 @@
             at = pl.ds(pl.multiple_of(i * step, step), step)
             for h in range(heads):
                 d = slice(head_dim * h, head_dim * (h + 1))
-                score_s[h, at, :] = jnp.sum(k_s[slot, at, d, :].astype(F32) * qt_s[d, :][None], axis=1)
+                score_s[h, at, :] = jnp.sum(k_s[at, d, CHUNK * c:CHUNK * (c + 1)].astype(F32) * qt_s[d, :][None], axis=1)
 
     def cross_mix(c):
-        slot = c % n_cross_slots
         step = 8
         valid = mask_s[:, CHUNK * c:CHUNK * (c + 1)] != 0
         for h in range(heads):
@@ -356,11 +366,14 @@
                 s = i * step + j
                 for h in range(heads):
                     d = slice(head_dim * h, head_dim * (h + 1))
-                    acc[h] = acc[h] + v_s[slot, s, d, :].astype(F32) * score_s[h, pl.ds(s, 1), :]
+                    acc[h] = acc[h] + v_s[s, d, CHUNK * c:CHUNK * (c + 1)].astype(F32) * score_s[h, pl.ds(s, 1), :]
             return tuple(acc)
 
-        zero = jnp.zeros((head_dim, CHUNK), F32)
-        acc = lax.fori_loop(0, src_len // step, mix, (zero,) * heads)
+        acc = (jnp.zeros((head_dim, CHUNK), F32),) * heads
+        if c == 0:
+            for i in range(src_len // SOURCE):
+                cross_part(1, i).wait()
+        acc = lax.fori_loop(0, src_len // step, mix, acc)
         cmix_s[me, CHUNK * c:CHUNK * (c + 1), :] = jnp.concatenate(acc, axis=0).T.astype(BF16)
         gather_send(1, block(cmix_s, me, c), cmix_s, c)
 
@@ -372,12 +385,13 @@
         gather_wait(1, cmix_s, c)
         project_heads(cmix_s, co_s, c, res_s)
         if c == 0:
-            down_load.wait()
+            for copy in mlp_loads:
+                copy.wait()
         normed = rms_norm(res_s[CHUNK * c:CHUNK * (c + 1), :], norm_m_ref[...])
         for n in range(0, d_ff, 256):
             end = min(d_ff, n + 256)
-            gate = dot(normed, gate_t[:, n:end])
-            up = dot(normed, up_t[:, n:end])
+            gate = dot_nt(normed, gate_s[n:end, :])
+            up = dot_nt(normed, up_s[n:end, :])
             hid_s[:, n:end] = (jax.nn.gelu(gate, approximate=True) * up).astype(BF16)
         hidden = hid_s[...]
         for n in range(0, d_model, 512):
@@ -406,33 +420,24 @@
         copy.start()
         return copy
 
-    gate_load.wait()
-    turn(gate_s, gate_t)
     gather_relay(0, mix_s, 0)
-    up_load.wait()
-    turn(up_s, up_t)
     cross_query(0)
     for c in range(1, chunks):
         gather_relay(0, mix_s, c)
     weight_send(1, cox_ref, co_s)
-    cross_start(1)
     cross_score(0)
+    cross_query(1)
     cross_mix(0)
-    own_co = (load(co_ref, shard(co_s, me)), load(cox_ref, shard(co_s, over)), load(com_ref, shard(co_s, mate)))
-    cross_start(2)
-    cross_query(1)
     cross_score(1)
     cross_mix(1)
-    down_load = load(down_ref, down_s)
-    cross_start(3)
     cross_query(2)
+    cross_score(2)
     gather_relay(1, cmix_s, 0)
-    cross_score(2)
+    cross_mix(2)
     mlp(0)
     gather_relay(1, cmix_s, 1)
-    cross_mix(2)
+    cross_query(3)
     chip_sum(0)
-    cross_query(3)
     cross_score(3)
     cross_mix(3)
     mlp(1)
@@ -463,12 +468,11 @@
     d_ff = gate_t.shape[0]
     src_len = cross_k.shape[0]
     chunks = rows // CHUNK
-    slots = 2
     anywhere = pl.BlockSpec(memory_space=pl.ANY)
     vmem = pl.BlockSpec(memory_space=pltpu.VMEM)
     dma = pltpu.SemaphoreType.DMA
     return pl.pallas_call(
-        functools.partial(rest_kernel, heads, slots),
+        functools.partial(rest_kernel, heads),
         in_specs=[anywhere] * 12 + [vmem, vmem] + [anywhere] * 3,
         out_specs=anywhere,
         out_shape=jax.ShapeDtypeStruct((rows, d_model), BF16),
@@ -482,11 +486,9 @@
             pltpu.VMEM((d_model, flat), BF16),
             pltpu.VMEM((d_ff, d_model), BF16),
             pltpu.VMEM((d_ff, d_model), BF16),
-            pltpu.VMEM((d_model, d_ff), BF16),
-            pltpu.VMEM((d_model, d_ff), BF16),
             pltpu.VMEM((d_ff, d_model), BF16),
-            pltpu.VMEM((slots, src_len, flat, CHUNK), BF16),
-            pltpu.VMEM((slots, src_len, flat, CHUNK), BF16),
+            pltpu.VMEM((src_len, flat, rows), BF16),
+            pltpu.VMEM((src_len, flat, rows), BF16),
             pltpu.VMEM((src_len, rows), jnp.int32),
             pltpu.VMEM((flat, CHUNK), F32),
             pltpu.VMEM((heads, src_len, CHUNK), F32),
@@ -499,7 +501,7 @@
             dma((2, 3, chunks)), dma((2, 3, chunks)),
             dma((2,)), dma((2,)),
             dma((3, chunks)), dma((3, chunks)),
-            dma((16,)), dma((2, slots)), dma((chunks,)),
+            dma((16,)), dma((2, src_len // SOURCE)), dma((chunks,)),
         ],
         compiler_params=pltpu.CompilerParams(collective_id=0, has_side_effects=True, vmem_limit_bytes=VMEM_BYTES),
         cost_estimate=pl.CostEstimate(flops=2 * rows * d_model * (8 * flat + flat + 3 * d_ff), bytes_accessed=50_000_000, transcendentals=rows * d_ff),

time: 103 us -> 108 us (1.049)
  Pallas kernels: 95.4 us -> 101 us
    pallas_call x1, Pallas kernels: 47 us -> 51.2 us  [rest_of_layer(): pl.pallas_call(functools.partial(rest_kernel, heads), in_specs=[anywhere]...]
    pallas_call x1, Pallas kernels: 48.4 us -> 49.6 us  [self_attention(): pl.pallas_call(functools.partial(self_kernel, heads, flat // heads), in_s...]
  transfers between devices with their start and end apart: 4 -> 4, of which waited for: 0 -> 0; matrix products, arithmetic and copies ran while one was open for 0% -> 0% of each run, Pallas kernels for 47% -> 46%
where the time goes in v7:
time: 108 us
  Pallas kernels  101 us (94%)
  starting transfers between devices  3.87 us (4%)
  local copies, waits for them, and re-layouts  2.65 us (2%)
    pallas_call x1, Pallas kernels, rest_of_layer(): pl.pallas_call(functools.partial(rest_kernel, heads), in_specs=[anywhere]...  51.2 us
    pallas_call x1, Pallas kernels, self_attention(): pl.pallas_call(functools.partial(self_kernel, heads, flat // heads), in_s...  49.6 us
    ppermute x1, starting transfers between devices, local_layer(): w_o_over = lax.ppermute(w_o, 'tp', swap)  3.36 us
    unnamed x1, local copies, waits for them, and re-layouts  2.65 us
  transfers between devices with their start and end apart: 4, of which 0 were waited for; matrix products, arithmetic and copies ran while one was open for 0% of the time, Pallas kernels for 46%

profile of v7, /device:TPU:0, one launch (start us, length us, event | category | flops | bytes accessed | tf_op | source)
XLA Modules:
  0.0 108.0 jit_solution(10170706368730876094)
XLA Ops:
  0.6 3.4 %collective-permute-start = (bf16[256,1536]{1,0:T(8,128)(2,1)}, bf16[256,1536]{1,0:T(8,128)(2,1)}, u32[]{:S(2)}, u32[]{:S(2)}) collective-permute-start(bf16[256,1536]{1,0:T(8,128)(2,1)} %wo_ref.1), channel_id=1, source_target_pairs={{0,2},{1,3},{2,0},{3,1},{4,6},{5,7},{6,4},{7,5}} | collective-permute-start | bytes 2359304 | tf_op jit(solution)/shard_map/ppermute | solution.py:520
  4.0 0.0 collective-permute-start.1
  4.0 0.1 collective-permute-start.2
  4.1 0.4 collective-permute-start.3
  4.5 49.6 %self_attention.1 = (bf16[512,256]{1,0:T(8,128)(2,1)}, bf16[512,256,128]{2,1,0:T(8,128)(2,1)}, bf16[512,256,128]{2,1,0:T(8,128)(2,1)}) custom-call(s32[512]{0:T(512)} %pos_ref.1, f32[4,32]{1,0:T(4,128)} %bitcast.29, bf16[512,1536]{1,0:T(8,128)(2,1)} %x_ref.3, bf16[1536,256]{1,0:T(8,128)(2,1)} %wq_ref.1, bf16[1536,256]{1,0:T(8,128)(2,1)} %wk_ref.1, ...), custom_call_target="tpu_custom_call" | custom-call | flops 2281701376 | bytes 134217728 | tf_op jit(solution)/shard_map/self_attention/pallas_call | solution.py:202
  54.1 0.0 collective-permute-done.wox_ref
  54.1 0.0 collective-permute-done.1.wom_ref
  54.1 0.0 collective-permute-done.2.cox_ref
  54.1 0.0 collective-permute-done.3.com_ref
  54.1 51.2 %rest_of_layer.1 = bf16[512,1536]{1,0:T(8,128)(2,1)} custom-call(bf16[512,1536]{1,0:T(8,128)(2,1)} %x_ref.3, bf16[512,256]{1,0:T(8,128)(2,1)} %get-tuple-element.6.mixed_ref, bf16[256,1536]{1,0:T(8,128)(2,1)} %wo_ref.1, bf16[256,1536]{1,0:T(8,128)(2,1)} %collective-permute-done.wox_ref, bf16[256,1536]{1,0:T(8,128)(2,1)} %collective-permute-done.1.wom_ref, ...), custom_call_target="tpu_custom_call" | custom-call | flops 8153726976 | bytes 50000000 | tf_op jit(solution)/shard_map/rest_of_layer/pallas_call | solution.py:474
  105.3 2.7 %copy.24 = bf16[512,1536]{1,0:T(8,128)(2,1)} copy(bf16[512,1536]{1,0:T(8,128)(2,1)} %rest_of_layer.1) | data formatting | bytes 3145728
Async XLA Ops:
  0.6 53.4 %collective-permute-start = (bf16[256,1536]{1,0:T(8,128)(2,1)}, bf16[256,1536]{1,0:T(8,128)(2,1)}, u32[]{:S(2)}, u32[]{:S(2)}) collective-permute-start(bf16[256,1536]{1,0:T(8,128)(2,1)} %wo_ref.1), channel_id=1, source_target_pairs={{0,2},{1,3},{2,0},{3,1},{4,6},{5,7},{6,4},{7,5}} | collective-permute-start | bytes 2359304 | tf_op jit(solution)/shard_map/ppermute | solution.py:520
  4.0 50.1 %collective-permute-start.1 = (bf16[256,1536]{1,0:T(8,128)(2,1)}, bf16[256,1536]{1,0:T(8,128)(2,1)}, u32[]{:S(2)}, u32[]{:S(2)}) collective-permute-start(bf16[256,1536]{1,0:T(8,128)(2,1)} %wo_ref.1), channel_id=1, source_target_pairs={{0,1},{1,0},{2,3},{3,2},{4,5},{5,4},{6,7},{7,6}} | collective-permute-start | bytes 2359304 | tf_op jit(solution)/shard_map/ppermute | solution.py:523
  4.0 50.1 %collective-permute-start.2 = (bf16[256,1536]{1,0:T(8,128)(2,1)}, bf16[256,1536]{1,0:T(8,128)(2,1)}, u32[]{:S(2)}, u32[]{:S(2)}) collective-permute-start(bf16[256,1536]{1,0:T(8,128)(2,1)} %co_ref.1), channel_id=1, source_target_pairs={{0,2},{1,3},{2,0},{3,1},{4,6},{5,7},{6,4},{7,5}} | collective-permute-start | bytes 2359304 | tf_op jit(solution)/shard_map/ppermute | solution.py:521
  4.1 50.0 %collective-permute-start.3 = (bf16[256,1536]{1,0:T(8,128)(2,1)}, bf16[256,1536]{1,0:T(8,128)(2,1)}, u32[]{:S(2)}, u32[]{:S(2)}) collective-permute-start(bf16[256,1536]{1,0:T(8,128)(2,1)} %co_ref.1), channel_id=1, source_target_pairs={{0,1},{1,0},{2,3},{3,2},{4,5},{5,4},{6,7},{7,6}} | collective-permute-start | bytes 2359304 | tf_op jit(solution)/shard_map/ppermute | solution.py:524

commit v8 on v6

--- a/solution.py
+++ b/solution.py
@@ -215,7 +215,7 @@
 def rest_kernel(heads, n_cross_slots,
                 x_ref, mixed_ref, wo_ref, wox_ref, wom_ref, co_ref, cox_ref, com_ref, cq_ref, gate_ref, up_ref, down_ref, norm_c_ref, norm_m_ref,
                 mask_ref, ck_ref, cv_ref, out_ref,
-                x_s, res_s, mix_s, cmix_s, wo_s, co_s, cq_s, gate_s, up_s, gate_t, up_t, down_s, k_s, v_s, mask_s,
+                x_s, res_s, part_f, mix_s, cmix_s, wo_s, co_s, cq_s, gate_s, up_s, gate_t, up_t, down_s, k_s, v_s, mask_s,
                 qt_s, score_s, hid_s, part_s, near_s, chip_s, far_s, done_s,
                 ag_send, ag_recv, w_send, w_recv, sum_send, sum_recv, load_sem, cross_sem, out_sem):
     me = lax.axis_index('tp')
@@ -278,8 +278,10 @@
         remote(block(buf, over, c), block(buf, over, c), ag_send.at[stage, 0, c], ag_recv.at[stage, 0, c], over).wait_recv()
         send(remote(block(buf, over, c), block(buf, over, c), ag_send.at[stage, 2, c], ag_recv.at[stage, 2, c], mate))
 
-    def gather_wait(stage, buf, c):
+    def gather_near(stage, buf, c):
         remote(block(buf, mate, c), block(buf, mate, c), ag_send.at[stage, 1, c], ag_recv.at[stage, 1, c], mate).wait_recv()
+
+    def gather_far(stage, buf, c):
         remote(block(buf, cater, c), block(buf, cater, c), ag_send.at[stage, 2, c], ag_recv.at[stage, 2, c], mate).wait_recv()
 
     def weight_send(which, ref_x, buf):
@@ -306,22 +308,36 @@
             at = pl.ds(pl.multiple_of(i * CHUNK, CHUNK), CHUNK)
             tall[at, :] = wide[:, at].T
 
-    def project_heads(buf, weight, c, add_to):
-        lhs = jnp.concatenate([buf[i, CHUNK * c:CHUNK * (c + 1), :] for i in range(4)], axis=1)
+    def chip_dot(buf, weight, first, c, n):
+        lhs = jnp.concatenate([buf[first, CHUNK * c:CHUNK * (c + 1), :], buf[first + 1, CHUNK * c:CHUNK * (c + 1), :]], axis=1)
+        return dot(lhs, weight[pl.ds(pl.multiple_of(first * flat, flat), 2 * flat), n:n + 512])
+
+    def chip_product(buf, weight, c):
         for n in range(0, d_model, 512):
-            res_s[CHUNK * c:CHUNK * (c + 1), n:n + 512] = add_to[CHUNK * c:CHUNK * (c + 1), n:n + 512].astype(F32) + dot(lhs, weight[:, n:n + 512])
-
-    def cross_query(c):
+            part_f[CHUNK * c:CHUNK * (c + 1), n:n + 512] = chip_dot(buf, weight, me - core, c, n)
+
+    def add_other_chip(buf, weight, c, add_to):
+        rows = slice(CHUNK * c, CHUNK * (c + 1))
+        for n in range(0, d_model, 512):
+            both = part_f[rows, n:n + 512] + chip_dot(buf, weight, over - core, c, n)
+            res_s[rows, n:n + 512] = add_to[rows, n:n + 512].astype(F32) + both
+
+    def early_product(c):
         if c == 0:
             own_mixed.wait()
-            x_load.wait()
             for copy in own_wo:
                 copy.wait()
-        gather_wait(0, mix_s, c)
+        gather_near(0, mix_s, c)
+        chip_product(mix_s, wo_s, c)
+
+    def cross_query(c):
+        if c == 0:
+            x_load.wait()
+        gather_far(0, mix_s, c)
         if c == 0:
             weight_wait(0, wo_s)
             q_load.wait()
-        project_heads(mix_s, wo_s, c, x_s)
+        add_other_chip(mix_s, wo_s, c, x_s)
         normed = rms_norm(res_s[CHUNK * c:CHUNK * (c + 1), :], norm_c_ref[...])
         qt_s[...] = dot(normed, cq_s[...]).astype(BF16).astype(F32).T
 
@@ -364,22 +380,27 @@
         cmix_s[me, CHUNK * c:CHUNK * (c + 1), :] = jnp.concatenate(acc, axis=0).T.astype(BF16)
         gather_send(1, block(cmix_s, me, c), cmix_s, c)
 
-    def mlp(c):
+    def mlp_up(c):
         if c == 0:
             for copy in own_co:
                 copy.wait()
+        gather_near(1, cmix_s, c)
+        chip_product(cmix_s, co_s, c)
+        if c == 0:
             weight_wait(1, co_s)
-        gather_wait(1, cmix_s, c)
-        project_heads(cmix_s, co_s, c, res_s)
-        if c == 0:
-            down_load.wait()
+        gather_far(1, cmix_s, c)
+        add_other_chip(cmix_s, co_s, c, res_s)
         normed = rms_norm(res_s[CHUNK * c:CHUNK * (c + 1), :], norm_m_ref[...])
         for n in range(0, d_ff, 256):
             end = min(d_ff, n + 256)
             gate = dot(normed, gate_t[:, n:end])
             up = dot(normed, up_t[:, n:end])
             hid_s[:, n:end] = (jax.nn.gelu(gate, approximate=True) * up).astype(BF16)
+
+    def mlp_down(c):
         hidden = hid_s[...]
+        if c == 0:
+            down_load.wait()
         for n in range(0, d_model, 512):
             part_s[c, :, n:n + 512] = dot(hidden, down_s[:, n:n + 512]).astype(BF16)
         give = pl.ds(pl.multiple_of((1 - core) * half, half), half)
@@ -406,6 +427,8 @@
         copy.start()
         return copy
 
+    for c in range(chunks):
+        early_product(c)
     gate_load.wait()
     turn(gate_s, gate_t)
     gather_relay(0, mix_s, 0)
@@ -422,27 +445,31 @@
     cross_start(2)
     cross_query(1)
     cross_score(1)
+    gather_relay(1, cmix_s, 0)
     cross_mix(1)
     down_load = load(down_ref, down_s)
     cross_start(3)
+    mlp_up(0)
+    mlp_down(0)
+    gather_relay(1, cmix_s, 1)
     cross_query(2)
-    gather_relay(1, cmix_s, 0)
+    chip_sum(0)
     cross_score(2)
-    mlp(0)
-    gather_relay(1, cmix_s, 1)
     cross_mix(2)
-    chip_sum(0)
     cross_query(3)
     cross_score(3)
+    gather_relay(1, cmix_s, 2)
     cross_mix(3)
-    mlp(1)
-    gather_relay(1, cmix_s, 2)
+    mlp_up(1)
+    mlp_down(1)
+    mlp_up(2)
     chip_sum(1)
-    mlp(2)
+    mlp_down(2)
     gather_relay(1, cmix_s, 3)
     full_sum(0)
+    mlp_up(3)
     chip_sum(2)
-    mlp(3)
+    mlp_down(3)
     stores = [store(0)]
     full_sum(1)
     chip_sum(3)
@@ -474,6 +501,7 @@
         out_shape=jax.ShapeDtypeStruct((rows, d_model), BF16),
         scratch_shapes=[
             pltpu.VMEM((rows, d_model), BF16),
+            pltpu.VMEM((rows, d_model), F32),
             pltpu.VMEM((rows, d_model), F32),
             pltpu.VMEM((4, rows, flat), BF16),
             pltpu.VMEM((4, rows, flat), BF16),

time: 103 us -> 109 us (1.058)
  Pallas kernels: 95.4 us -> 101 us
    pallas_call x1, Pallas kernels: 47 us -> 52.9 us  [rest_of_layer(): pl.pallas_call(functools.partial(rest_kernel, heads, slots), in_specs=[an...]
  transfers between devices with their start and end apart: 4 -> 4, of which waited for: 0 -> 0; matrix products, arithmetic and copies ran while one was open for 0% -> 0% of each run, Pallas kernels for 47% -> 45%
where the time goes in v8:
time: 109 us
  Pallas kernels  101 us (93%)
  starting transfers between devices  3.87 us (4%)
  local copies, waits for them, and re-layouts  2.65 us (2%)
    pallas_call x1, Pallas kernels, rest_of_layer(): pl.pallas_call(functools.partial(rest_kernel, heads, slots), in_specs=[an...  52.9 us
    pallas_call x1, Pallas kernels, self_attention(): pl.pallas_call(functools.partial(self_kernel, heads, flat // heads), in_s...  48.4 us
    ppermute x1, starting transfers between devices, local_layer(): w_o_over = lax.ppermute(w_o, 'tp', swap)  3.36 us
    unnamed x1, local copies, waits for them, and re-layouts  2.65 us
  transfers between devices with their start and end apart: 4, of which 0 were waited for; matrix products, arithmetic and copies ran while one was open for 0% of the time, Pallas kernels for 45%

profile of v8, /device:TPU:0, one launch (start us, length us, event | category | flops | bytes accessed | tf_op | source)
XLA Modules:
  0.0 108.5 jit_solution(14623801192383135832)
XLA Ops:
  0.6 3.4 %collective-permute-start = (bf16[256,1536]{1,0:T(8,128)(2,1)}, bf16[256,1536]{1,0:T(8,128)(2,1)}, u32[]{:S(2)}, u32[]{:S(2)}) collective-permute-start(bf16[256,1536]{1,0:T(8,128)(2,1)} %wo_ref.1), channel_id=1, source_target_pairs={{0,2},{1,3},{2,0},{3,1},{4,6},{5,7},{6,4},{7,5}} | collective-permute-start | bytes 2359304 | tf_op jit(solution)/shard_map/ppermute | solution.py:546
  4.0 0.0 collective-permute-start.1
  4.0 0.1 collective-permute-start.2
  4.1 0.4 collective-permute-start.3
  4.5 48.4 %self_attention.1 = (bf16[512,256]{1,0:T(8,128)(2,1)}, bf16[512,256,128]{2,1,0:T(8,128)(2,1)}, bf16[512,256,128]{2,1,0:T(8,128)(2,1)}) custom-call(s32[512]{0:T(512)} %pos_ref.1, f32[4,32]{1,0:T(4,128)} %bitcast.29, bf16[512,1536]{1,0:T(8,128)(2,1)} %x_ref.3, bf16[1536,256]{1,0:T(8,128)(2,1)} %wq_ref.1, bf16[1536,256]{1,0:T(8,128)(2,1)} %wk_ref.1, ...), custom_call_target="tpu_custom_call" | custom-call | flops 2281701376 | bytes 134217728 | tf_op jit(solution)/shard_map/self_attention/pallas_call | solution.py:182
  52.9 0.0 collective-permute-done.wox_ref
  53.0 0.0 collective-permute-done.1.wom_ref
  53.0 0.0 collective-permute-done.2.cox_ref
  53.0 0.0 collective-permute-done.3.com_ref
  53.0 52.9 %rest_of_layer.1 = bf16[512,1536]{1,0:T(8,128)(2,1)} custom-call(bf16[512,1536]{1,0:T(8,128)(2,1)} %x_ref.3, bf16[512,256]{1,0:T(8,128)(2,1)} %get-tuple-element.6.mixed_ref, bf16[256,1536]{1,0:T(8,128)(2,1)} %wo_ref.1, bf16[256,1536]{1,0:T(8,128)(2,1)} %collective-permute-done.wox_ref, bf16[256,1536]{1,0:T(8,128)(2,1)} %collective-permute-done.1.wom_ref, ...), custom_call_target="tpu_custom_call" | custom-call | flops 8153726976 | bytes 50000000 | tf_op jit(solution)/shard_map/rest_of_layer/pallas_call | solution.py:497
  105.9 2.7 %copy.24 = bf16[512,1536]{1,0:T(8,128)(2,1)} copy(bf16[512,1536]{1,0:T(8,128)(2,1)} %rest_of_layer.1) | data formatting | bytes 3145728
Async XLA Ops:
  0.6 52.3 %collective-permute-start = (bf16[256,1536]{1,0:T(8,128)(2,1)}, bf16[256,1536]{1,0:T(8,128)(2,1)}, u32[]{:S(2)}, u32[]{:S(2)}) collective-permute-start(bf16[256,1536]{1,0:T(8,128)(2,1)} %wo_ref.1), channel_id=1, source_target_pairs={{0,2},{1,3},{2,0},{3,1},{4,6},{5,7},{6,4},{7,5}} | collective-permute-start | bytes 2359304 | tf_op jit(solution)/shard_map/ppermute | solution.py:546
  4.0 49.0 %collective-permute-start.1 = (bf16[256,1536]{1,0:T(8,128)(2,1)}, bf16[256,1536]{1,0:T(8,128)(2,1)}, u32[]{:S(2)}, u32[]{:S(2)}) collective-permute-start(bf16[256,1536]{1,0:T(8,128)(2,1)} %wo_ref.1), channel_id=1, source_target_pairs={{0,1},{1,0},{2,3},{3,2},{4,5},{5,4},{6,7},{7,6}} | collective-permute-start | bytes 2359304 | tf_op jit(solution)/shard_map/ppermute | solution.py:549
  4.0 49.0 %collective-permute-start.2 = (bf16[256,1536]{1,0:T(8,128)(2,1)}, bf16[256,1536]{1,0:T(8,128)(2,1)}, u32[]{:S(2)}, u32[]{:S(2)}) collective-permute-start(bf16[256,1536]{1,0:T(8,128)(2,1)} %co_ref.1), channel_id=1, source_target_pairs={{0,2},{1,3},{2,0},{3,1},{4,6},{5,7},{6,4},{7,5}} | collective-permute-start | bytes 2359304 | tf_op jit(solution)/shard_map/ppermute | solution.py:547
  4.1 48.9 %collective-permute-start.3 = (bf16[256,1536]{1,0:T(8,128)(2,1)}, bf16[256,1536]{1,0:T(8,128)(2,1)}, u32[]{:S(2)}, u32[]{:S(2)}) collective-permute-start(bf16[256,1536]{1,0:T(8,128)(2,1)} %co_ref.1), channel_id=1, source_target_pairs={{0,1},{1,0},{2,3},{3,2},{4,5},{5,4},{6,7},{7,6}} | collective-permute-start | bytes 2359304 | tf_op jit(solution)/shard_map/ppermute | solution.py:550

commit v9 on v5

--- a/solution.py
+++ b/solution.py
@@ -9,9 +9,9 @@
 
 BUCKET_EDGES = tuple(int(math.ceil(16.0 * 8.0 ** (bucket_step / 16.0))) for bucket_step in range(1, 16))
 NEG_FILL = -1e30
-STEP_ROWS = 16
-SLOTS = 16
-AHEAD = 8
+STEP_ROWS = 32
+SLOTS = 8
+AHEAD = 4
 VMEM_BYTES = 67043328
 LANES = 128
 F32 = jnp.float32
@@ -112,14 +112,14 @@
         slot = lax.rem(step, SLOTS)
         group, part = step // per, lax.rem(step, per)
         shift = lax.rem(LANES - part * n, LANES)
-        k_new = pltpu.roll(kt_s[group], shift, 1)
-        v_new = pltpu.roll(vt_s[group], shift, 1)
+        k_new = pltpu.roll(kt_s[group], shift, 1).astype(BF16)
+        v_new = pltpu.roll(vt_s[group], shift, 1).astype(BF16)
         q_rows = jnp.where(own_head, dot(spread, q_s[pl.ds(first, n), :]), 0.0).astype(BF16)
         in_k, in_v = fetch(step)
 
         def update(cache, new_cols, b):
             at_pos = lane_bf == pos_ref[first + b].astype(F32).astype(BF16)
-            col = jnp.broadcast_to(new_cols[:, b:b + 1], (flat, LANES)).astype(BF16)
+            col = jnp.broadcast_to(new_cols[:, b:b + 1], (flat, LANES))
             updated = jnp.where(at_pos, col, cache[slot, b])
             cache[slot, b] = updated
             return updated
@@ -215,7 +215,7 @@
 def rest_kernel(heads, n_cross_slots,
                 x_ref, mixed_ref, wo_ref, wox_ref, co_ref, cox_ref, cq_ref, gate_ref, up_ref, down_ref, norm_c_ref, norm_m_ref,
                 mask_ref, ck_ref, cv_ref, out_ref,
-                x_s, res_s, mix_s, cmix_s, wo_s, co_s, cq_s, gate_s, up_s, gate_t, up_t, down_s, k_s, v_s, mask_s,
+                x_s, res_s, mix_s, cmix_s, wo_s, co_s, cq_s, gate_s, up_s, gate_t, down_s, k_s, v_s, mask_s,
                 qt_s, score_s, hid_s, part_s, near_s, chip_s, far_s, done_s,
                 ag_send, ag_recv, w_send, w_recv, sum_send, sum_recv, load_sem, cross_sem, out_sem):
     me = lax.axis_index('tp')
@@ -327,6 +327,23 @@
         normed = rms_norm(res_s[CHUNK * c:CHUNK * (c + 1), :], norm_c_ref[...])
         qt_s[...] = dot(normed, cq_s[...]).astype(BF16).astype(F32).T
 
+    sub = iota((8, CHUNK), 0)
+    masks = [lax.rem(sub, 2 * w) < w for w in (4, 2, 1)]
+
+    def turned(x, w):
+        return jnp.concatenate([x[w:], x[:w]], axis=0)
+
+    def fold(parts):
+        for w, mask in zip((4, 2, 1), masks):
+            folded = []
+            for j in range(w):
+                a, b = parts[j], parts[j + w]
+                keep = jnp.where(mask, a, b)
+                give = jnp.where(mask, turned(a, w), turned(b, 8 - w))
+                folded.append(keep + give)
+            parts = folded
+        return parts[0]
+
     def cross_score(c):
         slot = c % n_cross_slots
         for copy in cross_load(c):
@@ -340,7 +357,11 @@
             at = pl.ds(pl.multiple_of(i * step, step), step)
             for h in range(heads):
                 d = slice(head_dim * h, head_dim * (h + 1))
-                score_s[h, at, :] = jnp.sum(k_s[slot, at, d, :].astype(F32) * qt_s[d, :][None], axis=1)
+                parts = []
+                for j in range(step):
+                    prod = k_s[slot, i * step + j, d, :].astype(F32) * qt_s[d, :]
+                    parts.append(jnp.sum(prod.reshape(head_dim // 8, 8, CHUNK), axis=0))
+                score_s[h, at, :] = fold(parts)
 
     def cross_mix(c):
         slot = c % n_cross_slots
@@ -374,12 +395,13 @@
         gather_wait(1, cmix_s, c)
         project_heads(cmix_s, co_s, c, res_s)
         if c == 0:
+            up_load.wait()
             down_load.wait()
         normed = rms_norm(res_s[CHUNK * c:CHUNK * (c + 1), :], norm_m_ref[...])
         for n in range(0, d_ff, 256):
             end = min(d_ff, n + 256)
             gate = dot(normed, gate_t[:, n:end])
-            up = dot(normed, up_t[:, n:end])
+            up = dot_nt(normed, up_s[n:end, :])
             hid_s[:, n:end] = (jax.nn.gelu(gate, approximate=True) * up).astype(BF16)
         hidden = hid_s[...]
         for n in range(0, d_model, 512):
@@ -387,32 +409,40 @@
         give = pl.ds(pl.multiple_of((1 - core) * half, half), half)
         send(remote(part_s.at[c, give, :], near_s.at[c], sum_send.at[0, c], sum_recv.at[0, c], mate))
 
-    keep = pl.ds(pl.multiple_of(core * half, half), half)
-
-    def chip_sum(c):
-        remote(near_s.at[c], near_s.at[c], sum_send.at[0, c], sum_recv.at[0, c], mate).wait_recv()
-        chip_s[c] = (part_s[c, keep, :].astype(F32) + near_s[c].astype(F32)).astype(BF16)
-        send(remote(chip_s.at[c], far_s.at[c], sum_send.at[1, c], sum_recv.at[1, c], over))
-
-    def full_sum(c):
-        remote(far_s.at[c], far_s.at[c], sum_send.at[1, c], sum_recv.at[1, c], over).wait_recv()
-        mine = pl.ds(pl.multiple_of(CHUNK * c + core * half, half), half)
-        done_s[mine, :] = (res_s[mine, :] + (chip_s[c].astype(F32) + far_s[c].astype(F32))).astype(BF16)
-        send(remote(done_s.at[mine, :], done_s.at[mine, :], sum_send.at[2, c], sum_recv.at[2, c], mate))
-
-    def store(c):
-        other = pl.ds(pl.multiple_of(CHUNK * c + (1 - core) * half, half), half)
-        remote(done_s.at[other, :], done_s.at[other, :], sum_send.at[2, c], sum_recv.at[2, c], mate).wait_recv()
-        rows = pl.ds(CHUNK * c, CHUNK)
-        copy = pltpu.make_async_copy(done_s.at[rows, :], out_ref.at[rows, :], out_sem.at[c])
+    pieces = [(c, 0, half) for c in range(chunks - 1)] + [(chunks - 1, 0, half // 2), (chunks - 1, half // 2, half // 2)]
+
+    def chip_sum(p):
+        c, at, size = pieces[p]
+        if at == 0:
+            remote(near_s.at[c], near_s.at[c], sum_send.at[0, c], sum_recv.at[0, c], mate).wait_recv()
+        keep = pl.ds(pl.multiple_of(core * half + at, size), size)
+        piece = pl.ds(at, size)
+        chip_s[c, piece, :] = (part_s[c, keep, :].astype(F32) + near_s[c, piece, :].astype(F32)).astype(BF16)
+        send(remote(chip_s.at[c, piece, :], far_s.at[c, piece, :], sum_send.at[1, p], sum_recv.at[1, p], over))
+
+    def full_sum(p):
+        c, at, size = pieces[p]
+        piece = pl.ds(at, size)
+        remote(far_s.at[c, piece, :], far_s.at[c, piece, :], sum_send.at[1, p], sum_recv.at[1, p], over).wait_recv()
+        mine = pl.ds(pl.multiple_of(CHUNK * c + core * half + at, size), size)
+        done_s[mine, :] = (res_s[mine, :] + (chip_s[c, piece, :].astype(F32) + far_s[c, piece, :].astype(F32))).astype(BF16)
+        send(remote(done_s.at[mine, :], done_s.at[mine, :], sum_send.at[2, p], sum_recv.at[2, p], mate))
+        copy = pltpu.make_async_copy(done_s.at[mine, :], out_ref.at[mine, :], out_sem.at[0, p])
         copy.start()
-        return copy
-
+        stores.append(copy)
+
+    def store(p):
+        c, at, size = pieces[p]
+        other = pl.ds(pl.multiple_of(CHUNK * c + (1 - core) * half + at, size), size)
+        remote(done_s.at[other, :], done_s.at[other, :], sum_send.at[2, p], sum_recv.at[2, p], mate).wait_recv()
+        copy = pltpu.make_async_copy(done_s.at[other, :], out_ref.at[other, :], out_sem.at[1, p])
+        copy.start()
+        stores.append(copy)
+
+    stores = []
     gate_load.wait()
     turn(gate_s, gate_t)
     gather_relay(0, mix_s, 0)
-    up_load.wait()
-    turn(up_s, up_t)
     cross_query(0)
     for c in range(1, chunks):
         gather_relay(0, mix_s, c)
@@ -445,14 +475,17 @@
     full_sum(0)
     chip_sum(2)
     mlp(3)
-    stores = [store(0)]
+    store(0)
     full_sum(1)
     chip_sum(3)
-    stores.append(store(1))
+    chip_sum(4)
+    store(1)
     full_sum(2)
-    stores.append(store(2))
+    store(2)
     full_sum(3)
-    stores.append(store(3))
+    store(3)
+    full_sum(4)
+    store(4)
     for copy in stores:
         copy.wait()
     for copy in sends:
@@ -485,7 +518,6 @@
             pltpu.VMEM((d_ff, d_model), BF16),
             pltpu.VMEM((d_ff, d_model), BF16),
             pltpu.VMEM((d_model, d_ff), BF16),
-            pltpu.VMEM((d_model, d_ff), BF16),
             pltpu.VMEM((d_ff, d_model), BF16),
             pltpu.VMEM((slots, src_len, flat, CHUNK), BF16),
             pltpu.VMEM((slots, src_len, flat, CHUNK), BF16),
@@ -500,8 +532,8 @@
             pltpu.VMEM((rows, d_model), BF16),
             dma((2, 3, chunks)), dma((2, 3, chunks)),
             dma((2, 2)), dma((2, 2)),
-            dma((3, chunks)), dma((3, chunks)),
-            dma((16,)), dma((2, slots)), dma((chunks,)),
+            dma((3, chunks + 1)), dma((3, chunks + 1)),
+            dma((16,)), dma((2, slots)), dma((2, chunks + 1)),
         ],
         compiler_params=pltpu.CompilerParams(collective_id=0, has_side_effects=True, vmem_limit_bytes=VMEM_BYTES),
         cost_estimate=pl.CostEstimate(flops=2 * rows * d_model * (8 * flat + flat + 3 * d_ff), bytes_accessed=50_000_000, transcendentals=rows * d_ff),

time: 113 us -> 102 us (0.903)
  Pallas kernels: 106 us -> 95.6 us
    pallas_call x1, Pallas kernels: 58.8 us -> 48.4 us  [self_attention(): pl.pallas_call(functools.partial(self_kernel, heads, flat // heads), in_s...]
  transfers between devices with their start and end apart: 2 -> 2, of which waited for: 0 -> 0; matrix products, arithmetic and copies ran while one was open for 0% -> 0% of each run, Pallas kernels for 52% -> 47%
where the time goes in v9:
time: 102 us
  Pallas kernels  95.6 us (94%)
  starting transfers between devices  3.4 us (3%)
  local copies, waits for them, and re-layouts  2.65 us (3%)
    pallas_call x1, Pallas kernels, self_attention(): pl.pallas_call(functools.partial(self_kernel, heads, flat // heads), in_s...  48.4 us
    pallas_call x1, Pallas kernels, rest_of_layer(): pl.pallas_call(functools.partial(rest_kernel, heads, slots), in_specs=[an...  47.1 us
    ppermute x1, starting transfers between devices, local_layer(): w_o_over = lax.ppermute(w_o, 'tp', swap)  3.36 us
    unnamed x1, local copies, waits for them, and re-layouts  2.65 us
  transfers between devices with their start and end apart: 2, of which 0 were waited for; matrix products, arithmetic and copies ran while one was open for 0% of the time, Pallas kernels for 47%

profile of v9, /device:TPU:0, one launch (start us, length us, event | category | flops | bytes accessed | tf_op | source)
XLA Modules:
  0.0 102.3 jit_solution(15420464278854827356)
XLA Ops:
  0.6 3.4 %collective-permute-start = (bf16[256,1536]{1,0:T(8,128)(2,1)}, bf16[256,1536]{1,0:T(8,128)(2,1)}, u32[]{:S(2)}, u32[]{:S(2)}) collective-permute-start(bf16[256,1536]{1,0:T(8,128)(2,1)} %wo_ref.1), channel_id=1, source_target_pairs={{0,2},{1,3},{2,0},{3,1},{4,6},{5,7},{6,4},{7,5}} | collective-permute-start | bytes 2359304 | tf_op jit(solution)/shard_map/ppermute | solution.py:552
  4.0 0.0 collective-permute-start.1
  4.0 48.4 %self_attention.1 = (bf16[512,256]{1,0:T(8,128)(2,1)}, bf16[512,256,128]{2,1,0:T(8,128)(2,1)}, bf16[512,256,128]{2,1,0:T(8,128)(2,1)}) custom-call(s32[512]{0:T(512)} %pos_ref.1, f32[4,32]{1,0:T(4,128)} %bitcast.29, bf16[512,1536]{1,0:T(8,128)(2,1)} %x_ref.3, bf16[1536,256]{1,0:T(8,128)(2,1)} %wq_ref.1, bf16[1536,256]{1,0:T(8,128)(2,1)} %wk_ref.1, ...), custom_call_target="tpu_custom_call" | custom-call | flops 2281701376 | bytes 134217728 | tf_op jit(solution)/shard_map/self_attention/pallas_call | solution.py:182
  52.5 0.0 collective-permute-done.wox_ref
  52.5 0.0 collective-permute-done.1.cox_ref
  52.5 47.1 %rest_of_layer.1 = bf16[512,1536]{1,0:T(8,128)(2,1)} custom-call(bf16[512,1536]{1,0:T(8,128)(2,1)} %x_ref.3, bf16[512,256]{1,0:T(8,128)(2,1)} %get-tuple-element.6.mixed_ref, bf16[256,1536]{1,0:T(8,128)(2,1)} %wo_ref.1, bf16[256,1536]{1,0:T(8,128)(2,1)} %collective-permute-done.wox_ref, bf16[256,1536]{1,0:T(8,128)(2,1)} %co_ref.1, ...), custom_call_target="tpu_custom_call" | custom-call | flops 8153726976 | bytes 50000000 | tf_op jit(solution)/shard_map/rest_of_layer/pallas_call | solution.py:505
  99.6 2.7 %copy.24 = bf16[512,1536]{1,0:T(8,128)(2,1)} copy(bf16[512,1536]{1,0:T(8,128)(2,1)} %rest_of_layer.1) | data formatting | bytes 3145728
Async XLA Ops:
  0.6 51.8 %collective-permute-start = (bf16[256,1536]{1,0:T(8,128)(2,1)}, bf16[256,1536]{1,0:T(8,128)(2,1)}, u32[]{:S(2)}, u32[]{:S(2)}) collective-permute-start(bf16[256,1536]{1,0:T(8,128)(2,1)} %wo_ref.1), channel_id=1, source_target_pairs={{0,2},{1,3},{2,0},{3,1},{4,6},{5,7},{6,4},{7,5}} | collective-permute-start | bytes 2359304 | tf_op jit(solution)/shard_map/ppermute | solution.py:552
  4.0 48.5 %collective-permute-start.1 = (bf16[256,1536]{1,0:T(8,128)(2,1)}, bf16[256,1536]{1,0:T(8,128)(2,1)}, u32[]{:S(2)}, u32[]{:S(2)}) collective-permute-start(bf16[256,1536]{1,0:T(8,128)(2,1)} %co_ref.1), channel_id=1, source_target_pairs={{0,2},{1,3},{2,0},{3,1},{4,6},{5,7},{6,4},{7,5}} | collective-permute-start | bytes 2359304 | tf_op jit(solution)/shard_map/ppermute | solution.py:553

commit v10 on v9

--- a/solution.py
+++ b/solution.py
@@ -10,8 +10,8 @@
 BUCKET_EDGES = tuple(int(math.ceil(16.0 * 8.0 ** (bucket_step / 16.0))) for bucket_step in range(1, 16))
 NEG_FILL = -1e30
 STEP_ROWS = 32
-SLOTS = 8
-AHEAD = 4
+SLOTS = 11
+AHEAD = 6
 VMEM_BYTES = 67043328
 LANES = 128
 F32 = jnp.float32
@@ -541,6 +541,35 @@
     )(x_in, mixed, w_o, w_o_over, cross_o, cross_o_over, cross_q, gate_t, up_t, w_down, norm_cross, norm_mlp, mask_t, cross_k, cross_v)
 
 
+HAND_PIECES = 4
+
+
+def hand_out(x_out):
+    rows = x_out.shape[0] // HAND_PIECES
+
+    def kernel(x_ref, out_ref, held, in_sem, out_sem):
+        part = [pl.ds(rows * i, rows) for i in range(HAND_PIECES)]
+        ins = [pltpu.make_async_copy(x_ref.at[p], held.at[p], in_sem.at[i]) for i, p in enumerate(part)]
+        outs = [pltpu.make_async_copy(held.at[p], out_ref.at[p], out_sem.at[i]) for i, p in enumerate(part)]
+        for copy in ins:
+            copy.start()
+        for arrived, copy in zip(ins, outs):
+            arrived.wait()
+            copy.start()
+        for copy in outs:
+            copy.wait()
+
+    return pl.pallas_call(
+        kernel,
+        in_specs=[pl.BlockSpec(memory_space=pl.ANY)],
+        out_specs=pl.BlockSpec(memory_space=pl.ANY),
+        out_shape=jax.ShapeDtypeStruct(x_out.shape, x_out.dtype),
+        scratch_shapes=[pltpu.VMEM(x_out.shape, x_out.dtype), pltpu.SemaphoreType.DMA((HAND_PIECES,)), pltpu.SemaphoreType.DMA((HAND_PIECES,))],
+        compiler_params=pltpu.CompilerParams(vmem_limit_bytes=VMEM_BYTES),
+        name='hand_out',
+    )(x_out)
+
+
 def solution(mesh):
     def local_layer(x_in, tok_pos, self_k, self_v, cross_k, cross_v, enc_mask, rel_bias, w_q, w_k, w_v, w_o, cross_q, cross_o, w_gate, w_up, w_down, norm_self, norm_cross, norm_mlp):
         rows, t_len, heads, head_dim = self_k.shape
@@ -554,7 +583,7 @@
         mixed_self, new_k, new_v = self_attention(tok_pos, rel_bias.T, x_in, w_q, w_k, w_v, norm_self, to_kernel(self_k), to_kernel(self_v), heads)
         x_out = rest_of_layer(x_in, mixed_self, w_o, w_o_over, cross_o, cross_o_over, cross_q, w_gate.T, w_up.T, w_down, norm_cross, norm_mlp,
                               enc_mask.T, cross_view(cross_k), cross_view(cross_v), heads)
-        return x_out, from_kernel(new_k), from_kernel(new_v)
+        return hand_out(x_out), from_kernel(new_k), from_kernel(new_v)
 
     cache_spec = P('dp', None, 'tp', None)
     split_cols = P(None, 'tp')

time: 102 us -> 104 us (1.020)
  Pallas kernels: 95.6 us -> 99.5 us
  local copies, waits for them, and re-layouts: 2.65 us -> 0 us
    unnamed x1 -> x0, local copies, waits for them, and re-layouts: 2.65 us -> none
    pallas_call x0 -> x1, Pallas kernels: none -> 2.2 us  [hand_out(): pl.pallas_call(kernel, in_specs=[pl.BlockSpec(memory_space=pl.ANY)], out_...]
    pallas_call x1, Pallas kernels: 48.4 us -> 50.2 us  [self_attention(): pl.pallas_call(functools.partial(self_kernel, heads, flat // heads), in_s...]
  transfers between devices with their start and end apart: 2 -> 2, of which waited for: 0 -> 0; matrix products, arithmetic and copies ran while one was open for 0% -> 0% of each run, Pallas kernels for 47% -> 48%
where the time goes in v10:
time: 104 us
  Pallas kernels  99.5 us (96%)
  starting transfers between devices  3.4 us (3%)
    pallas_call x1, Pallas kernels, self_attention(): pl.pallas_call(functools.partial(self_kernel, heads, flat // heads), in_s...  50.2 us
    pallas_call x1, Pallas kernels, rest_of_layer(): pl.pallas_call(functools.partial(rest_kernel, heads, slots), in_specs=[an...  47.1 us
    ppermute x1, starting transfers between devices, local_layer(): w_o_over = lax.ppermute(w_o, 'tp', swap)  3.36 us
    pallas_call x1, Pallas kernels, hand_out(): pl.pallas_call(kernel, in_specs=[pl.BlockSpec(memory_space=pl.ANY)], out_...  2.2 us
  transfers between devices with their start and end apart: 2, of which 0 were waited for; matrix products, arithmetic and copies ran while one was open for 0% of the time, Pallas kernels for 48%

profile of v10, /device:TPU:0, one launch (start us, length us, event | category | flops | bytes accessed | tf_op | source)
XLA Modules:
  0.0 103.7 jit_solution(942043594308889415)
XLA Ops:
  0.6 3.4 %collective-permute-start = (bf16[256,1536]{1,0:T(8,128)(2,1)}, bf16[256,1536]{1,0:T(8,128)(2,1)}, u32[]{:S(2)}, u32[]{:S(2)}) collective-permute-start(bf16[256,1536]{1,0:T(8,128)(2,1)} %wo_ref.1), channel_id=1, source_target_pairs={{0,2},{1,3},{2,0},{3,1},{4,6},{5,7},{6,4},{7,5}} | collective-permute-start | bytes 2359304 | tf_op jit(solution)/shard_map/ppermute | solution.py:581
  4.0 0.0 collective-permute-start.1
  4.0 50.2 %self_attention.1 = (bf16[512,256]{1,0:T(8,128)(2,1)}, bf16[512,256,128]{2,1,0:T(8,128)(2,1)}, bf16[512,256,128]{2,1,0:T(8,128)(2,1)}) custom-call(s32[512]{0:T(512)} %pos_ref.1, f32[4,32]{1,0:T(4,128)} %bitcast.29, bf16[512,1536]{1,0:T(8,128)(2,1)} %x_ref.3, bf16[1536,256]{1,0:T(8,128)(2,1)} %wq_ref.1, bf16[1536,256]{1,0:T(8,128)(2,1)} %wk_ref.1, ...), custom_call_target="tpu_custom_call" | custom-call | flops 2281701376 | bytes 134217728 | tf_op jit(solution)/shard_map/self_attention/pallas_call | solution.py:182
  54.2 0.0 collective-permute-done.wox_ref
  54.2 0.0 collective-permute-done.1.cox_ref
  54.2 47.1 %rest_of_layer.1.x_ref = bf16[512,1536]{1,0:T(8,128)(2,1)} custom-call(bf16[512,1536]{1,0:T(8,128)(2,1)} %x_ref.3, bf16[512,256]{1,0:T(8,128)(2,1)} %get-tuple-element.6.mixed_ref, bf16[256,1536]{1,0:T(8,128)(2,1)} %wo_ref.1, bf16[256,1536]{1,0:T(8,128)(2,1)} %collective-permute-done.wox_ref, bf16[256,1536]{1,0:T(8,128)(2,1)} %co_ref.1, ...), custom_call_target="tpu_custom_call" | custom-call | flops 8153726976 | bytes 50000000 | tf_op jit(solution)/shard_map/rest_of_layer/pallas_call | solution.py:505
  101.3 2.2 %hand_out.1 = bf16[512,1536]{1,0:T(8,128)(2,1)} custom-call(bf16[512,1536]{1,0:T(8,128)(2,1)} %rest_of_layer.1.x_ref), custom_call_target="tpu_custom_call" | custom-call | tf_op jit(solution)/shard_map/hand_out/pallas_call | solution.py:562
Async XLA Ops:
  0.6 53.6 %collective-permute-start = (bf16[256,1536]{1,0:T(8,128)(2,1)}, bf16[256,1536]{1,0:T(8,128)(2,1)}, u32[]{:S(2)}, u32[]{:S(2)}) collective-permute-start(bf16[256,1536]{1,0:T(8,128)(2,1)} %wo_ref.1), channel_id=1, source_target_pairs={{0,2},{1,3},{2,0},{3,1},{4,6},{5,7},{6,4},{7,5}} | collective-permute-start | bytes 2359304 | tf_op jit(solution)/shard_map/ppermute | solution.py:581
  4.0 50.2 %collective-permute-start.1 = (bf16[256,1536]{1,0:T(8,128)(2,1)}, bf16[256,1536]{1,0:T(8,128)(2,1)}, u32[]{:S(2)}, u32[]{:S(2)}) collective-permute-start(bf16[256,1536]{1,0:T(8,128)(2,1)} %co_ref.1), channel_id=1, source_target_pairs={{0,2},{1,3},{2,0},{3,1},{4,6},{5,7},{6,4},{7,5}} | collective-permute-start | bytes 2359304 | tf_op jit(solution)/shard_map/ppermute | solution.py:582

commit v11 on v10

--- a/solution.py
+++ b/solution.py
@@ -10,8 +10,8 @@
 BUCKET_EDGES = tuple(int(math.ceil(16.0 * 8.0 ** (bucket_step / 16.0))) for bucket_step in range(1, 16))
 NEG_FILL = -1e30
 STEP_ROWS = 32
-SLOTS = 11
-AHEAD = 6
+SLOTS = 8
+AHEAD = 2
 VMEM_BYTES = 67043328
 LANES = 128
 F32 = jnp.float32

time: 104 us -> 103 us (level)
  no operation moved by 1% of the time
where the time goes in v11:
time: 103 us
  Pallas kernels  98.9 us (96%)
  starting transfers between devices  3.4 us (3%)
    pallas_call x1, Pallas kernels, self_attention(): pl.pallas_call(functools.partial(self_kernel, heads, flat // heads), in_s...  49.6 us
    pallas_call x1, Pallas kernels, rest_of_layer(): pl.pallas_call(functools.partial(rest_kernel, heads, slots), in_specs=[an...  47.1 us
    ppermute x1, starting transfers between devices, local_layer(): w_o_over = lax.ppermute(w_o, 'tp', swap)  3.36 us
    pallas_call x1, Pallas kernels, hand_out(): pl.pallas_call(kernel, in_specs=[pl.BlockSpec(memory_space=pl.ANY)], out_...  2.2 us
  transfers between devices with their start and end apart: 2, of which 0 were waited for; matrix products, arithmetic and copies ran while one was open for 0% of the time, Pallas kernels for 48%

profile of v11, /device:TPU:0, one launch (start us, length us, event | category | flops | bytes accessed | tf_op | source)
XLA Modules:
  0.0 103.1 jit_solution(9378833464168550421)
XLA Ops:
  0.6 3.4 %collective-permute-start = (bf16[256,1536]{1,0:T(8,128)(2,1)}, bf16[256,1536]{1,0:T(8,128)(2,1)}, u32[]{:S(2)}, u32[]{:S(2)}) collective-permute-start(bf16[256,1536]{1,0:T(8,128)(2,1)} %wo_ref.1), channel_id=1, source_target_pairs={{0,2},{1,3},{2,0},{3,1},{4,6},{5,7},{6,4},{7,5}} | collective-permute-start | bytes 2359304 | tf_op jit(solution)/shard_map/ppermute | solution.py:581
  4.0 0.0 collective-permute-start.1
  4.0 49.6 %self_attention.1 = (bf16[512,256]{1,0:T(8,128)(2,1)}, bf16[512,256,128]{2,1,0:T(8,128)(2,1)}, bf16[512,256,128]{2,1,0:T(8,128)(2,1)}) custom-call(s32[512]{0:T(512)} %pos_ref.1, f32[4,32]{1,0:T(4,128)} %bitcast.29, bf16[512,1536]{1,0:T(8,128)(2,1)} %x_ref.3, bf16[1536,256]{1,0:T(8,128)(2,1)} %wq_ref.1, bf16[1536,256]{1,0:T(8,128)(2,1)} %wk_ref.1, ...), custom_call_target="tpu_custom_call" | custom-call | flops 2281701376 | bytes 134217728 | tf_op jit(solution)/shard_map/self_attention/pallas_call | solution.py:182
  53.6 0.0 collective-permute-done.wox_ref
  53.6 0.0 collective-permute-done.1.cox_ref
  53.6 47.1 %rest_of_layer.1.x_ref = bf16[512,1536]{1,0:T(8,128)(2,1)} custom-call(bf16[512,1536]{1,0:T(8,128)(2,1)} %x_ref.3, bf16[512,256]{1,0:T(8,128)(2,1)} %get-tuple-element.6.mixed_ref, bf16[256,1536]{1,0:T(8,128)(2,1)} %wo_ref.1, bf16[256,1536]{1,0:T(8,128)(2,1)} %collective-permute-done.wox_ref, bf16[256,1536]{1,0:T(8,128)(2,1)} %co_ref.1, ...), custom_call_target="tpu_custom_call" | custom-call | flops 8153726976 | bytes 50000000 | tf_op jit(solution)/shard_map/rest_of_layer/pallas_call | solution.py:505
  100.8 2.2 %hand_out.1 = bf16[512,1536]{1,0:T(8,128)(2,1)} custom-call(bf16[512,1536]{1,0:T(8,128)(2,1)} %rest_of_layer.1.x_ref), custom_call_target="tpu_custom_call" | custom-call | tf_op jit(solution)/shard_map/hand_out/pallas_call | solution.py:562
Async XLA Ops:
  0.6 53.0 %collective-permute-start = (bf16[256,1536]{1,0:T(8,128)(2,1)}, bf16[256,1536]{1,0:T(8,128)(2,1)}, u32[]{:S(2)}, u32[]{:S(2)}) collective-permute-start(bf16[256,1536]{1,0:T(8,128)(2,1)} %wo_ref.1), channel_id=1, source_target_pairs={{0,2},{1,3},{2,0},{3,1},{4,6},{5,7},{6,4},{7,5}} | collective-permute-start | bytes 2359304 | tf_op jit(solution)/shard_map/ppermute | solution.py:581
  4.0 49.6 %collective-permute-start.1 = (bf16[256,1536]{1,0:T(8,128)(2,1)}, bf16[256,1536]{1,0:T(8,128)(2,1)}, u32[]{:S(2)}, u32[]{:S(2)}) collective-permute-start(bf16[256,1536]{1,0:T(8,128)(2,1)} %co_ref.1), channel_id=1, source_target_pairs={{0,2},{1,3},{2,0},{3,1},{4,6},{5,7},{6,4},{7,5}} | collective-permute-start | bytes 2359304 | tf_op jit(solution)/shard_map/ppermute | solution.py:582
